TPU v7x, 32 devices: a whole 2x2x4 slice. The times are simulated.
32 devices in a mesh: dp: 4 (over y, x), fsdp: 8 (over z, core).
Axes of the slice: x: 2, y: 2, z: 4, core: 2. Of those that a mesh axis runs over, the one named last changes fastest.
Arguments:
- inputs: bfloat16 [65536, 512], P(('dp', 'fsdp')), may hold values from -6 to 6
- cotangent: bfloat16 [65536, 512], P(('dp', 'fsdp')), may hold values from -6 to 6
- feature_omega: bfloat16 [8, 64, 256], replicated, may hold values from -6 to 6
- seg_start: int32 [64], P(('dp', 'fsdp')), may hold values from 0 to 1, as said below
- seg_len: int32 [64], P(('dp', 'fsdp')), may hold values from 0 to 1024, as said below
- step_count: int32 [], replicated, may hold values from 1 to 20
- w_qkv: float32 [512, 1536], P(('dp', 'fsdp')), may hold values from -0.25 to 0.25
- w_out: float32 [512, 512], P(('dp', 'fsdp')), may hold values from -1 to 1
- w_up: float32 [512, 2048], P(('dp', 'fsdp')), may hold values from -0.26516504 to 0.26516504
- w_down: float32 [2048, 512], P(('dp', 'fsdp')), may hold values from -0.125 to 0.125
- gains: float32 [2, 512], P(None, ('dp', 'fsdp')), may hold values from 0.3 to 3.1
- m_qkv: float32 [512, 1536], P(('dp', 'fsdp')), may hold values from -0.0009765625 to 0.0009765625
- m_out: float32 [512, 512], P(('dp', 'fsdp')), may hold values from -0.0009765625 to 0.0009765625
- m_up: float32 [512, 2048], P(('dp', 'fsdp')), may hold values from -0.0009765625 to 0.0009765625
- m_down: float32 [2048, 512], P(('dp', 'fsdp')), may hold values from -0.0009765625 to 0.0009765625
- m_gains: float32 [2, 512], P(None, ('dp', 'fsdp')), may hold values from -0.0029296875 to 0.0029296875
- v_qkv: float32 [512, 1536], P(('dp', 'fsdp')), may hold values from 1.58894e-08 to 1.271152e-07
- v_out: float32 [512, 512], P(('dp', 'fsdp')), may hold values from 1.58894e-09 to 1.271152e-08
- v_up: float32 [512, 2048], P(('dp', 'fsdp')), may hold values from 2.224516e-09 to 1.7796127e-08
- v_down: float32 [2048, 512], P(('dp', 'fsdp')), may hold values from 3.17788e-09 to 2.542304e-08
- v_gains: float32 [2, 512], P(None, ('dp', 'fsdp')), may hold values from 1.430046e-07 to 1.1440368e-06
Outputs:
- out_rows: bfloat16 [65536, 512], P(('dp', 'fsdp'))
- grad_inputs: float32 [65536, 512], P(('dp', 'fsdp'))
- grad_norm: float32 [], replicated
- grad_qkv: float32 [512, 1536], P(('dp', 'fsdp'))
- var_qkv: float32 [512, 1536], P(('dp', 'fsdp'))
- new_qkv: float32 [512, 1536], P(('dp', 'fsdp'))
- grad_out: float32 [512, 512], P(('dp', 'fsdp'))
- var_out: float32 [512, 512], P(('dp', 'fsdp'))
- new_out: float32 [512, 512], P(('dp', 'fsdp'))
- grad_up: float32 [512, 2048], P(('dp', 'fsdp'))
- var_up: float32 [512, 2048], P(('dp', 'fsdp'))
- new_up: float32 [512, 2048], P(('dp', 'fsdp'))
- grad_down: float32 [2048, 512], P(('dp', 'fsdp'))
- var_down: float32 [2048, 512], P(('dp', 'fsdp'))
- new_down: float32 [2048, 512], P(('dp', 'fsdp'))
- grad_gains: float32 [2, 512], P(None, ('dp', 'fsdp'))
- var_gains: float32 [2, 512], P(None, ('dp', 'fsdp'))
- new_gains: float32 [2, 512], P(None, ('dp', 'fsdp'))
Inputs may be any that keep to these rules, and one draw needn't show every extreme that they name: Each device holds 2 consecutive segments; its first segment has seg_start 1, so no protein crosses devices; a protein is 1 to 2 segments. Residues fill a segment from its start; all segments of a protein but its last are full, and a protein of one segment is full; after a device's last protein come empty segments (seg_len 0, seg_start 0); a segment with seg_start 1 is never empty; in every draw some device is full.
All inputs are finite; a program needn't handle non-finite values.
Results may differ from a plain program's by a relative error of at most 0.025.
The roundings to bfloat16 on the way count: a program that leaves them out, or rounds other values in their place, can miss the bound.
Values may be sent and summed in bfloat16 or wider, within the bound.
A program may use at most 256 MiB of HBM per device.

v0:
```python
import jax
import jax.numpy as jnp
from jax import lax
from jax.sharding import PartitionSpec as P

D = 512
HEADS = 8
HD = 64
FEAT = 256
SEG = 1024
TILE = 256


norm_eps = 1e-05
clip_level = 1.0
rate_matrix = 0.03
rate_gain = 0.4
beta_first = 0.9
beta_second = 0.95
adam_eps = 1e-08
decay_weight = 0.1
highest = lax.Precision.HIGHEST


def layer_norm(input_rows, gain_row):
    centred = input_rows - jnp.mean(input_rows, axis=-1, keepdims=True)
    spread = jnp.mean(centred * centred, axis=-1, keepdims=True)
    return centred * lax.rsqrt(spread + norm_eps) * gain_row


def feature_map(projected, values):
    feat_scale = HD ** (-0.25)
    square = jnp.sum(values * values, axis=-1, keepdims=True) * (0.5 * feat_scale * feat_scale)
    return jnp.exp(projected * feat_scale - square)


def gelu_exact(hidden):
    return jax.nn.gelu(hidden, approximate=False)


def token_mask(lengths):
    position = jnp.arange(SEG, dtype=jnp.int32)[None, :]
    return (position < lengths[:, None]).astype(jnp.float32).reshape(lengths.shape[0] * SEG)


def tile_links(starts):
    protein_id = jnp.cumsum(starts)
    per_tile = jnp.repeat(protein_id, SEG // TILE)
    tile_index = jnp.arange(per_tile.shape[0], dtype=jnp.int32)
    same_protein = per_tile[:, None] == per_tile[None, :]
    earlier = tile_index[None, :] < tile_index[:, None]
    return (same_protein & earlier).astype(jnp.float32)


def causal_mask():
    return (jnp.arange(TILE)[:, None] >= jnp.arange(TILE)[None, :]).astype(jnp.float32)


def fetch(shards):
    return (
        lax.all_gather(shards[0], ("dp", "fsdp"), axis=0, tiled=True),
        lax.all_gather(shards[1], ("dp", "fsdp"), axis=0, tiled=True),
        lax.all_gather(shards[2], ("dp", "fsdp"), axis=0, tiled=True),
        lax.all_gather(shards[3], ("dp", "fsdp"), axis=0, tiled=True),
        lax.all_gather(shards[4], ("dp", "fsdp"), axis=1, tiled=True),
    )


def attention_parts(qkv_low, omega, valid_mask, links):
    tokens = qkv_low.shape[0]
    tiles = tokens // TILE
    split = qkv_low.reshape(tokens, 3, HEADS, HD)
    queries = split[:, 0]
    key_rows = split[:, 1]
    value_rows = split[:, 2]
    proj_query = jnp.einsum("thd,hdm->thm", queries, omega, preferred_element_type=jnp.float32)
    proj_key = jnp.einsum("thd,hdm->thm", key_rows, omega, preferred_element_type=jnp.float32)
    exp_query = feature_map(proj_query, queries.astype(jnp.float32))
    exp_key = feature_map(proj_key, key_rows.astype(jnp.float32))
    query_feat = exp_query.astype(jnp.bfloat16).reshape(tiles, TILE, HEADS, FEAT)
    key_feat = (
        (exp_key * valid_mask[:, None, None]).astype(jnp.bfloat16).reshape(tiles, TILE, HEADS, FEAT)
    )
    value_tiles = value_rows.reshape(tiles, TILE, HEADS, HD)
    scores = jnp.einsum("cihm,cjhm->chij", query_feat, key_feat, preferred_element_type=jnp.float32)
    weights = (scores * causal_mask()).astype(jnp.bfloat16)
    tile_kv = jnp.einsum(
        "cjhm,cjhd->chmd", key_feat, value_tiles, preferred_element_type=jnp.float32
    )
    key_sums = jnp.sum(key_feat, axis=1, dtype=jnp.float32)
    prefix_state = jnp.einsum("cd,dhme->chme", links, tile_kv, precision=highest).astype(
        jnp.bfloat16
    )
    totals = jnp.einsum("cd,dhm->chm", links, key_sums, precision=highest).astype(jnp.bfloat16)
    numerator = jnp.einsum(
        "chij,cjhd->cihd", weights, value_tiles, preferred_element_type=jnp.float32
    ) + jnp.einsum("cihm,chmd->cihd", query_feat, prefix_state, preferred_element_type=jnp.float32)
    denominator = jnp.transpose(
        jnp.sum(weights, axis=-1, dtype=jnp.float32), (0, 2, 1)
    ) + jnp.einsum("cihm,chm->cih", query_feat, totals, preferred_element_type=jnp.float32)
    return (
        queries,
        key_rows,
        value_tiles,
        exp_query,
        exp_key,
        query_feat,
        key_feat,
        weights,
        prefix_state,
        totals,
        numerator,
        denominator,
    )


def feature_back(grad_feat, exp_feat, values_low, omega):
    feat_scale = HD ** (-0.25)
    weighted = grad_feat * exp_feat
    grad_proj = (weighted * feat_scale).astype(jnp.bfloat16)
    direct = (
        -jnp.sum(weighted, axis=-1, keepdims=True)
        * values_low.astype(jnp.float32)
        * (feat_scale * feat_scale)
    )
    return jnp.einsum("thm,hdm->thd", grad_proj, omega, preferred_element_type=jnp.float32) + direct


def attention_backward(qkv_low, omega, valid_mask, links, grad_attended):
    (
        queries,
        key_rows,
        value_tiles,
        exp_query,
        exp_key,
        query_feat,
        key_feat,
        weights,
        prefix_state,
        totals,
        numerator,
        denominator,
    ) = attention_parts(qkv_low, omega, valid_mask, links)
    tokens = qkv_low.shape[0]
    tiles = tokens // TILE
    grad_att = grad_attended.reshape(tiles, TILE, HEADS, HD)
    grad_num = (grad_att / denominator[..., None]).astype(jnp.bfloat16)
    grad_den = (-jnp.sum(grad_att * numerator, axis=-1) / (denominator * denominator)).astype(
        jnp.bfloat16
    )
    grad_weights = (
        jnp.einsum("cihd,cjhd->chij", grad_num, value_tiles, preferred_element_type=jnp.float32)
        + jnp.transpose(grad_den, (0, 2, 1)).astype(jnp.float32)[..., None]
    )
    grad_scores = grad_weights.astype(jnp.bfloat16) * causal_mask().astype(jnp.bfloat16)
    grad_values = jnp.einsum(
        "chij,cihd->cjhd", weights, grad_num, preferred_element_type=jnp.float32
    )
    grad_state = jnp.einsum(
        "cihm,cihd->chmd", query_feat, grad_num, preferred_element_type=jnp.float32
    )
    grad_totals = jnp.einsum(
        "cih,cihm->chm", grad_den, query_feat, preferred_element_type=jnp.float32
    )
    grad_kv = jnp.einsum("cd,chme->dhme", links, grad_state, precision=highest).astype(jnp.bfloat16)
    grad_sums = jnp.einsum("cd,chm->dhm", links, grad_totals, precision=highest)
    grad_qfeat = (
        jnp.einsum("cihd,chmd->cihm", grad_num, prefix_state, preferred_element_type=jnp.float32)
        + jnp.einsum("chij,cjhm->cihm", grad_scores, key_feat, preferred_element_type=jnp.float32)
        + grad_den.astype(jnp.float32)[..., None] * totals.astype(jnp.float32)[:, None]
    )
    grad_kfeat = (
        jnp.einsum("chij,cihm->cjhm", grad_scores, query_feat, preferred_element_type=jnp.float32)
        + jnp.einsum("cjhd,chmd->cjhm", value_tiles, grad_kv, preferred_element_type=jnp.float32)
        + grad_sums[:, None]
    )
    grad_values = grad_values + jnp.einsum(
        "cjhm,chmd->cjhd", key_feat, grad_kv, preferred_element_type=jnp.float32
    )
    grad_qfeat = grad_qfeat.reshape(tokens, HEADS, FEAT)
    grad_kfeat = grad_kfeat.reshape(tokens, HEADS, FEAT) * valid_mask[:, None, None]
    grad_query = feature_back(grad_qfeat, exp_query, queries, omega)
    grad_key = feature_back(grad_kfeat, exp_key, key_rows, omega)
    grad_value = grad_values.reshape(tokens, HEADS, HD)
    stacked = jnp.stack([grad_query, grad_key, grad_value], axis=1).reshape(tokens, 3 * HEADS * HD)
    return stacked.astype(jnp.bfloat16)


def on_device(
    inputs,
    cotangent,
    feature_omega,
    seg_start,
    seg_len,
    step_count,
    w_qkv,
    w_out,
    w_up,
    w_down,
    gains,
    m_qkv,
    m_out,
    m_up,
    m_down,
    m_gains,
    v_qkv,
    v_out,
    v_up,
    v_down,
    v_gains,
):
    shards = (w_qkv, w_out, w_up, w_down, gains)
    low_shards = tuple((piece.astype(jnp.bfloat16) for piece in shards))
    qkv_full, out_full, up_full, down_full, gain_full = fetch(low_shards)
    input_rows = inputs.astype(jnp.float32)
    tokens = input_rows.shape[0]
    valid_mask = token_mask(seg_len)
    links = tile_links(seg_start)
    gain_one = gain_full[0].astype(jnp.float32)
    gain_two = gain_full[1].astype(jnp.float32)
    normed = layer_norm(input_rows, gain_one).astype(jnp.bfloat16)
    qkv_low = jnp.dot(normed, qkv_full, preferred_element_type=jnp.float32).astype(jnp.bfloat16)
    parts = attention_parts(qkv_low, feature_omega, valid_mask, links)
    attended = (parts[10] / parts[11][..., None]).reshape(tokens, D).astype(jnp.bfloat16)
    middle = input_rows + jnp.dot(attended, out_full, preferred_element_type=jnp.float32)
    normed_two = layer_norm(middle, gain_two).astype(jnp.bfloat16)
    hidden = jnp.dot(normed_two, up_full, preferred_element_type=jnp.float32)
    active = gelu_exact(hidden).astype(jnp.bfloat16)
    result = middle + jnp.dot(active, down_full, preferred_element_type=jnp.float32)
    out_rows = result.astype(jnp.bfloat16)
    qkv_full, out_full, up_full, down_full, gain_full = fetch(low_shards)
    grad_rows_out = cotangent * valid_mask[:, None].astype(jnp.bfloat16)
    grad_down = jnp.einsum("tf,td->fd", active, grad_rows_out, preferred_element_type=jnp.float32)
    grad_active = jnp.einsum(
        "td,fd->tf", grad_rows_out, down_full, preferred_element_type=jnp.float32
    )
    gelu_value, gelu_pull = jax.vjp(gelu_exact, hidden)
    grad_hidden = gelu_pull(grad_active)[0].astype(jnp.bfloat16)
    grad_up = jnp.einsum("td,tf->df", normed_two, grad_hidden, preferred_element_type=jnp.float32)
    grad_normed_two = jnp.einsum(
        "tf,df->td", grad_hidden, up_full, preferred_element_type=jnp.float32
    )
    norm_value, norm_pull = jax.vjp(layer_norm, middle, gain_two)
    grad_mid_norm, grad_gain_two = norm_pull(grad_normed_two)
    grad_middle = grad_rows_out.astype(jnp.float32) + grad_mid_norm
    grad_branch = grad_middle.astype(jnp.bfloat16)
    grad_out = jnp.einsum("td,te->de", attended, grad_branch, preferred_element_type=jnp.float32)
    grad_attended = jnp.einsum(
        "te,de->td", grad_branch, out_full, preferred_element_type=jnp.float32
    )
    grad_qkv_low = attention_backward(qkv_low, feature_omega, valid_mask, links, grad_attended)
    grad_qkv = jnp.einsum("td,te->de", normed, grad_qkv_low, preferred_element_type=jnp.float32)
    grad_normed = jnp.einsum(
        "te,de->td", grad_qkv_low, qkv_full, preferred_element_type=jnp.float32
    )
    first_value, first_pull = jax.vjp(layer_norm, input_rows, gain_one)
    grad_rows_norm, grad_gain_one = first_pull(grad_normed)
    grad_inputs = grad_middle + grad_rows_norm
    grad_gain_rows = jnp.stack([grad_gain_one, grad_gain_two], axis=0)
    reduced = (
        lax.psum_scatter(grad_qkv, ("dp", "fsdp"), scatter_dimension=0, tiled=True),
        lax.psum_scatter(grad_out, ("dp", "fsdp"), scatter_dimension=0, tiled=True),
        lax.psum_scatter(grad_up, ("dp", "fsdp"), scatter_dimension=0, tiled=True),
        lax.psum_scatter(grad_down, ("dp", "fsdp"), scatter_dimension=0, tiled=True),
        lax.psum_scatter(grad_gain_rows, ("dp", "fsdp"), scatter_dimension=1, tiled=True),
    )
    local_squares = sum((jnp.sum(piece * piece) for piece in reduced))
    grad_norm = jnp.sqrt(lax.psum(local_squares, ("dp", "fsdp")))
    factor = jnp.minimum(1.0, clip_level / grad_norm)
    count = step_count.astype(jnp.float32)
    first_fix = 1.0 - jnp.power(beta_first, count)
    second_fix = 1.0 - jnp.power(beta_second, count)

    def update(weight, first, second, gradient, rate):
        clipped = gradient * factor
        first_new = beta_first * first + (1.0 - beta_first) * clipped
        second_new = beta_second * second + (1.0 - beta_second) * clipped * clipped
        direction = first_new / first_fix / (jnp.sqrt(second_new / second_fix) + adam_eps)
        return (clipped, second_new, weight - rate * (direction + decay_weight * weight))

    grad_qkv_c, var_qkv, new_qkv = update(w_qkv, m_qkv, v_qkv, reduced[0], rate_matrix)
    grad_out_c, var_out, new_out = update(w_out, m_out, v_out, reduced[1], rate_matrix)
    grad_up_c, var_up, new_up = update(w_up, m_up, v_up, reduced[2], rate_matrix)
    grad_down_c, var_down, new_down = update(w_down, m_down, v_down, reduced[3], rate_matrix)
    grad_gains_c, var_gains, new_gains = update(gains, m_gains, v_gains, reduced[4], rate_gain)
    return (
        out_rows,
        grad_inputs,
        grad_norm,
        grad_qkv_c,
        var_qkv,
        new_qkv,
        grad_out_c,
        var_out,
        new_out,
        grad_up_c,
        var_up,
        new_up,
        grad_down_c,
        var_down,
        new_down,
        grad_gains_c,
        var_gains,
        new_gains,
    )


def solution(mesh):
    return jax.shard_map(
        on_device,
        mesh=mesh,
        in_specs=(
            P(("dp", "fsdp"), None),
            P(("dp", "fsdp"), None),
            P(),
            P(("dp", "fsdp")),
            P(("dp", "fsdp")),
            P(),
            P(("dp", "fsdp"), None),
            P(("dp", "fsdp"), None),
            P(("dp", "fsdp"), None),
            P(("dp", "fsdp"), None),
            P(None, ("dp", "fsdp")),
            P(("dp", "fsdp"), None),
            P(("dp", "fsdp"), None),
            P(("dp", "fsdp"), None),
            P(("dp", "fsdp"), None),
            P(None, ("dp", "fsdp")),
            P(("dp", "fsdp"), None),
            P(("dp", "fsdp"), None),
            P(("dp", "fsdp"), None),
            P(("dp", "fsdp"), None),
            P(None, ("dp", "fsdp")),
        ),
        out_specs=(
            P(("dp", "fsdp"), None),
            P(("dp", "fsdp"), None),
            P(),
            P(("dp", "fsdp"), None),
            P(("dp", "fsdp"), None),
            P(("dp", "fsdp"), None),
            P(("dp", "fsdp"), None),
            P(("dp", "fsdp"), None),
            P(("dp", "fsdp"), None),
            P(("dp", "fsdp"), None),
            P(("dp", "fsdp"), None),
            P(("dp", "fsdp"), None),
            P(("dp", "fsdp"), None),
            P(("dp", "fsdp"), None),
            P(("dp", "fsdp"), None),
            P(None, ("dp", "fsdp")),
            P(None, ("dp", "fsdp")),
            P(None, ("dp", "fsdp")),
        ),
        check_vma=False,
    )
```

profile of v0, /device:TPU:0, one launch (start us, length us, event | category | flops | bytes accessed | tf_op | source)
XLA Modules:
  0.0 1137.5 jit_solution(6331408006338267767)
XLA Ops:
  7.2 1.6 convert_element_type.175
  8.9 1.5 convert_element_type.193
  10.5 1.5 convert_element_type.195
  15.2 43.0 %all-gather = bf16[32,16,2]{1,2,0:T(2,128)(2,1)S(1)} all-gather(bf16[1,16,2]{1,2,0:T(2,128)(2,1)S(1)} %convert_bitcast_fusion), channel_id=1, replica_groups=mesh['dp'=4,'fsdp'=8] {'dp','fsdp'}, dimensions={0}, use_global_device_ids=true | all-gather | bytes 2112 | tf_op jit(solution)/shard_map/all_gather | solution.py:65
  59.8 39.4 %all_gather.21 = bf16[512,512]{1,0:T(8,128)(2,1)S(1)} all-gather(bf16[16,512]{1,0:T(8,128)(2,1)S(1)} %convert_element_type.191), channel_id=1, replica_groups=mesh['dp'=4,'fsdp'=8] {'dp','fsdp'}, dimensions={0}, use_global_device_ids=true | all-gather | bytes 540672 | tf_op jit(solution)/shard_map/all_gather | solution.py:62
  99.2 3.1 copy.102
  103.4 4.0 copy.117
  107.3 5.3 convolution_convert_fusion
  114.0 2.1 copy.157
  116.1 7.6 fusion.9
  123.7 10.1 convert_reduce_fusion
  135.1 1.4 fusion.24
  137.2 5.2 fusion.63
  142.4 2.3 fusion.57
  144.7 4.7 fusion.53
  149.4 11.5 %convert_reduce_fusion.1 = (f32[8,8,256]{2,1,0:T(8,128)S(1)}, bf16[8,8,256,256]{2,3,1,0:T(8,128)(2,1)}) fusion(f32[256,256]{0,1:T(8,128)S(1)} %fusion.89, bf16[8,256,8,256]{3,1,0,2:T(8,128)(2,1)} %bitcast.190, bf16[8,256,8,256]{3,1,0,2:T(8,128)(2,1)} %bitcast.183), kind=kOutput, calls=%fused_computation.29 | convolution fusion | flops 2164244480 | bytes 25493504 | tf_op jit(solution)/shard_map/cihm,cjhm->chij/dot_general | solution.py:85
  160.8 9.0 fusion.42
  171.9 1.5 fusion.132
  173.4 2.0 copy-done.8
  176.5 46.2 %multiply_convert_fusion.2 = (bf16[2048,2048]{1,0:T(8,128)(2,1)}, f32[2048,2048]{1,0:T(8,128)}, f32[2048,2048]{1,0:T(8,128)}) fusion(bf16[512,2048]{1,0:T(8,128)(2,1)} %all-gather.7.cloned.1.call-done, f32[2048,512]{0,1:T(8,128)} %copy-done.8, f32[512]{0:T(512)S(1)} %bitcast.230, f32[2048]{0:T(1024)S(1)} %fusion.105, f32[2048]{0:T(1024)S(1)} %broadcast_multiply_fusion.6), kind=kOutput, calls=%fused_computation.15 | convolution fusion | flops 4571791360 | bytes 48252928 | tf_op jit(solution)/shard_map/dot_general | solution.py:227
  222.7 18.1 %add_convert_fusion.1 = bf16[2048,2048]{1,0:T(8,128)(2,1)} fusion(f32[2048,2048]{1,0:T(8,128)} %get-tuple-element.102, f32[2048,2048]{1,0:T(8,128)} %get-tuple-element.118, bf16[2048,512]{1,0:T(8,128)(2,1)} %all-gather.9.cloned.1.call-done, bf16[2048,512]{0,1:T(8,128)(2,1)S(1)} %copy-done.13, bf16[2048]{0:T(1024)(128)(2,1)S(1)} %bitcast.218), kind=kOutput, calls=%fused_computation.14 | convolution fusion | flops 4354736128 | bytes 46141440 | tf_op jit(solution)/shard_map/td,fd->tf/dot_general | solution.py:234
  240.9 11.0 multiply_reduce_fusion
  251.9 1.5 fusion.130
  256.8 2.0 copy.160
  259.0 2.4 fusion.43
  261.7 3.8 fusion.50
  265.5 5.6 add_convert_fusion
  271.1 13.0 %fusion.14 = f32[8,8,256,256]{2,3,1,0:T(8,128)} fusion(bf16[8,8,256,256]{3,2,1,0:T(8,128)(2,1)} %add_convert_fusion, bf16[256,256]{1,0:T(8,128)(2,1)S(1)} %copy-done.24, bf16[8,256,8,256]{3,1,0,2:T(8,128)(2,1)} %bitcast.184), kind=kOutput, calls=%fused_computation.39 | convolution fusion | flops 2151677952 | bytes 33685504 | tf_op jit(solution)/shard_map/chij,cihm->cjhm/dot_general | solution.py:173
  284.1 13.9 %fusion.16 = f32[8,8,256,256]{2,3,1,0:T(8,128)} fusion(bf16[8,8,256,256]{3,2,1,0:T(8,128)(2,1)} %add_convert_fusion, bf16[8,256,8,256]{3,1,0,2:T(8,128)(2,1)} %bitcast.191, bf16[256,256]{1,0:T(8,128)(2,1)S(1)} %copy-done.24), kind=kOutput, calls=%fused_computation.41 | convolution fusion | flops 2164260864 | bytes 33685504 | tf_op jit(solution)/shard_map/chij,cjhm->cihm/dot_general | solution.py:169
  298.0 4.7 fusion.55
  303.0 4.3 fusion.66
  308.6 6.2 fusion.22
  314.8 4.0 fusion.73
  318.8 4.5 copy.138
  323.3 4.2 stack_reshape.4
  327.5 13.8 %bitcast_add_fusion = f32[8,256,8,256]{3,1,2,0:T(8,128)} fusion(f32[8,8,256,256]{2,3,1,0:T(8,128)} %fusion.16, bf16[8,256,8,64]{1,3,2,0:T(8,128)(2,1)S(1)} %get-tuple-element.106, f32[8,8,256]{2,1,0:T(8,128)S(1)} %copy-done.39, f32[8,256,8]{1,2,0:T(8,128)S(1)} %get-tuple-element.95, bf16[8,8,256,64]{2,0,3,1:T(8,128)(2,1)} %fusion.63), kind=kOutput, calls=%fused_computation.5 | convolution fusion | flops 549453824 | bytes 37879808 | tf_op jit(solution)/shard_map/cihd,chmd->cihm/dot_general | solution.py:168
  341.2 6.8 copy.126
  348.1 13.9 %fusion.126 = (f32[2048,8]{0,1:T(8,128)S(1)}, f32[2048,8,256]{2,0,1:T(8,128)}) fusion(f32[2048,8]{0,1:T(8,128)S(1)} %copy-done.28, f32[8,2048,256]{2,1,0:T(8,128)} %get-tuple-element.110, f32[8,256,8,256]{3,1,0,2:T(8,128)S(1)} %copy.126), kind=kLoop, calls=%fused_computation.202 | loop fusion | flops 16760832 | bytes 50462720 | tf_op jit(solution)/shard_map/reduce_sum | solution.py:122
  362.1 10.7 add_bitcast_fusion
  372.7 6.8 copy.134
  379.6 14.6 %fusion.128 = (f32[2048,8]{0,1:T(8,128)S(1)}, f32[2048,8,256]{2,0,1:T(8,128)}) fusion(f32[2048,8]{0,1:T(8,128)S(1)} %copy-done.26, f32[8,2048,256]{2,1,0:T(8,128)} %get-tuple-element.111, f32[2048]{0:T(1024)S(1)} %bitcast.217, f32[8,256,8,256]{3,1,0,2:T(8,128)S(1)} %copy.134), kind=kLoop, calls=%fused_computation.204 | loop fusion | flops 20955136 | bytes 50470912 | tf_op jit(solution)/shard_map/reduce_sum | solution.py:122
  394.2 10.4 fusion.61
  404.5 10.3 fusion.60
  414.9 3.7 pad_maximum_fusion
  418.8 3.5 fusion.41
  422.4 2.0 copy-done.17
  424.3 1.7 fusion.31
  427.0 4.5 fusion.133
  431.7 7.9 fusion.86
  439.7 11.2 fusion.119
  451.6 10.7 fusion.80
  463.0 11.1 add_convert_fusion.3
  474.2 3.9 copy.139
  478.1 6.4 add_add_fusion.2
  484.5 73.4 %reduce-scatter.16.cloned.1.call-done = f32[16,2]{1,0:T(8,128)} async-done(((f32[512,2]{1,0:T(8,128)}), f32[16,2]{1,0:T(8,128)}) %reduce-scatter.16.cloned.1.call-update) | async-done | bytes 144
  559.3 132.0 %reduce-scatter.10.cloned.1.call-done = f32[16,512]{1,0:T(8,128)} async-done(((f32[512,512]{1,0:T(8,128)}), f32[16,512]{1,0:T(8,128)}) %reduce-scatter.10.cloned.1.call-update) | async-done | bytes 32784 | tf_op jit(solution)/shard_map/reduce_scatter | solution.py:262
  692.6 101.4 %reduce-scatter.8.cloned.1.call-done = f32[16,1536]{1,0:T(8,128)} async-done(((f32[512,1536]{1,0:T(8,128)}), f32[16,1536]{1,0:T(8,128)}) %reduce-scatter.8.cloned.1.call-update) | async-done | bytes 98320 | tf_op jit(solution)/shard_map/reduce_scatter | solution.py:261
  794.0 1.5 multiply_reduce_fusion.5
  796.8 140.9 %reduce-scatter.12.cloned.1.call-done = f32[16,2048]{1,0:T(8,128)} async-done(((f32[512,2048]{1,0:T(8,128)}), f32[16,2048]{1,0:T(8,128)}) %reduce-scatter.12.cloned.1.call-update) | async-done | bytes 131088 | tf_op jit(solution)/shard_map/reduce_scatter | solution.py:263
  937.7 1.5 multiply_reduce_fusion.4
  939.9 139.6 %reduce-scatter.14.cloned.1.call-done = f32[64,512]{1,0:T(8,128)} async-done(((f32[2048,512]{1,0:T(8,128)}), f32[64,512]{1,0:T(8,128)}) %reduce-scatter.14.cloned.1.call-update) | async-done | bytes 131088 | tf_op jit(solution)/shard_map/reduce_scatter | solution.py:264
  1079.5 1.5 multiply_reduce_fusion.3
  1082.6 5.5 copy.140
  1088.1 36.8 %psum.7 = f32[]{:T(128)} all-reduce(f32[]{:T(128)S(6)} %add.218), channel_id=1, replica_groups=mesh['dp'=4,'fsdp'=8] {'dp','fsdp'}, use_global_device_ids=true, to_apply=%region_28.29 | all-reduce | flops 1 | bytes 8 | tf_op jit(solution)/shard_map/psum | solution.py:268
  (240 shorter events, 26.1 us)
Async XLA Ops:
  7.2 109.0 %copy-start = (bf16[8,64,256]{2,1,0:T(8,128)(2,1)S(1)}, bf16[8,64,256]{2,1,0:T(8,128)(2,1)}, u32[]{:S(2)}) copy-start(bf16[8,64,256]{2,1,0:T(8,128)(2,1)} %param.23) | copy-start | bytes 786436
  7.2 100.1 %all-gather.5.cloned.1.call-start = ((), (), s32[]{:S(2)}) async-start(), calls=%async_computation.5 | async-start | bytes 1622016 | tf_op jit(solution)/shard_map/all_gather | solution.py:61
  8.8 167.7 %all-gather.7.cloned.1.call-start = ((), (), s32[]{:S(2)}) async-start(), calls=%async_computation.6 | async-start | bytes 2162688 | tf_op jit(solution)/shard_map/all_gather | solution.py:63
  10.4 212.3 %all-gather.9.cloned.1.call-start = ((), (), s32[]{:S(2)}) async-start(), calls=%async_computation.7 | async-start | bytes 2162688 | tf_op jit(solution)/shard_map/all_gather | solution.py:64
  12.1 545.8 %reduce-scatter.16.cloned.1.call-start = ((), (), s32[]{:S(2)}) async-start(), calls=%async_computation.12 | async-start | bytes 270336
  13.4 110.3 %copy-start.50 = (f32[1,8,2,128]{3,1,2,0:T(8,128)}, f32[1,8,2,128]{3,1,2,0:T(8,128)S(1)}, u32[]{:S(2)}) copy-start(f32[1,8,2,128]{3,1,2,0:T(8,128)S(1)} %copy.229) | copy-start | bytes 24580
  14.5 122.0 %copy-start.70 = (s32[8]{0:T(128)}, s32[8]{0:T(128)S(1)}, u32[]{:S(2)}) copy-start(s32[8]{0:T(128)S(1)} %eq.15) | copy-start | bytes 100
  58.3 49.0 %copy-start.72 = (f32[1,512]{1,0:T(1,128)}, f32[1,512]{1,0:T(1,128)S(1)}, u32[]{:S(2)}) copy-start(f32[1,512]{1,0:T(1,128)S(1)} %get-tuple-element.108) | copy-start | bytes 6148
  58.3 193.6 %copy-start.74 = (f32[1,512]{1,0:T(1,128)}, f32[1,512]{1,0:T(1,128)S(1)}, u32[]{:S(2)}) copy-start(f32[1,512]{1,0:T(1,128)S(1)} %get-tuple-element.107) | copy-start | bytes 6148
  99.2 72.6 %copy-start.21 = (bf16[512,512]{1,0:T(8,128)(2,1)}, bf16[512,512]{1,0:T(8,128)(2,1)S(1)}, u32[]{:S(2)}) copy-start(bf16[512,512]{1,0:T(8,128)(2,1)S(1)} %all_gather.21) | copy-start | bytes 1572868
  102.4 69.5 %copy-start.3 = (bf16[2048,512]{0,1:T(8,128)(2,1)}, bf16[2048,512]{0,1:T(8,128)(2,1)S(1)}, u32[]{:S(2)}) copy-start(bf16[2048,512]{0,1:T(8,128)(2,1)S(1)} %copy.102) | copy-start | bytes 6291460
  102.8 9.9 copy-start.42
  103.3 9.3 copy-start.58
  103.4 9.3 copy-start.54
  116.1 7.6 copy-start.27
  116.1 7.6 copy-start.25
  123.7 21.0 %copy-start.1 = (bf16[2048,8,256]{2,0,1:T(8,128)(2,1)}, bf16[2048,8,256]{2,0,1:T(8,128)(2,1)S(1)}, u32[]{:S(2)}) copy-start(bf16[2048,8,256]{2,0,1:T(8,128)(2,1)S(1)} %get-tuple-element.109) | copy-start | bytes 25165828
  123.7 11.4 copy-start.5
  144.7 16.1 %copy-start.29 = (f32[8,8,1,256]{3,2,1,0:T(1,128)}, f32[8,8,1,256]{3,2,1,0:T(1,128)S(1)}, u32[]{:S(2)}) copy-start(f32[8,8,1,256]{3,2,1,0:T(1,128)S(1)} %fusion.57) | copy-start | bytes 196612
  160.8 9.0 copy-start.40
  160.8 9.0 copy-start.31
  173.4 78.5 %copy-start.62 = (f32[2048]{0:T(1024)}, f32[2048]{0:T(1024)S(1)}, u32[]{:S(2)}) copy-start(f32[2048]{0:T(1024)S(1)} %broadcast_multiply_fusion.6) | copy-start | bytes 24580
  176.5 75.4 %copy-start.68 = (f32[2048]{0:T(1024)}, f32[2048]{0:T(1024)S(1)}, u32[]{:S(2)}) copy-start(f32[2048]{0:T(1024)S(1)} %fusion.105) | copy-start | bytes 24580
  176.5 46.2 %copy-start.13 = (bf16[2048,512]{0,1:T(8,128)(2,1)S(1)}, bf16[2048,512]{0,1:T(8,128)(2,1)}, u32[]{:S(2)}) copy-start(bf16[2048,512]{0,1:T(8,128)(2,1)} %copy.117) | copy-start | bytes 6291460
  176.5 46.2 %copy-start.64 = (bf16[1,8,2,128]{3,1,2,0:T(8,128)(2,1)S(1)}, bf16[1,8,2,128]{3,1,2,0:T(8,128)(2,1)}, u32[]{:S(2)}) copy-start(bf16[1,8,2,128]{3,1,2,0:T(8,128)(2,1)} %copy.230) | copy-start | bytes 12292
  240.8 11.0 copy-start.61
  240.9 11.0 copy-start.9
  265.5 5.6 copy-start.24
  298.0 5.0 copy-start.12
  303.0 11.8 %slice-start.2 = ((s8[8388608]{0:T(1024)(128)(4,1)}), s8[4194304]{0:T(1024)(128)(4,1)S(1)}, s32[]{:S(2)}) async-start(s8[8388608]{0:T(1024)(128)(4,1)} %bitcast.207), calls=%async_computation.15 | async-start | bytes 8388608
  308.6 6.2 slice-start.3
  318.8 8.7 copy-start.39
  341.2 6.8 copy-start.28
  348.1 14.0 %copy-start.7 = (bf16[64,8,8,256]{3,2,1,0:T(8,128)(2,1)S(1)}, bf16[64,8,8,256]{3,2,1,0:T(8,128)(2,1)}, u32[]{:S(2)}) copy-start(bf16[64,8,8,256]{3,2,1,0:T(8,128)(2,1)} %copy.157) | copy-start | bytes 6291460
  348.1 14.0 %copy-start.16 = (bf16[8,8,256,64]{2,0,3,1:T(8,128)(2,1)S(1)}, bf16[8,8,256,64]{2,0,3,1:T(8,128)(2,1)}, u32[]{:S(2)}) copy-start(bf16[8,8,256,64]{2,0,3,1:T(8,128)(2,1)} %copy-done.15) | copy-start | bytes 6291460
  372.7 6.8 copy-start.26
  372.7 6.8 copy-start.51
  418.8 5.5 copy-start.55
  427.0 264.3 %reduce-scatter.10.cloned.1.call-start = ((), (), s32[]{:S(2)}) async-start(), calls=%async_computation.9 | async-start | bytes 1081344 | tf_op jit(solution)/shard_map/reduce_scatter | solution.py:262
  431.5 8.2 copy-start.63
  431.5 8.2 copy-start.69
  431.5 8.2 copy-start.75
  431.5 362.5 %reduce-scatter.8.cloned.1.call-start = ((), (), s32[]{:S(2)}) async-start(), calls=%async_computation.8 | async-start | bytes 3244032 | tf_op jit(solution)/shard_map/reduce_scatter | solution.py:261
  439.7 498.0 %reduce-scatter.12.cloned.1.call-start = ((), (), s32[]{:S(2)}) async-start(), calls=%async_computation.10 | async-start | bytes 4325376 | tf_op jit(solution)/shard_map/reduce_scatter | solution.py:263
  451.0 628.6 %reduce-scatter.14.cloned.1.call-start = ((), (), s32[]{:S(2)}) async-start(), calls=%async_computation.11 | async-start | bytes 4325376 | tf_op jit(solution)/shard_map/reduce_scatter | solution.py:264
  1082.3 43.3 %copy-start.77 = (f32[2,16]{1,0:T(2,128)S(1)}, f32[2,16]{1,0:T(2,128)}, u32[]{:S(2)}) copy-start(f32[2,16]{1,0:T(2,128)} %param.31) | copy-start | bytes 388
  1082.4 43.3 %copy-start.78 = (f32[2,16]{1,0:T(2,128)S(1)}, f32[2,16]{1,0:T(2,128)}, u32[]{:S(2)}) copy-start(f32[2,16]{1,0:T(2,128)} %param.36) | copy-start | bytes 388
  1082.4 43.3 %copy-start.79 = (f32[2,16]{1,0:T(2,128)S(1)}, f32[2,16]{1,0:T(2,128)}, u32[]{:S(2)}) copy-start(f32[2,16]{1,0:T(2,128)} %param.41) | copy-start | bytes 388
  1082.4 43.9 %copy-start.44 = (f32[16,512]{1,0:T(8,128)S(1)}, f32[16,512]{1,0:T(8,128)}, u32[]{:S(2)}) copy-start(f32[16,512]{1,0:T(8,128)} %param.28) | copy-start | bytes 98308
  1082.4 43.9 %copy-start.45 = (f32[16,512]{1,0:T(8,128)S(1)}, f32[16,512]{1,0:T(8,128)}, u32[]{:S(2)}) copy-start(f32[16,512]{1,0:T(8,128)} %reduce-scatter.10.cloned.1.call-done) | copy-start | bytes 98308
  1082.4 43.9 %copy-start.66 = (f32[16,512]{1,0:T(8,128)S(1)}, f32[16,512]{1,0:T(8,128)}, u32[]{:S(2)}) copy-start(f32[16,512]{1,0:T(8,128)} %param.33) | copy-start | bytes 98308
  1082.4 43.9 %copy-start.67 = (f32[16,512]{1,0:T(8,128)S(1)}, f32[16,512]{1,0:T(8,128)}, u32[]{:S(2)}) copy-start(f32[16,512]{1,0:T(8,128)} %param.38) | copy-start | bytes 98308
  1082.4 44.5 %copy-start.37 = (f32[16,1536]{1,0:T(8,128)S(1)}, f32[16,1536]{1,0:T(8,128)}, u32[]{:S(2)}) copy-start(f32[16,1536]{1,0:T(8,128)} %param.27) | copy-start | bytes 294916
  1082.4 44.5 %copy-start.38 = (f32[16,1536]{1,0:T(8,128)S(1)}, f32[16,1536]{1,0:T(8,128)}, u32[]{:S(2)}) copy-start(f32[16,1536]{1,0:T(8,128)} %reduce-scatter.8.cloned.1.call-done) | copy-start | bytes 294916
  1082.5 44.5 %copy-start.52 = (f32[16,1536]{1,0:T(8,128)S(1)}, f32[16,1536]{1,0:T(8,128)}, u32[]{:S(2)}) copy-start(f32[16,1536]{1,0:T(8,128)} %param.32) | copy-start | bytes 294916
  1082.5 44.5 %copy-start.53 = (f32[16,1536]{1,0:T(8,128)S(1)}, f32[16,1536]{1,0:T(8,128)}, u32[]{:S(2)}) copy-start(f32[16,1536]{1,0:T(8,128)} %param.37) | copy-start | bytes 294916
  1082.5 45.2 %copy-start.33 = (f32[64,512]{1,0:T(8,128)S(1)}, f32[64,512]{1,0:T(8,128)}, u32[]{:S(2)}) copy-start(f32[64,512]{1,0:T(8,128)} %param.30) | copy-start | bytes 393220
  1082.5 45.2 %copy-start.36 = (f32[64,512]{1,0:T(8,128)S(1)}, f32[64,512]{1,0:T(8,128)}, u32[]{:S(2)}) copy-start(f32[64,512]{1,0:T(8,128)} %reduce-scatter.14.cloned.1.call-done) | copy-start | bytes 393220
  1082.5 45.2 %copy-start.46 = (f32[64,512]{1,0:T(8,128)S(1)}, f32[64,512]{1,0:T(8,128)}, u32[]{:S(2)}) copy-start(f32[64,512]{1,0:T(8,128)} %param.35) | copy-start | bytes 393220
  1082.5 45.2 %copy-start.47 = (f32[64,512]{1,0:T(8,128)S(1)}, f32[64,512]{1,0:T(8,128)}, u32[]{:S(2)}) copy-start(f32[64,512]{1,0:T(8,128)} %param.40) | copy-start | bytes 393220
  1082.5 46.0 %copy-start.34 = (f32[16,2048]{1,0:T(8,128)S(1)}, f32[16,2048]{1,0:T(8,128)}, u32[]{:S(2)}) copy-start(f32[16,2048]{1,0:T(8,128)} %param.29) | copy-start | bytes 393220
  1082.5 46.0 %copy-start.35 = (f32[16,2048]{1,0:T(8,128)S(1)}, f32[16,2048]{1,0:T(8,128)}, u32[]{:S(2)}) copy-start(f32[16,2048]{1,0:T(8,128)} %reduce-scatter.12.cloned.1.call-done) | copy-start | bytes 393220
  1082.5 46.0 %copy-start.48 = (f32[16,2048]{1,0:T(8,128)S(1)}, f32[16,2048]{1,0:T(8,128)}, u32[]{:S(2)}) copy-start(f32[16,2048]{1,0:T(8,128)} %param.34) | copy-start | bytes 393220
  1082.6 46.0 %copy-start.49 = (f32[16,2048]{1,0:T(8,128)S(1)}, f32[16,2048]{1,0:T(8,128)}, u32[]{:S(2)}) copy-start(f32[16,2048]{1,0:T(8,128)} %param.39) | copy-start | bytes 393220
  (29 other events, 83.0 us)
Sparse Core Ops, SparseCore 0:
  11.6 58.1 all-gather.4
  73.4 55.3 all-gather.6
  132.3 55.3 all-gather.8
  427.1 130.7 reduce-scatter.15
  560.1 131.1 reduce-scatter.9
  696.5 97.4 reduce-scatter.7
  796.3 141.3 reduce-scatter.11
  940.0 139.5 reduce-scatter.13
where the time goes:
time: 1150 us; the launch traced here: 1140 us
  waiting for transfers between devices  587 us (51%)
  matrix products  285 us (25%)
  blocking collectives  119 us (10%)
  other arithmetic  65.6 us (6%)
  local copies, waits for them, and re-layouts  58.5 us (5%)
  between operations  21.3 us (2%)
    reduce_scatter x1, waiting for transfers between devices, on_device(): lax.psum_scatter(grad_up, ('dp', 'fsdp'), scatter_dimension=0, tiled=True)  141 us
    reduce_scatter x1, waiting for transfers between devices, on_device(): lax.psum_scatter(grad_down, ('dp', 'fsdp'), scatter_dimension=0, tiled=True)  140 us
    reduce_scatter x1, waiting for transfers between devices, on_device(): lax.psum_scatter(grad_out, ('dp', 'fsdp'), scatter_dimension=0, tiled=True)  132 us
    reduce_scatter x1, waiting for transfers between devices, on_device(): lax.psum_scatter(grad_qkv, ('dp', 'fsdp'), scatter_dimension=0, tiled=True)  101 us
    unnamed x9, waiting for transfers between devices  73.5 us
    dot_general x1, matrix products, on_device(): hidden = jnp.dot(normed_two, up_full, preferred_element_type=jnp.float32)  46.2 us
    all_gather x1, blocking collectives, fetch(): lax.all_gather(shards[4], ('dp', 'fsdp'), axis=1, tiled=True)  43 us
    all_gather x1, blocking collectives, fetch(): lax.all_gather(shards[1], ('dp', 'fsdp'), axis=0, tiled=True)  39.4 us
  transfers between devices with their start and end apart: 8, of which 5 were waited for; matrix products, arithmetic and copies ran while one was open for 17% of the time, Pallas kernels for 0%

commit v1 on v0

v1 whole, which is shorter than its diff:
```python
import functools
import math

import jax
import jax.numpy as jnp
from jax import lax
from jax.experimental import pallas as pl
from jax.experimental.pallas import tpu as pltpu
from jax.sharding import PartitionSpec as P

D = 512
HEADS = 8
HD = 64
FEAT = 256
FF = 2048
SEG = 1024
TILE = 256
PAIRS = HEADS // 2
WIDE = 3 * D

norm_eps = 1e-05
clip_level = 1.0
rate_matrix = 0.03
rate_gain = 0.4
beta_first = 0.9
beta_second = 0.95
adam_eps = 1e-08
decay_weight = 0.1

feat_scale = HD ** (-0.25)
log2_e = math.log2(math.e)
f32 = jnp.float32
bf16 = jnp.bfloat16
MESH = pl.DeviceIdType.MESH


def dot_nn(a, b):
    return lax.dot_general(a, b, (((1,), (0,)), ((), ())), preferred_element_type=f32)


def dot_nt(a, b):
    return lax.dot_general(a, b, (((1,), (1,)), ((), ())), preferred_element_type=f32)


def dot_tn(a, b):
    return lax.dot_general(a, b, (((0,), (0,)), ((), ())), preferred_element_type=f32)


def normalise(rows):
    centred = rows - jnp.mean(rows, axis=-1, keepdims=True)
    spread = jnp.mean(centred * centred, axis=-1, keepdims=True)
    inverse = lax.rsqrt(spread + norm_eps)
    return centred * inverse, inverse


def normalise_back(grad, gain, unit, inverse):
    scaled = grad * gain
    first = jnp.mean(scaled, axis=-1, keepdims=True)
    second = jnp.mean(scaled * unit, axis=-1, keepdims=True)
    return inverse * (scaled - first - unit * second)


def lane_masks(rows):
    lane = lax.broadcasted_iota(jnp.int32, (rows, 2 * HD), 1)
    return lane, lane < HD


def with_ones(value_pair, low):
    wide = value_pair.astype(f32)
    return (
        jnp.where(low, wide, 1.0).astype(bf16),
        jnp.where(low, 1.0, wide).astype(bf16),
    )


def valid_rows(tile, lens_ref):
    per_seg = SEG // TILE
    place = lax.broadcasted_iota(jnp.int32, (TILE, 1), 0) + (tile % per_seg) * TILE
    return (place < lens_ref[tile // per_seg]).astype(f32)


AXES = ("dp", "fsdp")
EXTRA = 128
FULL = WIDE + EXTRA
ROWS = {"qkv": 16, "out": 16, "up": 16, "down": 64}
COLS = {"qkv": FULL, "out": D, "up": FF, "down": D}
LATE = ("out", "up", "down")


def place():
    dp, inner = lax.axis_index("dp"), lax.axis_index("fsdp")
    z, core = inner // 2, inner % 2
    y, x = dp // 2, dp % 2
    across = y * 2 + (1 - x)
    along = (1 - y) * 2 + x
    return {
        "dp": dp, "z": z, "core": core,
        "first": core * along + (1 - core) * across,
        "second": core * across + (1 - core) * along,
        "diag": (1 - y) * 2 + (1 - x),
    }


def greet(devices):
    barrier = pltpu.get_barrier_semaphore()
    for device in devices:
        pl.semaphore_signal(barrier, inc=1, device_id=device, device_id_type=MESH)
    pl.semaphore_wait(barrier, len(devices))


def near_devices(at):
    devices = [{"fsdp": (at["z"] + i) % 4 * 2 + at["core"]} for i in range(1, 4)]
    devices += [{"fsdp": at["z"] * 2 + 1 - at["core"]}]
    devices += [{"dp": at["first"]}, {"dp": at["second"]}]
    return devices


def gather_copy(at, own, full, send, recv, k):
    dp, z, core = at["dp"], at["z"], at["core"]
    sibling = {"fsdp": z * 2 + 1 - core}
    if k < 3:
        src, dst, device = own, full.at[dp, z, core], {"fsdp": (z + 1 + k) % 4 * 2 + core}
    else:
        which = {3: "dp", 4: "dp", 5: "dp", 6: "first", 7: "first", 8: "second", 9: "diag"}[k]
        src = dst = full.at[at[which], :, core]
        device = {4: {"dp": at["first"]}, 5: {"dp": at["second"]}, 6: {"dp": at["second"]}}.get(k, sibling)
    return pltpu.make_async_remote_copy(
        src_ref=src, dst_ref=dst, send_sem=send.at[k], recv_sem=recv.at[k],
        device_id=device, device_id_type=MESH,
    )


def attention_forward_tile(
    tile, starts_ref, lens_ref, x_ref, weight, gain_row, omega_ref,
    qkv_ref, fq_ref, fk_ref, o_ref, rden_ref, prefix_ref, state_ref,
):
    per_seg = SEG // TILE

    @pl.when(tile % per_seg == 0)
    def _():
        begins = jnp.logical_or(tile == 0, starts_ref[tile // per_seg] != 0)
        state_ref[...] = jnp.where(begins, 0.0, state_ref[...])

    unit, _ = normalise(x_ref[...].astype(f32))
    normed = (unit * gain_row).astype(bf16)
    qkv_ref[...] = dot_nn(normed, weight()).astype(bf16)
    valid = valid_rows(tile, lens_ref)
    _, low = lane_masks(TILE)
    causal = lax.broadcasted_iota(jnp.int32, (TILE, TILE), 0) >= lax.broadcasted_iota(
        jnp.int32, (TILE, TILE), 1
    )
    for pair in range(PAIRS):
        lanes = slice(pair * 2 * HD, (pair + 1) * 2 * HD)
        feats = []
        for part in range(2):
            rows = qkv_ref[:, part * D + pair * 2 * HD : part * D + (pair + 1) * 2 * HD]
            wide = rows.astype(f32)
            square = wide * wide
            proj = dot_nn(rows, omega_ref[pair])
            for odd in range(2):
                total = jnp.sum(
                    jnp.where(low, 0.0, square) if odd else jnp.where(low, square, 0.0),
                    axis=-1, keepdims=True,
                )
                value = jnp.exp2(
                    proj[:, odd * FEAT : (odd + 1) * FEAT] * (feat_scale * log2_e)
                    - total * (0.5 * feat_scale * feat_scale * log2_e)
                )
                if part:
                    value = value * valid
                feats.append(value.astype(bf16))
        value_pair = qkv_ref[:, 2 * D + pair * 2 * HD : 2 * D + (pair + 1) * 2 * HD]
        ones = with_ones(value_pair, low)
        mixed = []
        for odd in range(2):
            head = 2 * pair + odd
            query_feat, key_feat = feats[odd], feats[2 + odd]
            fq_ref[:, head * FEAT : (head + 1) * FEAT] = query_feat
            fk_ref[:, head * FEAT : (head + 1) * FEAT] = key_feat
            weights = jnp.where(causal, dot_nt(query_feat, key_feat), 0.0).astype(bf16)
            before = state_ref[head]
            before_low = before.astype(bf16)
            prefix_ref[0, head] = before_low
            mixed.append(dot_nn(weights, ones[odd]) + dot_nt(query_feat, before_low))
            state_ref[head] = before + dot_tn(ones[odd], key_feat)
        top = jnp.where(low, mixed[0], mixed[1])
        bottom = pltpu.roll(jnp.where(low, mixed[1], mixed[0]), HD, 1)
        o_ref[:, lanes] = (top / bottom).astype(bf16)
        rden_ref[:, lanes] = 1.0 / bottom


def spread_projection(omega_ref, wide_ref):
    wide_ref[...] = jnp.zeros_like(wide_ref)
    for pair in range(PAIRS):
        wide_ref[pair, :HD, :FEAT] = omega_ref[2 * pair]
        wide_ref[pair, HD:, FEAT:] = omega_ref[2 * pair + 1]


def ones_projection(omega_ref, wide_ref):
    wide_ref[...] = jnp.ones_like(wide_ref)
    for head in range(HEADS):
        odd = head % 2
        wide_ref[head, odd * HD : (odd + 1) * HD, :] = omega_ref[head]


def attention_forward_local_kernel(
    starts_ref, lens_ref, x_ref, w_ref, gain_ref, omega_ref,
    qkv_ref, fq_ref, fk_ref, o_ref, rden_ref, prefix_ref, state_ref, wide_ref,
):
    tile = pl.program_id(0)

    @pl.when(tile == 0)
    def _():
        spread_projection(omega_ref, wide_ref)

    attention_forward_tile(
        tile, starts_ref, lens_ref, x_ref, lambda: w_ref[...], gain_ref[0:1, :], wide_ref,
        qkv_ref, fq_ref, fk_ref, o_ref, rden_ref, prefix_ref, state_ref,
    )


def attention_forward_kernel(
    starts_ref, lens_ref, x_ref, omega_ref, wq_ref, wo_ref, wu_ref, wd_ref, gains_ref,
    qkv_ref, fq_ref, fk_ref, o_ref, rden_ref, prefix_ref, gain_ref, fullq_ref, fullo_ref, fullu_ref, fulld_ref,
    state_ref, wide_ref, held_ref, so_ref, su_ref, sd_ref, pad_ref, send, recv, local,
):
    tile = pl.program_id(0)
    last = pl.num_programs(0) - 1
    at = place()
    dp, z, core = at["dp"], at["z"], at["core"]
    own = [held_ref.at[dp, z, core], so_ref, su_ref, sd_ref]
    full = [held_ref, fullo_ref, fullu_ref, fulld_ref]

    def copy(w, k):
        return gather_copy(at, own[w], full[w], send.at[w], recv.at[w], k)

    def keep(w):
        if w == 0:
            return pltpu.make_async_copy(held_ref, fullq_ref, local.at[0])
        return pltpu.make_async_copy(own[w], full[w].at[dp, z, core], local.at[w])

    @pl.when(tile == 0)
    def _():
        pad_ref[...] = jnp.zeros_like(pad_ref)
        pad_ref[0:2, 0:16] = gains_ref[...]
        flat = pad_ref[...]
        shift = inner_lane(at)
        turned = flat
        for i in range(1, 8):
            turned = jnp.where(shift == i, pltpu.roll(flat, 16 * i, 1), turned)
        row = lax.broadcasted_iota(jnp.int32, (16, 128), 0)
        band = flat_index(at) // 8
        placed = jnp.where(row == band, turned[0:1, :], 0.0) + jnp.where(
            row == band + 4, turned[1:2, :], 0.0
        )
        held_ref[dp, z, core, :, :WIDE] = wq_ref[...].astype(bf16)
        held_ref[dp, z, core, :, WIDE:] = placed.astype(bf16)
        greet(near_devices(at))
        for k in range(3):
            copy(0, k).start()
        so_ref[...] = wo_ref[...].astype(bf16)
        su_ref[...] = wu_ref[...].astype(bf16)
        sd_ref[...] = wd_ref[...].astype(bf16)
        spread_projection(omega_ref, wide_ref)
        for w in range(1, 4):
            keep(w).start()
        for k in range(3):
            copy(0, k).wait_recv()
        for k in (4, 5, 3):
            copy(0, k).start()
        for w in range(1, 4):
            for k in range(3):
                copy(w, k).start()
        copy(0, 4).wait_recv()
        copy(0, 6).start()
        copy(0, 7).start()
        copy(0, 5).wait_recv()
        copy(0, 8).start()
        copy(0, 6).wait_recv()
        copy(0, 9).start()
        for k in (3, 7, 8, 9):
            copy(0, k).wait_recv()
        keep(0).start()
        packed = held_ref[..., WIDE:].astype(f32)
        total = jnp.sum(packed.reshape(32, 16, 128), axis=0)
        gain_ref[...] = jnp.zeros_like(gain_ref)
        for i in range(2):
            for j in range(4):
                gain_ref[i : i + 1, 128 * j : 128 * (j + 1)] = total[4 * i + j : 4 * i + j + 1, :]

    for w in range(1, 4):

        @pl.when(tile == 1)
        def _(w=w):
            keep(w).wait()
            for k in range(3):
                copy(w, k).wait_recv()
            for k in (4, 5, 3):
                copy(w, k).start()

        @pl.when(tile == 2 + (w > 1))
        def _(w=w):
            copy(w, 4).wait_recv()
            copy(w, 6).start()
            copy(w, 7).start()
            copy(w, 5).wait_recv()
            copy(w, 8).start()

        @pl.when(tile == 5)
        def _(w=w):
            copy(w, 6).wait_recv()
            copy(w, 9).start()

    attention_forward_tile(
        tile, starts_ref, lens_ref, x_ref, lambda: held_ref[..., :WIDE].reshape(D, WIDE), gain_ref[0:1, :], wide_ref,
        qkv_ref, fq_ref, fk_ref, o_ref, rden_ref, prefix_ref, state_ref,
    )

    @pl.when(tile == last)
    def _():
        keep(0).wait()
        for w in range(4):
            if w:
                for k in (3, 7, 8, 9):
                    copy(w, k).wait_recv()
            for k in range(10):
                copy(w, k).wait_send()


def inner_lane(at):
    return flat_index(at) % 8


def flat_index(at):
    return at["dp"] * 8 + at["z"] * 2 + at["core"]


def attention_backward_tile(
    tile, tiles, starts_ref, x_ref, qkv_ref, fq_ref, fk_ref, o_ref, rden_ref, do_ref, dmid_ref,
    prefix_ref, weight, gain, omega_ref, gin_ref, acc_ref, suffix_ref, dqkv_ref, dgain_ref,
):
    per_seg = SEG // TILE

    @pl.when(tile == tiles - 1)
    def _():
        acc_ref[...] = jnp.zeros_like(acc_ref)
        dgain_ref[...] = jnp.zeros_like(dgain_ref)

    @pl.when(tile % per_seg == per_seg - 1)
    def _():
        after = jnp.minimum(tile // per_seg + 1, tiles // per_seg - 1)
        ends = jnp.logical_or(tile == tiles - 1, starts_ref[after] != 0)
        suffix_ref[...] = jnp.where(ends, 0.0, suffix_ref[...])

    lane, low = lane_masks(TILE)
    row_at = lax.broadcasted_iota(jnp.int32, (TILE, TILE), 0)
    col_at = lax.broadcasted_iota(jnp.int32, (TILE, TILE), 1)
    causal = row_at >= col_at
    anti = row_at <= col_at
    state_row = lax.broadcasted_iota(jnp.int32, (2 * HD, FEAT), 0)
    for pair in range(PAIRS):
        lanes = slice(pair * 2 * HD, (pair + 1) * 2 * HD)
        scaled = do_ref[:, lanes] * rden_ref[:, lanes]
        product = scaled * o_ref[:, lanes].astype(f32)
        scaled = scaled.astype(bf16).astype(f32)
        ones = with_ones(qkv_ref[:, 2 * D + pair * 2 * HD : 2 * D + (pair + 1) * 2 * HD], low)
        back_q, back_k, back_v = [], [], []
        for odd in range(2):
            head = 2 * pair + odd
            free = 0 if odd else HD
            mine = jnp.logical_not(low) if odd else low
            grad_den = -jnp.sum(jnp.where(mine, product, 0.0), axis=-1, keepdims=True)
            grad_one = jnp.where(
                mine, scaled, jnp.where(lane == free, grad_den, 0.0)
            ).astype(bf16)
            query_feat = fq_ref[:, head * FEAT : (head + 1) * FEAT]
            key_feat = fk_ref[:, head * FEAT : (head + 1) * FEAT]
            one = ones[odd]
            after = suffix_ref[head]
            edge = after[free : free + 1, :]
            rest = edge - edge.astype(bf16).astype(f32)
            after_low = jnp.where(state_row == free + 1, rest, after).astype(bf16)
            before_low = prefix_ref[0, head]
            weights_t = jnp.where(anti, dot_nt(key_feat, query_feat), 0.0).astype(bf16)
            grad_w = jnp.where(causal, dot_nt(grad_one, one), 0.0).astype(bf16)
            grad_wt = jnp.where(anti, dot_nt(one, grad_one), 0.0).astype(bf16)
            grad_fq = dot_nn(grad_w, key_feat) + dot_nn(grad_one, before_low)
            grad_fk = dot_nn(grad_wt, query_feat) + dot_nn(one, after_low)
            back_v.append(dot_nn(weights_t, grad_one) + dot_nt(key_feat, after_low))
            suffix_ref[head] = after + dot_tn(grad_one, query_feat)
            grad_pq = (grad_fq * query_feat.astype(f32) * feat_scale).astype(bf16)
            grad_pk = (grad_fk * key_feat.astype(f32) * feat_scale).astype(bf16)
            back_q.append(dot_nt(grad_pq, omega_ref[head]))
            back_k.append(dot_nt(grad_pk, omega_ref[head]))
        for part, back in enumerate((back_q, back_k)):
            at = slice(part * D + pair * 2 * HD, part * D + (pair + 1) * 2 * HD)
            top = jnp.where(low, back[0], back[1])
            bottom = pltpu.roll(jnp.where(low, back[1], back[0]), HD, 1)
            dqkv_ref[:, at] = (
                top - bottom * feat_scale * qkv_ref[:, at].astype(f32)
            ).astype(bf16)
        dqkv_ref[:, 2 * D + pair * 2 * HD : 2 * D + (pair + 1) * 2 * HD] = jnp.where(
            low, back_v[0], back_v[1]
        ).astype(bf16)

    unit, inverse = normalise(x_ref[...].astype(f32))
    normed_t = (unit * gain).astype(bf16).T
    acc_ref[...] += dot_nn(normed_t, dqkv_ref[...])
    grad_normed = dot_nt(dqkv_ref[...], weight())
    dgain_ref[0:1, :] += jnp.sum(grad_normed * unit, axis=0, keepdims=True)
    gin_ref[...] = dmid_ref[...] + normalise_back(grad_normed, gain, unit, inverse)


def gain_block(dgain_ref, dgain2_ref):
    first = dgain_ref[0:1, :]
    second = dgain2_ref[0:1, :]
    rows = [first[:, i * 128 : (i + 1) * 128] for i in range(4)]
    rows += [second[:, i * 128 : (i + 1) * 128] for i in range(4)]
    rows += [jnp.zeros((8, 128), f32)]
    return jnp.concatenate(rows, axis=0).astype(bf16)


def attention_backward_local_kernel(
    tiles,
    starts_ref, x_ref, qkv_ref, fq_ref, fk_ref, o_ref, rden_ref, do_ref, dmid_ref,
    prefix_ref, w_ref, gain_ref, omega_ref,
    gin_ref, gw_ref, dgain_ref, acc_ref, suffix_ref, dqkv_ref, wide_ref,
):
    step = pl.program_id(0)

    @pl.when(step == 0)
    def _():
        ones_projection(omega_ref, wide_ref)

    attention_backward_tile(
        tiles - 1 - step, tiles, starts_ref, x_ref, qkv_ref, fq_ref, fk_ref, o_ref, rden_ref, do_ref, dmid_ref,
        prefix_ref, lambda: w_ref[...], gain_ref[0:1, :], wide_ref, gin_ref, acc_ref, suffix_ref, dqkv_ref, dgain_ref,
    )

    @pl.when(step == tiles - 1)
    def _():
        gw_ref[...] = acc_ref[...].astype(bf16)


def scatter_copy(at, grad, part, sums, boxes, send, recv, k):
    z, core = at["z"], at["core"]
    if k == 0:
        src, dst, device = grad.at[:, :, 1 - core], sums, {"fsdp": z * 2 + 1 - core}
    elif k == 1:
        src, dst, device = part.at[at["diag"]], boxes.at[0], {"dp": at["second"]}
    elif k == 2:
        src, dst, device = part.at[at["second"]], boxes.at[1], {"dp": at["second"]}
    elif k == 3:
        src, dst, device = part.at[at["first"]], boxes.at[2], {"dp": at["first"]}
    else:
        there = (z + k - 3) % 4
        src, dst, device = part.at[at["dp"], there], boxes.at[3, k - 4], {"fsdp": there * 2 + core}
    return pltpu.make_async_remote_copy(
        src_ref=src, dst_ref=dst, send_sem=send.at[k], recv_sem=recv.at[k],
        device_id=device, device_id_type=MESH,
    )


def add_low(left, right):
    return (left.astype(f32) + right.astype(f32)).astype(bf16)


def scatter_last(at, part, boxes):
    total = part[at["dp"], at["z"]].astype(f32)
    for i in range(3):
        total = total + boxes[3, i].astype(f32)
    return total


def attention_backward_kernel(
    tiles,
    starts_ref, x_ref, qkv_ref, fq_ref, fk_ref, o_ref, rden_ref, do_ref, dmid_ref,
    prefix_ref, w_ref, gain_ref, omega_ref, dgain2_ref, go_ref, gu_ref, gd_ref,
    gin_ref, gw_ref, ro_ref, ru_ref, rd_ref,
    acc_ref, suffix_ref, dqkv_ref, dgain_ref, wide_ref,
    po_ref, pu_ref, pd_ref, so_ref, su_ref, sd_ref, bo_ref, bu_ref, bd_ref, send, recv, local,
):
    step = pl.program_id(0)
    at = place()
    dp, core = at["dp"], at["core"]
    grads, parts, sums, boxes, results = (
        (go_ref, gu_ref, gd_ref), (po_ref, pu_ref, pd_ref), (so_ref, su_ref, sd_ref),
        (bo_ref, bu_ref, bd_ref), (ro_ref, ru_ref, rd_ref),
    )

    def copy(w, k):
        return scatter_copy(at, grads[w], parts[w], sums[w], boxes[w], send.at[w], recv.at[w], k)

    def keep(w):
        return pltpu.make_async_copy(grads[w].at[:, :, core], parts[w], local.at[w])

    @pl.when(step == 0)
    def _():
        greet(near_devices(at))
        for w in range(3):
            copy(w, 0).start()
            keep(w).start()
        ones_projection(omega_ref, wide_ref)

    @pl.when(step == 1)
    def _():
        for w in range(3):
            keep(w).wait()
            copy(w, 0).wait_recv()
            parts[w][at["diag"]] = add_low(parts[w][at["diag"]], sums[w][at["diag"]])
            copy(w, 1).start()
        for w in range(3):
            for name in ("second", "first", "dp"):
                parts[w][at[name]] = add_low(parts[w][at[name]], sums[w][at[name]])
                if name == "second":
                    copy(w, 2).start()

    @pl.when(step == 3)
    def _():
        for w in range(3):
            copy(w, 1).wait_recv()
            parts[w][at["first"]] = add_low(parts[w][at["first"]], boxes[w][0])
            copy(w, 3).start()

    @pl.when(step == 5)
    def _():
        for w in range(3):
            copy(w, 2).wait_recv()
            copy(w, 3).wait_recv()
            parts[w][dp] = add_low(add_low(parts[w][dp], boxes[w][1]), boxes[w][2])
            for k in (4, 5, 6):
                copy(w, k).start()

    attention_backward_tile(
        tiles - 1 - step, tiles, starts_ref, x_ref, qkv_ref, fq_ref, fk_ref, o_ref, rden_ref, do_ref, dmid_ref,
        prefix_ref, lambda: w_ref[...], gain_ref[0:1, :], wide_ref, gin_ref, acc_ref, suffix_ref, dqkv_ref, dgain_ref,
    )

    @pl.when(step == tiles - 1)
    def _():
        gw_ref[:, :WIDE] = acc_ref[...].astype(bf16)
        stacked = gain_block(dgain_ref, dgain2_ref)
        for i in range(D // 16):
            gw_ref[16 * i : 16 * (i + 1), WIDE:] = stacked
        for w in range(3):
            for k in (4, 5, 6):
                copy(w, k).wait_recv()
            results[w][...] = scatter_last(at, parts[w], boxes[w])
            for k in range(7):
                copy(w, k).wait_send()


def finish_kernel(
    gq_ref, ro_ref, ru_ref, rd_ref,
    rq_ref, norm_ref,
    part_ref, sums_ref, boxes_ref, near_ref, far_ref, send, recv, near_send, near_recv, far_send, far_recv,
):
    at = place()
    dp, z, core = at["dp"], at["z"], at["core"]
    inner = z * 2 + core

    def copy(k):
        return scatter_copy(at, gq_ref, part_ref, sums_ref, boxes_ref, send, recv, k)

    others = [{"fsdp": (z + i // 2) % 4 * 2 + (core + i) % 2} for i in range(1, 8)]
    far = [{"dp": (dp + i) % 4} for i in range(1, 4)]
    greet(others + far)
    copy(0).start()
    row = lax.broadcasted_iota(jnp.int32, (16, EXTRA), 0)
    lane = lax.broadcasted_iota(jnp.int32, (16, EXTRA), 1)
    index = flat_index(at)
    mine = jnp.logical_and(row % 4 == index // 8, lane // 16 == index % 8)
    mine = jnp.logical_and(mine, row < 8)

    def squares(value):
        return jnp.sum((value * value).reshape(-1, 8, value.shape[-1]), axis=0)

    def narrow(value):
        return sum(value[:, 128 * i : 128 * (i + 1)] for i in range(value.shape[1] // 128))

    local = narrow(squares(ro_ref[...])) + narrow(squares(ru_ref[...])) + narrow(squares(rd_ref[...]))
    copy(0).wait_recv()
    for name in ("diag", "second", "first", "dp"):
        part_ref[at[name]] = add_low(gq_ref[at[name], :, core], sums_ref[at[name]])
        if name == "diag":
            copy(1).start()
        if name == "second":
            copy(2).start()
    copy(1).wait_recv()
    part_ref[at["first"]] = add_low(part_ref[at["first"]], boxes_ref[0])
    copy(3).start()
    copy(2).wait_recv()
    part_ref[dp] = add_low(part_ref[dp], boxes_ref[1])
    copy(3).wait_recv()
    part_ref[dp] = add_low(part_ref[dp], boxes_ref[2])
    for k in (4, 5, 6):
        copy(k).start()
    for k in (4, 5, 6):
        copy(k).wait_recv()
    total = scatter_last(at, part_ref, boxes_ref)
    rq_ref[...] = total
    local = local + narrow(squares(total[:, :WIDE])) + squares(jnp.where(mine, total[:, WIDE:], 0.0))
    near_ref[inner] = local

    def near(i):
        return pltpu.make_async_remote_copy(
            src_ref=near_ref.at[inner], dst_ref=near_ref.at[inner], send_sem=near_send.at[i],
            recv_sem=near_recv.at[i], device_id=others[i], device_id_type=MESH,
        )

    def across(i):
        return pltpu.make_async_remote_copy(
            src_ref=far_ref.at[dp], dst_ref=far_ref.at[dp], send_sem=far_send.at[i],
            recv_sem=far_recv.at[i], device_id=far[i], device_id_type=MESH,
        )

    for i in range(7):
        near(i).start()
    for i in range(7):
        near(i).wait_recv()
    group = near_ref[0]
    for i in range(1, 8):
        group = group + near_ref[i]
    far_ref[dp] = group
    for i in range(3):
        across(i).start()
    for i in range(3):
        across(i).wait_recv()
    norm_ref[...] = far_ref[0] + far_ref[1] + far_ref[2] + far_ref[3]
    for i in range(7):
        near(i).wait_send()
    for i in range(3):
        across(i).wait_send()
    for k in range(7):
        copy(k).wait_send()


def update_kernel(
    index_ref, count_ref, rq_ref, ro_ref, ru_ref, rd_ref, total_ref,
    wq_ref, wo_ref, wu_ref, wd_ref, wg_ref, mq_ref, mo_ref, mu_ref, md_ref, mg_ref,
    vq_ref, vo_ref, vu_ref, vd_ref, vg_ref,
    norm_ref, gq_ref, nvq_ref, nwq_ref, go_ref, nvo_ref, nwo_ref, gu_ref, nvu_ref, nwu_ref,
    gd_ref, nvd_ref, nwd_ref, gg_ref, nvg_ref, nwg_ref,
):
    total = jnp.sum(jnp.sum(total_ref[...], axis=0, keepdims=True), axis=1, keepdims=True)
    norm = jnp.sqrt(total)
    norm_ref[...] = norm
    factor = jnp.minimum(1.0, clip_level / norm)
    count = jnp.full((1, 1), count_ref[0], jnp.int32).astype(f32)
    first_fix = 1.0 - jnp.exp2(count * math.log2(beta_first))
    second_fix = 1.0 - jnp.exp2(count * math.log2(beta_second))

    def update(grad, weight, first, second, rate, outs):
        clipped = grad * factor
        first_new = beta_first * first + (1.0 - beta_first) * clipped
        second_new = beta_second * second + (1.0 - beta_second) * clipped * clipped
        direction = first_new / first_fix / (jnp.sqrt(second_new / second_fix) + adam_eps)
        outs[0][...] = clipped
        outs[1][...] = second_new
        outs[2][...] = weight - rate * (direction + decay_weight * weight)

    update(rq_ref[:, :WIDE], wq_ref[...], mq_ref[...], vq_ref[...], rate_matrix, (gq_ref, nvq_ref, nwq_ref))
    update(ro_ref[...], wo_ref[...], mo_ref[...], vo_ref[...], rate_matrix, (go_ref, nvo_ref, nwo_ref))
    update(ru_ref[...], wu_ref[...], mu_ref[...], vu_ref[...], rate_matrix, (gu_ref, nvu_ref, nwu_ref))
    update(rd_ref[...], wd_ref[...], md_ref[...], vd_ref[...], rate_matrix, (gd_ref, nvd_ref, nwd_ref))
    index = index_ref[0]
    packed = rq_ref[:8, WIDE:]
    row = lax.broadcasted_iota(jnp.int32, (8, EXTRA), 0)
    packed = jnp.where(row % 4 == index // 8, packed, 0.0)
    turned = packed
    for i in range(1, 8):
        turned = jnp.where(index % 8 == i, pltpu.roll(packed, EXTRA - 16 * i, 1), turned)
    grad = jnp.concatenate(
        [jnp.sum(turned[:4], axis=0, keepdims=True), jnp.sum(turned[4:], axis=0, keepdims=True)], axis=0
    )[:, :16]
    update(grad, wg_ref[...], mg_ref[...], vg_ref[...], rate_gain, (gg_ref, nvg_ref, nwg_ref))


def feed_forward_kernel(
    block, chunk,
    lens_ref, x_ref, o_ref, cot_ref, wo_ref, wu_ref, wd_ref, gain_ref,
    out_ref, dmid_ref, do_ref, gwo_ref, gwu_ref, gwd_ref, dgain_ref,
    awo_ref, awu_ref, awd_ref, norm_ref, normt_ref, dyt_ref, dy_ref, y_ref, dn_ref,
):
    step = pl.program_id(0)
    steps = pl.num_programs(0)

    @pl.when(step == 0)
    def _():
        awo_ref[...] = jnp.zeros_like(awo_ref)
        awu_ref[...] = jnp.zeros_like(awu_ref)
        awd_ref[...] = jnp.zeros_like(awd_ref)
        dgain_ref[...] = jnp.zeros_like(dgain_ref)

    per_seg = SEG // block
    place = lax.broadcasted_iota(jnp.int32, (block, 1), 0) + (step % per_seg) * block
    valid = (place < lens_ref[step // per_seg]).astype(f32)
    dy = (cot_ref[...].astype(f32) * valid).astype(bf16)
    dy_ref[...] = dy
    dyt_ref[...] = dy.T
    gain = gain_ref[1:2, :]
    attended = o_ref[...]
    middle = x_ref[...].astype(f32) + dot_nn(attended, wo_ref[...])
    unit, inverse = normalise(middle)
    normed = (unit * gain).astype(bf16)
    norm_ref[...] = normed
    normt_ref[...] = normed.T
    y_ref[...] = middle
    dn_ref[...] = jnp.zeros_like(dn_ref)

    @pl.loop(0, FF // chunk)
    def _(index):
        at = pl.ds(pl.multiple_of(index * chunk, chunk), chunk)
        hidden = dot_nn(norm_ref[...], wu_ref[:, at])
        inner = 0.5 + 0.5 * lax.erf(hidden * (0.5**0.5))
        bell = jnp.exp2(hidden * hidden * (-0.5 * log2_e)) * (1.0 / math.sqrt(2.0 * math.pi))
        active = (hidden * inner).astype(bf16)
        slope = inner + hidden * bell
        y_ref[...] += dot_nn(active, wd_ref[at, :])
        grad_hidden = (slope * dot_nt(dy_ref[...], wd_ref[at, :])).astype(bf16)
        awd_ref[:, at] += dot_nn(dyt_ref[...], active)
        awu_ref[:, at] += dot_nn(normt_ref[...], grad_hidden)
        dn_ref[...] += dot_nt(grad_hidden, wu_ref[:, at])

    out_ref[...] = y_ref[...].astype(bf16)
    grad_normed = dn_ref[...]
    dgain_ref[0:1, :] += jnp.sum(grad_normed * unit, axis=0, keepdims=True)
    grad_middle = dy_ref[...].astype(f32) + normalise_back(grad_normed, gain, unit, inverse)
    dmid_ref[...] = grad_middle
    branch = grad_middle.astype(bf16)
    awo_ref[...] += dot_tn(attended, branch)
    do_ref[...] = dot_nt(branch, wo_ref[...])

    @pl.when(step == steps - 1)
    def _():
        gwo_ref[...] = awo_ref[...].astype(bf16)
        gwu_ref[...] = awu_ref[...].astype(bf16)
        gwd_ref[...] = awd_ref[...].astype(bf16).T


def whole(shape):
    return pl.BlockSpec(shape, lambda i: (0,) * len(shape), pipeline_mode=pl.Buffered(1))


def whole_out(shape):
    return pl.BlockSpec(shape, lambda i: (0,) * len(shape))


smem = pl.BlockSpec(memory_space=pltpu.SMEM)


def feed_forward(lens, x, o, cot, wo, wu, wd, gains, block=512, chunk=512):
    tokens = x.shape[0]

    def rows(width):
        return pl.BlockSpec((block, width), lambda i: (i, 0))

    return pl.pallas_call(
        functools.partial(feed_forward_kernel, block, chunk),
        grid=(tokens // block,),
        in_specs=[smem, rows(D), rows(D), rows(D), whole((D, D)), whole((D, FF)), whole((FF, D)), whole((8, D))],
        out_specs=[rows(D), rows(D), rows(D), whole_out((D, D)), whole_out((D, FF)), whole_out((FF, D)), whole_out((8, D))],
        out_shape=[
            jax.ShapeDtypeStruct((tokens, D), bf16),
            jax.ShapeDtypeStruct((tokens, D), f32),
            jax.ShapeDtypeStruct((tokens, D), f32),
            jax.ShapeDtypeStruct((D, D), bf16),
            jax.ShapeDtypeStruct((D, FF), bf16),
            jax.ShapeDtypeStruct((FF, D), bf16),
            jax.ShapeDtypeStruct((8, D), f32),
        ],
        scratch_shapes=[
            pltpu.VMEM((D, D), f32), pltpu.VMEM((D, FF), f32), pltpu.VMEM((D, FF), f32),
            pltpu.VMEM((block, D), bf16), pltpu.VMEM((D, block), bf16), pltpu.VMEM((D, block), bf16),
            pltpu.VMEM((block, D), bf16), pltpu.VMEM((block, D), f32), pltpu.VMEM((block, D), f32),
        ],
        compiler_params=pltpu.CompilerParams(vmem_limit_bytes=60 << 20),
    )(lens, x, o, cot, wo, wu, wd, gains)


def tile_rows(width, tiles=None):
    if tiles is None:
        return pl.BlockSpec((TILE, width), lambda i: (i, 0))
    return pl.BlockSpec((TILE, width), lambda i: (tiles - 1 - i, 0))


hbm = pl.BlockSpec(memory_space=pl.ANY)
vmem = pl.BlockSpec(memory_space=pltpu.VMEM)


def five(name, dtype=bf16):
    return (4, 4, 2, ROWS[name], COLS[name])


def forward_outs(tokens):
    tiles = tokens // TILE
    specs = [tile_rows(WIDE), tile_rows(HEADS * FEAT), tile_rows(HEADS * FEAT), tile_rows(D), tile_rows(D),
             pl.BlockSpec((1, HEADS, 2 * HD, FEAT), lambda i: (i, 0, 0, 0))]
    shapes = [
        jax.ShapeDtypeStruct((tokens, WIDE), bf16),
        jax.ShapeDtypeStruct((tokens, HEADS * FEAT), bf16),
        jax.ShapeDtypeStruct((tokens, HEADS * FEAT), bf16),
        jax.ShapeDtypeStruct((tokens, D), bf16),
        jax.ShapeDtypeStruct((tokens, D), f32),
        jax.ShapeDtypeStruct((tiles, HEADS, 2 * HD, FEAT), bf16),
    ]
    scratch = [pltpu.VMEM((HEADS, 2 * HD, FEAT), f32), pltpu.VMEM((PAIRS, 2 * HD, 2 * FEAT), bf16)]
    return specs, shapes, scratch


def attention_forward_local(starts, lens, x, w_qkv, gains, omega):
    tokens = x.shape[0]
    specs, shapes, scratch = forward_outs(tokens)
    return pl.pallas_call(
        attention_forward_local_kernel,
        grid=(tokens // TILE,),
        in_specs=[smem, smem, tile_rows(D), whole((D, WIDE)), whole((8, D)), whole((HEADS, HD, FEAT))],
        out_specs=specs,
        out_shape=shapes,
        scratch_shapes=scratch,
        compiler_params=pltpu.CompilerParams(vmem_limit_bytes=48 << 20),
    )(starts, lens, x, w_qkv, gains, omega)


def attention_forward(starts, lens, x, omega, wq, wo, wu, wd, gains):
    tokens = x.shape[0]
    specs, shapes, scratch = forward_outs(tokens)
    return pl.pallas_call(
        attention_forward_kernel,
        grid=(tokens // TILE,),
        in_specs=[smem, smem, tile_rows(D), whole((HEADS, HD, FEAT)), whole(wq.shape), whole(wo.shape), whole(wu.shape),
                  whole(wd.shape), whole(gains.shape)],
        out_specs=specs + [whole_out((8, D)), hbm, hbm, hbm, hbm],
        out_shape=shapes + [jax.ShapeDtypeStruct((8, D), f32)]
        + [jax.ShapeDtypeStruct(five(name), bf16) for name in ("qkv",) + LATE],
        scratch_shapes=scratch + [pltpu.VMEM(five("qkv"), bf16)]
        + [pltpu.VMEM((ROWS[name], COLS[name]), bf16) for name in LATE]
        + [pltpu.VMEM((8, 128), f32), pltpu.SemaphoreType.DMA((4, 10)), pltpu.SemaphoreType.DMA((4, 10)),
           pltpu.SemaphoreType.DMA((4,))],
        compiler_params=pltpu.CompilerParams(vmem_limit_bytes=48 << 20, collective_id=0, has_side_effects=True),
    )(starts, lens, x, omega, wq, wo, wu, wd, gains)


def backward_specs(tokens):
    tiles = tokens // TILE
    rows = functools.partial(tile_rows, tiles=tiles)
    ins = [smem, rows(D), rows(WIDE), rows(HEADS * FEAT), rows(HEADS * FEAT), rows(D), rows(D), rows(D), rows(D),
           pl.BlockSpec((1, HEADS, 2 * HD, FEAT), lambda i: (tiles - 1 - i, 0, 0, 0)),
           whole((D, WIDE)), whole((8, D)), whole((HEADS, HD, FEAT))]
    scratch = [pltpu.VMEM((D, WIDE), f32), pltpu.VMEM((HEADS, 2 * HD, FEAT), f32), pltpu.VMEM((TILE, WIDE), bf16)]
    wide = pltpu.VMEM((HEADS, 2 * HD, FEAT), bf16)
    return tiles, rows(D), ins, scratch, wide


def attention_backward_local(args):
    tokens = args[1].shape[0]
    tiles, rows, ins, scratch, wide = backward_specs(tokens)
    return pl.pallas_call(
        functools.partial(attention_backward_local_kernel, tiles),
        grid=(tiles,),
        in_specs=ins,
        out_specs=[rows, whole_out((D, WIDE)), whole_out((8, D))],
        out_shape=[
            jax.ShapeDtypeStruct((tokens, D), f32),
            jax.ShapeDtypeStruct((D, WIDE), bf16),
            jax.ShapeDtypeStruct((8, D), f32),
        ],
        scratch_shapes=scratch + [wide],
        compiler_params=pltpu.CompilerParams(vmem_limit_bytes=56 << 20),
    )(*args)


def attention_backward(args, dgain2, grads):
    tokens = args[1].shape[0]
    tiles, rows, ins, scratch, wide = backward_specs(tokens)
    half = [(4, 4, ROWS[name], COLS[name]) for name in LATE]
    grads = [grad.reshape(five(name)) for grad, name in zip(grads, LATE)]
    return pl.pallas_call(
        functools.partial(attention_backward_kernel, tiles),
        grid=(tiles,),
        in_specs=ins + [whole((8, D)), hbm, hbm, hbm],
        out_specs=[rows, whole_out((D, FULL))] + [whole_out((ROWS[name], COLS[name])) for name in LATE],
        out_shape=[
            jax.ShapeDtypeStruct((tokens, D), f32),
            jax.ShapeDtypeStruct((D, FULL), bf16),
        ]
        + [jax.ShapeDtypeStruct((ROWS[name], COLS[name]), f32) for name in LATE],
        scratch_shapes=scratch
        + [pltpu.VMEM((8, D), f32), wide]
        + [pltpu.VMEM(shape, bf16) for shape in half]
        + [pltpu.VMEM(shape, bf16) for shape in half]
        + [pltpu.VMEM(shape, bf16) for shape in half]
        + [pltpu.SemaphoreType.DMA((3, 7)), pltpu.SemaphoreType.DMA((3, 7)), pltpu.SemaphoreType.DMA((3,))],
        compiler_params=pltpu.CompilerParams(vmem_limit_bytes=60 << 20, collective_id=1, has_side_effects=True),
    )(*args, dgain2, *grads)


def finish(grad_wide, reduced):
    grad_wide = grad_wide.reshape(five("qkv"))
    half = (4, 4, 16, FULL)
    return pl.pallas_call(
        finish_kernel,
        in_specs=[vmem] * 4,
        out_specs=[vmem] * 2,
        out_shape=[jax.ShapeDtypeStruct((16, FULL), f32), jax.ShapeDtypeStruct((8, 128), f32)],
        scratch_shapes=[pltpu.VMEM(half, bf16)] * 3
        + [pltpu.VMEM((8, 8, 128), f32), pltpu.VMEM((4, 8, 128), f32)]
        + [pltpu.SemaphoreType.DMA((7,))] * 4
        + [pltpu.SemaphoreType.DMA((3,))] * 2,
        compiler_params=pltpu.CompilerParams(vmem_limit_bytes=48 << 20, collective_id=2, has_side_effects=True),
    )(grad_wide, *reduced)


def update_all(index, count, grads, total, weights, firsts, seconds):
    shapes = [jax.ShapeDtypeStruct((1, 1), f32)]
    for weight in weights:
        shapes += [jax.ShapeDtypeStruct(weight.shape, f32)] * 3
    return pl.pallas_call(
        update_kernel,
        in_specs=[smem, smem] + [vmem] * 20,
        out_specs=[vmem] * 16,
        out_shape=shapes,
    )(index.reshape(1), count.reshape(1), *grads, total, *weights, *firsts, *seconds)


def on_device(
    sizes, inputs, cotangent, feature_omega, seg_start, seg_len, step_count,
    w_qkv, w_out, w_up, w_down, gains,
    m_qkv, m_out, m_up, m_down, m_gains,
    v_qkv, v_out, v_up, v_down, v_gains,
):
    weights = (w_qkv, w_out, w_up, w_down, gains)
    firsts = (m_qkv, m_out, m_up, m_down, m_gains)
    seconds = (v_qkv, v_out, v_up, v_down, v_gains)
    if sizes == (4, 8):
        (qkv, fq, fk, attended, rden, prefix, gain_full, qkv_full, out_full, up_full, down_full) = attention_forward(
            seg_start, seg_len, inputs, feature_omega, *weights
        )
        qkv_full = qkv_full.reshape(D, FULL)
        out_rows, dmid, grad_attended, grad_out, grad_up, grad_down, dgain2 = feed_forward(
            seg_len, inputs, attended, cotangent, out_full.reshape(D, D), up_full.reshape(D, FF),
            down_full.reshape(FF, D), gain_full,
        )
        grad_inputs, grad_wide, *late = attention_backward(
            (seg_start, inputs, qkv, fq, fk, attended, rden, grad_attended, dmid, prefix, qkv_full, gain_full,
             feature_omega),
            dgain2, (grad_out, grad_up, grad_down),
        )
        reduced, total = finish(grad_wide, late)
        index = lax.axis_index("dp") * 8 + lax.axis_index("fsdp")
        norm, *updated = update_all(index, step_count, (reduced, *late), total, weights, firsts, seconds)
        return (out_rows, grad_inputs, norm.reshape(()), *updated)

    def gather(piece, axis=0):
        return lax.all_gather(piece.astype(bf16), AXES, axis=axis, tiled=True)

    qkv_full, out_full, up_full, down_full = (gather(piece) for piece in weights[:4])
    gain_full = jnp.pad(gather(gains, 1).astype(f32), ((0, 6), (0, 0)))
    qkv, fq, fk, attended, rden, prefix = attention_forward_local(
        seg_start, seg_len, inputs, qkv_full, gain_full, feature_omega
    )
    out_rows, dmid, grad_attended, grad_out, grad_up, grad_down, dgain2 = feed_forward(
        seg_len, inputs, attended, cotangent, out_full, up_full, down_full, gain_full
    )
    grad_inputs, grad_qkv, dgain = attention_backward_local(
        (seg_start, inputs, qkv, fq, fk, attended, rden, grad_attended, dmid, prefix, qkv_full, gain_full,
         feature_omega)
    )

    def scatter(piece, axis=0):
        return lax.psum_scatter(piece.astype(f32), AXES, scatter_dimension=axis, tiled=True)

    reduced = [scatter(piece) for piece in (grad_qkv, grad_out, grad_up, grad_down)]
    reduced.append(scatter(jnp.concatenate([dgain[:1], dgain2[:1]], axis=0), 1))
    grad_norm = jnp.sqrt(lax.psum(sum(jnp.sum(piece * piece) for piece in reduced), AXES))
    factor = jnp.minimum(1.0, clip_level / grad_norm)
    count = step_count.astype(f32)
    first_fix = 1.0 - jnp.power(beta_first, count)
    second_fix = 1.0 - jnp.power(beta_second, count)
    updated = []
    rates = (rate_matrix,) * 4 + (rate_gain,)
    for weight, first, second, gradient, rate in zip(weights, firsts, seconds, reduced, rates):
        clipped = gradient * factor
        first_new = beta_first * first + (1.0 - beta_first) * clipped
        second_new = beta_second * second + (1.0 - beta_second) * clipped * clipped
        direction = first_new / first_fix / (jnp.sqrt(second_new / second_fix) + adam_eps)
        updated += [clipped, second_new, weight - rate * (direction + decay_weight * weight)]
    return (out_rows, grad_inputs, grad_norm, *updated)


def solution(mesh):
    return jax.shard_map(
        functools.partial(on_device, tuple(mesh.shape[name] for name in AXES)),
        mesh=mesh,
        in_specs=(
            P(("dp", "fsdp"), None),
            P(("dp", "fsdp"), None),
            P(),
            P(("dp", "fsdp")),
            P(("dp", "fsdp")),
            P(),
            P(("dp", "fsdp"), None),
            P(("dp", "fsdp"), None),
            P(("dp", "fsdp"), None),
            P(("dp", "fsdp"), None),
            P(None, ("dp", "fsdp")),
            P(("dp", "fsdp"), None),
            P(("dp", "fsdp"), None),
            P(("dp", "fsdp"), None),
            P(("dp", "fsdp"), None),
            P(None, ("dp", "fsdp")),
            P(("dp", "fsdp"), None),
            P(("dp", "fsdp"), None),
            P(("dp", "fsdp"), None),
            P(("dp", "fsdp"), None),
            P(None, ("dp", "fsdp")),
        ),
        out_specs=(
            P(("dp", "fsdp"), None),
            P(("dp", "fsdp"), None),
            P(),
            P(("dp", "fsdp"), None),
            P(("dp", "fsdp"), None),
            P(("dp", "fsdp"), None),
            P(("dp", "fsdp"), None),
            P(("dp", "fsdp"), None),
            P(("dp", "fsdp"), None),
            P(("dp", "fsdp"), None),
            P(("dp", "fsdp"), None),
            P(("dp", "fsdp"), None),
            P(("dp", "fsdp"), None),
            P(("dp", "fsdp"), None),
            P(("dp", "fsdp"), None),
            P(None, ("dp", "fsdp")),
            P(None, ("dp", "fsdp")),
            P(None, ("dp", "fsdp")),
        ),
        check_vma=False,
    )
```

time: 1150 us -> 212 us (0.18); the launches traced: 1140 us -> 212 us
  waiting for transfers between devices: 587 us -> 0 us
  matrix products: 285 us -> 0 us
  Pallas kernels: 0 us -> 190 us
  blocking collectives: 119 us -> 0 us
  other arithmetic: 65.6 us -> 0 us
  local copies, waits for them, and re-layouts: 58.5 us -> 20.2 us
  between operations: 21.3 us -> 1.39 us
    reduce_scatter x4 -> x0, waiting for transfers between devices: 514 us -> none  [the longest x1 141 us: on_device(): lax.psum_scatter(grad_up, ('dp', 'fsdp'), scatter_dimension=0, tiled=True)]
    dot_general x34 -> x0, matrix products: 285 us -> none  [the longest x1 46.2 us: on_device(): hidden = jnp.dot(normed_two, up_full, preferred_element_type=jnp.float32)]
    pallas_call x0 -> x5, Pallas kernels: none -> 190 us  [the longest x1 63.5 us: attention_forward(): pl.pallas_call(attention_forward_kernel, grid=(tokens // TILE,), in_specs...]
    all_gather x2 -> x0, blocking collectives: 82.4 us -> none  [the longest x1 43 us: fetch(): lax.all_gather(shards[4], ('dp', 'fsdp'), axis=1, tiled=True)]
    unnamed x9 -> x0, waiting for transfers between devices: 73.5 us -> none
    reduce_sum x14 -> x0, other arithmetic: 43.3 us -> none  [the longest x2 28.5 us: feature_back(): jnp.sum(weighted, axis=-1, keepdims=True)]
    psum x1 -> x0, blocking collectives: 36.8 us -> none  [on_device(): grad_norm = jnp.sqrt(lax.psum(local_squares, ('dp', 'fsdp')))]
    add x3 -> x0, local copies, waits for them, and re-layouts: 18.1 us -> none  [the longest x1 6.82 us: attention_backward(): jnp.einsum('cihd,chmd->cihm', grad_num, prefix_state, preferred_element_t...]
  transfers between devices with their start and end apart: 8 -> 0, of which waited for: 5 -> 0; matrix products, arithmetic and copies ran while one was open for 17% -> 0% of each run, Pallas kernels for 0% -> 0%
where the time goes in v1:
time: 212 us
  Pallas kernels  190 us (90%)
  local copies, waits for them, and re-layouts  20.2 us (10%)
    pallas_call x1, Pallas kernels, attention_forward(): pl.pallas_call(attention_forward_kernel, grid=(tokens // TILE,), in_specs...  63.5 us
    pallas_call x1, Pallas kernels, attention_backward(): pl.pallas_call(functools.partial(attention_backward_kernel, tiles), grid=...  50.8 us
    pallas_call x1, Pallas kernels, feed_forward(): pl.pallas_call(functools.partial(feed_forward_kernel, block, chunk), grid...  45.4 us
    pallas_call x1, Pallas kernels, finish(): pl.pallas_call(finish_kernel, in_specs=[vmem] * 4, out_specs=[vmem] * 2,...  27.6 us
    unnamed x37, local copies, waits for them, and re-layouts  20.2 us

profile of v1, /device:TPU:0, one launch (start us, length us, event | category | flops | bytes accessed | tf_op | source)
XLA Modules:
  0.0 211.6 jit_solution(17229045133937657543)
XLA Ops:
  0.7 0.0 copy-start.3
  0.7 0.9 copy-done.3
  1.6 0.0 copy-start.5
  1.6 0.9 copy-done.5
  2.5 0.0 copy-start.6
  2.5 0.9 copy-done.6
  3.4 0.0 copy-start.9
  3.4 0.9 copy-done.9
  4.3 0.0 copy-start.10
  4.3 0.8 copy-done.10
  5.1 0.0 copy-start.15
  5.1 0.7 copy-done.15
  5.7 0.0 copy-start.16
  5.8 0.7 copy-done.16
  6.4 0.0 copy-start.17
  6.4 0.7 copy-done.17
  7.1 63.5 %shard_map.340 = (bf16[2048,1536]{1,0:T(8,128)(2,1)}, bf16[2048,2048]{1,0:T(8,128)(2,1)}, bf16[2048,2048]{1,0:T(8,128)(2,1)}, bf16[2048,512]{1,0:T(8,128)(2,1)S(...) custom-call(s32[2]{0:T(128)S(1)} %copy-done.17, ...), custom_call_target="tpu_custom_call" | custom-call | tf_op jit(solution)/shard_map/pallas_call | solution.py:828
  70.5 0.0 copy-start
  70.6 1.3 copy-done
  71.9 0.0 copy-start.2
  71.9 1.2 copy-done.2
  73.1 0.0 copy-start.4
  73.1 0.8 copy-done.4
  73.9 0.0 copy-start.13
  73.9 0.6 copy-done.13
  74.5 45.4 %shard_map.341 = (bf16[2048,512]{1,0:T(8,128)(2,1)}, f32[2048,512]{1,0:T(8,128)}, f32[2048,512]{1,0:T(8,128)}, bf16[512,512]{1,0:T(8,128)(2,1)}, bf16[512,2048]{...) custom-call(s32[2]{0:T(128)} %lens_ref.3, bf16[2048,512]{1,0:T(8,128)(2,1)} %x_ref.5, ...), custom_call_target="tpu_custom_call" | custom-call | tf_op jit(solution)/shard_map/pallas_call | solution.py:758
  120.0 50.8 %shard_map.342 = (f32[2048,512]{1,0:T(8,128)}, bf16[512,1664]{1,0:T(8,128)(2,1)}, f32[16,512]{1,0:T(8,128)}, f32[16,2048]{1,0:T(8,128)}, f32[64,512]{1,0:T(8,128)}) custom-call(s32[2]{0:T(128)} %starts_ref.3, bf16[2048,512]{1,0:T(8,128)(2,1)} %x_ref.5, bf16[2048,1536]{1,0:T(8,128)(2,1)} %get-tuple-element.65.qkv_ref, ...), custom_call_target="tpu_custom_call" | custom-call | tf_op jit(solution)/shard_map/pallas_call | solution.py:878
  171.5 0.0 copy-start.1
  171.5 1.4 copy-done.1
  172.9 0.0 copy-start.7
  172.9 0.9 copy-done.7
  173.8 0.0 copy-start.8
  173.8 0.9 copy-done.8
  174.7 0.0 copy-start.11
  174.7 0.8 copy-done.11
  175.5 27.6 %shard_map.343 = (f32[16,1664]{1,0:T(8,128)S(1)}, f32[8,128]{1,0:T(8,128)S(1)}) custom-call(bf16[4,4,2,16,1664]{4,3,2,1,0:T(8,128)(2,1)S(1)} %bitcast.12, f32[16,512]{1,0:T(8,128)S(1)} %copy-done.11, f32[16,2048]{1,0:T(8,128)S(1)} %copy-done.7, f32[64,512]{1,0:T(8,128)S(1)} %copy-done.8), custom_call_target="tpu_custom_call" | custom-call | tf_op jit(solution)/shard_map/pallas_call | solution.py:901
  203.1 0.0 copy-start.12
  203.1 0.6 copy-done.12
  203.7 0.0 copy-start.14
  203.7 0.6 copy-done.14
  204.3 2.7 %shard_map.344 = (f32[1,1]{1,0:T(1,128)}, f32[16,1536]{1,0:T(8,128)}, f32[16,1536]{1,0:T(8,128)}, f32[16,1536]{1,0:T(8,128)}, f32[16,512]{1,0:T(8,128)}, /*index...) custom-call(s32[1]{0:T(128)} %bitcast.7.index_ref, ...), custom_call_target="tpu_custom_call" | custom-call | tf_op jit(solution)/shard_map/pallas_call | solution.py:918
  207.0 4.6 %copy.41 = f32[2048,512]{1,0:T(8,128)} copy(f32[2048,512]{1,0:T(8,128)} %get-tuple-element.119) | data formatting | bytes 8388608
Async XLA Ops:
  0.7 1.0 copy-start.3
  1.6 0.9 copy-start.5
  2.5 0.9 copy-start.6
  3.4 0.9 copy-start.9
  4.3 0.8 copy-start.10
  5.1 0.7 copy-start.15
  5.7 0.7 copy-start.16
  6.4 0.7 copy-start.17
  70.5 1.4 copy-start
  71.9 1.2 copy-start.2
  73.1 0.8 copy-start.4
  73.9 0.6 copy-start.13
  171.5 1.5 copy-start.1
  172.9 0.9 copy-start.7
  173.8 0.9 copy-start.8
  174.7 0.8 copy-start.11
  203.1 0.6 copy-start.12
  203.7 0.6 copy-start.14

commit v2 on v0

v2 whole, which is shorter than its diff:
```python
import functools
import math

import jax
import jax.numpy as jnp
from jax import lax
from jax.experimental import pallas as pl
from jax.experimental.pallas import tpu as pltpu
from jax.sharding import PartitionSpec as P

D = 512
HEADS = 8
HD = 64
FEAT = 256
FF = 2048
SEG = 1024
TILE = 256
PAIRS = HEADS // 2
DUO = 2 * HD
BLOCK = 1024
TILES_BLOCK = BLOCK // TILE
UPDATE_ROWS = 512
WIDE = 3 * D
CHUNK = 3 * DUO
EXTRA = 128
AXES = ("dp", "fsdp")

norm_eps = 1e-05
clip_level = 1.0
rate_matrix = 0.03
rate_gain = 0.4
beta_first = 0.9
beta_second = 0.95
adam_eps = 1e-08
decay_weight = 0.1

feat_scale = HD ** (-0.25)
log2_e = math.log2(math.e)
f32 = jnp.float32
bf16 = jnp.bfloat16
MESH = pl.DeviceIdType.MESH
VMEM_LIMIT = 63 << 20


def dot_nn(a, b):
    return lax.dot_general(a, b, (((1,), (0,)), ((), ())), preferred_element_type=f32)


def dot_nt(a, b):
    return lax.dot_general(a, b, (((1,), (1,)), ((), ())), preferred_element_type=f32)


def dot_tn(a, b):
    return lax.dot_general(a, b, (((0,), (0,)), ((), ())), preferred_element_type=f32)


def normalise(rows):
    centred = rows - jnp.mean(rows, axis=-1, keepdims=True)
    spread = jnp.mean(centred * centred, axis=-1, keepdims=True)
    inverse = lax.rsqrt(spread + norm_eps)
    return centred * inverse, inverse


def normalise_back(grad, gain, unit, inverse):
    scaled = grad * gain
    first = jnp.mean(scaled, axis=-1, keepdims=True)
    second = jnp.mean(scaled * unit, axis=-1, keepdims=True)
    return inverse * (scaled - first - unit * second)


def lane_masks(rows):
    lane = lax.broadcasted_iota(jnp.int32, (rows, DUO), 1)
    return lane, lane < HD


def causal_masks():
    row = lax.broadcasted_iota(jnp.int32, (TILE, TILE), 0)
    col = lax.broadcasted_iota(jnp.int32, (TILE, TILE), 1)
    return row >= col, row <= col


def with_ones(value_pair, low):
    wide = value_pair.astype(f32)
    return (
        jnp.where(low, wide, 1.0).astype(bf16),
        jnp.where(low, 1.0, wide).astype(bf16),
    )


def place():
    dp, inner = lax.axis_index("dp"), lax.axis_index("fsdp")
    z, core = inner // 2, inner % 2
    y, x = dp // 2, dp % 2
    across = y * 2 + (1 - x)
    along = (1 - y) * 2 + x
    return {
        "dp": dp, "z": z, "core": core, "flat": dp * 8 + inner,
        "first": core * along + (1 - core) * across,
        "second": core * across + (1 - core) * along,
        "diag": (1 - y) * 2 + (1 - x),
    }


def greet(devices):
    barrier = pltpu.get_barrier_semaphore()
    for device in devices:
        pl.semaphore_signal(barrier, inc=1, device_id=device, device_id_type=MESH)


def greeted(devices):
    pl.semaphore_wait(pltpu.get_barrier_semaphore(), len(devices))


def near_devices(at):
    devices = [{"fsdp": (at["z"] + i) % 4 * 2 + at["core"]} for i in range(1, 4)]
    devices += [{"fsdp": at["z"] * 2 + 1 - at["core"]}]
    devices += [{"dp": at["first"]}, {"dp": at["second"]}]
    return devices


def halves(up, down):
    return [up.at[..., i * (FF // 2) : (i + 1) * (FF // 2)] for i in range(2)] + [
        down.at[:, :, :, i * 32 : (i + 1) * 32, :] for i in range(2)
    ]


def gather_copy(at, own, full, send, recv, k):
    dp, z, core = at["dp"], at["z"], at["core"]
    sibling = {"fsdp": z * 2 + 1 - core}
    if k < 3:
        src, dst, device = own, full.at[dp, z, core], {"fsdp": (z + 1 + k) % 4 * 2 + core}
    else:
        which = {3: "dp", 4: "dp", 5: "dp", 6: "first", 7: "first", 8: "second", 9: "diag"}[k]
        src = dst = full.at[at[which], :, core]
        device = {4: {"dp": at["first"]}, 5: {"dp": at["second"]}, 6: {"dp": at["second"]}}.get(k, sibling)
    return pltpu.make_async_remote_copy(
        src_ref=src, dst_ref=dst, send_sem=send.at[k], recv_sem=recv.at[k],
        device_id=device, device_id_type=MESH,
    )


def gather_stage(copy, stage):
    if stage == 0:
        for k in range(3):
            copy(k).start()
    elif stage == 1:
        for k in range(3):
            copy(k).wait_recv()
        for k in (4, 5, 3):
            copy(k).start()
    elif stage == 2:
        copy(4).wait_recv()
        copy(6).start()
        copy(7).start()
        copy(5).wait_recv()
        copy(8).start()
    elif stage == 3:
        copy(6).wait_recv()
        copy(9).start()
    else:
        for k in (3, 7, 8, 9):
            copy(k).wait_recv()


GATHER_PLAN = {
    0: [(0, 0), (1, 0), (2, 0), (3, 0), (0, 1), (4, 0), (5, 0), (6, 0), (7, 0), (8, 0),
        (0, 2), (1, 1), (2, 1), (3, 1), (0, 3), (0, 4), (1, 2), (4, 1), (5, 1)],
    1: [(1, 3), (2, 2), (3, 2), (6, 1)],
    2: [(1, 4), (4, 2), (5, 2), (7, 1), (2, 3), (3, 3)],
    3: [(6, 2), (8, 1), (4, 3)],
    4: [(2, 4), (5, 3)],
    5: [(7, 2), (6, 3)],
    6: [(3, 4), (8, 2), (4, 4), (5, 4)],
    7: [(7, 3), (8, 3), (6, 4)],
    8: [(7, 4), (8, 4)],
}


def scatter_copy(at, grad, part, sums, boxes, send, recv, k):
    z, core = at["z"], at["core"]
    if k == 0:
        src, dst, device = grad.at[:, :, 1 - core], sums, {"fsdp": z * 2 + 1 - core}
    elif k == 1:
        src, dst, device = part.at[at["diag"]], boxes.at[0], {"dp": at["second"]}
    elif k == 2:
        src, dst, device = part.at[at["second"]], boxes.at[1], {"dp": at["second"]}
    elif k == 3:
        src, dst, device = part.at[at["first"]], boxes.at[2], {"dp": at["first"]}
    else:
        there = (z + k - 3) % 4
        src, dst, device = part.at[at["dp"], there], boxes.at[3, k - 4], {"fsdp": there * 2 + core}
    return pltpu.make_async_remote_copy(
        src_ref=src, dst_ref=dst, send_sem=send.at[k], recv_sem=recv.at[k],
        device_id=device, device_id_type=MESH,
    )


def direct_copy(at, part, boxes, send, recv, i):
    dp, z = (at["dp"] + i // 4) % 4, (at["z"] + i % 4) % 4
    return pltpu.make_async_remote_copy(
        src_ref=part.at[dp, z], dst_ref=boxes.at[i - 1], send_sem=send.at[i - 1], recv_sem=recv.at[i - 1],
        device_id={"dp": dp, "fsdp": z * 2 + at["core"]}, device_id_type=MESH,
    )


def all_devices(at):
    inner = at["z"] * 2 + at["core"]
    return [{"dp": (at["dp"] + i // 8) % 4, "fsdp": (inner + i % 8) % 8} for i in range(1, 32)]


def add_low(left, right):
    return left + right


def scatter_stage(at, copy, mine, part, sums, boxes, stage):
    dp = at["dp"]
    if stage == 0:
        copy(0).start()
    elif stage == 1:
        copy(0).wait_recv()
        for name in ("diag", "second", "first", "dp"):
            part[at[name]] = add_low(mine(at[name]), sums[at[name]])
            if name == "diag":
                copy(1).start()
            if name == "second":
                copy(2).start()
    elif stage == 2:
        copy(1).wait_recv()
        part[at["first"]] = add_low(part[at["first"]], boxes[0])
        copy(3).start()
    elif stage == 3:
        copy(2).wait_recv()
        part[dp] = add_low(part[dp], boxes[1])
        copy(3).wait_recv()
        part[dp] = add_low(part[dp], boxes[2])
        for k in (4, 5, 6):
            copy(k).start()
    else:
        for k in (4, 5, 6):
            copy(k).wait_recv()


def scatter_total(at, part, boxes):
    total = part[at["dp"], at["z"]].astype(f32)
    for i in range(3):
        total = total + boxes[3, i].astype(f32)
    return total


SCATTER_PLAN = {
    1: [(0, 0), (1, 0), (2, 0), (3, 0), (4, 0)],
    2: [(0, 1), (1, 1), (2, 1)],
    3: [(5, 1), (3, 1), (0, 2)],
    4: [(1, 2), (2, 2), (4, 1)],
    5: [(5, 2), (6, 1), (3, 2), (0, 3)],
    6: [(4, 2), (7, 1), (1, 3), (2, 3)],
    7: [(6, 2), (5, 3), (3, 3), (7, 2), (0, 4)],
}


def spread_projection(omega_ref, wide_ref):
    wide_ref[...] = jnp.zeros_like(wide_ref)
    wide_ref[:HD, :FEAT] = omega_ref[0]
    wide_ref[HD:, FEAT:] = omega_ref[1]


def ones_projection(omega_ref, wide_ref):
    wide_ref[...] = jnp.ones_like(wide_ref)
    for odd in range(2):
        wide_ref[odd, odd * HD : (odd + 1) * HD, :] = omega_ref[odd]


def forward_step(
    block, starts_ref, lens_ref, normed, weight, wide_ref,
    qkv_ref, fq_ref, fk_ref, o_ref, rden_ref, prefix_ref, state_ref,
):
    per_seg = SEG // BLOCK

    @pl.when(block % per_seg == 0)
    def _():
        begins = jnp.logical_or(block == 0, starts_ref[block // per_seg] != 0)
        state_ref[...] = jnp.where(begins, 0.0, state_ref[...])

    qkv_ref[0] = dot_nn(normed, weight).astype(bf16)
    position = lax.broadcasted_iota(jnp.int32, (BLOCK, 1), 0) + (block % per_seg) * BLOCK
    valid = (position < lens_ref[block // per_seg]).astype(f32)
    _, low = lane_masks(BLOCK)
    feats = []
    for part, feat_ref in enumerate((fq_ref, fk_ref)):
        rows = qkv_ref[0, :, part * DUO : (part + 1) * DUO]
        wide = rows.astype(f32)
        square = wide * wide
        proj = dot_nn(rows, wide_ref[...])
        for odd in range(2):
            total = jnp.sum(
                jnp.where(low, 0.0, square) if odd else jnp.where(low, square, 0.0), axis=-1, keepdims=True
            )
            value = jnp.exp2(
                proj[:, odd * FEAT : (odd + 1) * FEAT] * (feat_scale * log2_e)
                - total * (0.5 * feat_scale * feat_scale * log2_e)
            )
            if part:
                value = value * valid
            value = value.astype(bf16)
            feat_ref[0, :, odd * FEAT : (odd + 1) * FEAT] = value
            feats.append(value)
    _, low = lane_masks(TILE)
    causal, _ = causal_masks()
    cuts = [slice(tile * TILE, (tile + 1) * TILE) for tile in range(TILES_BLOCK)]
    values = qkv_ref[0, :, 2 * DUO :]
    ones = [with_ones(values[at], low) for at in cuts]
    turned = [[one.T for one in pair] for pair in ones]
    weights = [
        [
            jnp.where(causal, dot_nt(feats[odd][at], feats[2 + odd][at]), 0.0).astype(bf16)
            for odd in range(2)
        ]
        for at in cuts
    ]
    sums = [[dot_nn(turned[i][odd], feats[2 + odd][at]) for odd in range(2)] for i, at in enumerate(cuts)]
    states = [state_ref[odd] for odd in range(2)]
    for i, at in enumerate(cuts):
        mixed = []
        for odd in range(2):
            before_low = states[odd].astype(bf16)
            prefix_ref[0, i, odd] = before_low
            mixed.append(dot_nn(weights[i][odd], ones[i][odd]) + dot_nt(feats[odd][at], before_low))
            states[odd] = states[odd] + sums[i][odd]
        top = jnp.where(low, mixed[0], mixed[1])
        bottom = pltpu.roll(jnp.where(low, mixed[1], mixed[0]), HD, 1)
        o_ref[at, :] = (top / bottom).astype(bf16)
        rden_ref[0, at, :] = 1.0 / bottom
    for odd in range(2):
        state_ref[odd] = states[odd]


def block_rows(block):
    return pl.ds(pl.multiple_of(block * BLOCK, BLOCK), BLOCK)


def forward_local_kernel(
    starts_ref, lens_ref, x_ref, w_ref, gain_ref, omega_ref,
    qkv_ref, fq_ref, fk_ref, o_ref, rden_ref, prefix_ref, normed_ref, state_ref, wide_ref,
):
    pair, block = pl.program_id(0), pl.program_id(1)
    rows = block_rows(block)

    @pl.when(pair == 0)
    def _():
        unit, _ = normalise(x_ref[rows, :].astype(f32))
        normed_ref[rows, :] = (unit * gain_ref[0:1, :]).astype(bf16)

    @pl.when(block == 0)
    def _():
        spread_projection(omega_ref, wide_ref)

    forward_step(
        block, starts_ref, lens_ref, normed_ref[rows, :], w_ref[...], wide_ref,
        qkv_ref, fq_ref, fk_ref, o_ref, rden_ref, prefix_ref, state_ref,
    )


def forward_kernel(
    starts_ref, lens_ref, x_ref, omega_ref, wq_ref, wo_ref, wu_ref, wd_ref, gains_ref,
    qkv_ref, fq_ref, fk_ref, o_ref, rden_ref, prefix_ref, normed_ref, wpair_ref, gain_ref,
    fullo_ref, fullu_ref, fulld_ref,
    state_ref, wide_ref, rows_ref, unit_ref, head_ref, held_ref, heldo_ref, heldu_ref, heldd_ref, pad_ref,
    send, recv, local,
):
    pair, block = pl.program_id(0), pl.program_id(1)
    blocks = pl.num_programs(1)
    step = pair * blocks + block
    at = place()
    dp, z, core = at["dp"], at["z"], at["core"]
    full = [head_ref, held_ref.at[0], held_ref.at[1], held_ref.at[2], heldo_ref]
    full += [heldu_ref.at[0], heldu_ref.at[1], heldd_ref.at[0], heldd_ref.at[1]]
    own = [array.at[dp, z, core] for array in full]
    leave = [fullo_ref] + halves(fullu_ref, fulld_ref)
    partners = near_devices(at)

    def copy(w, k):
        return gather_copy(at, own[w], full[w], send.at[w], recv.at[w], k)

    def keep(w):
        return pltpu.make_async_copy(full[w], leave[w - 4], local.at[w])

    def fetch():
        return pltpu.make_async_copy(x_ref, rows_ref, local.at[0])

    def stages(plan):
        for w, stage in plan:
            gather_stage(functools.partial(copy, w), stage)
            if stage == 4 and w > 3:
                keep(w).start()

    @pl.when(step == 0)
    def _():
        greet(partners)
        fetch().start()
        pad_ref[...] = jnp.zeros_like(pad_ref)
        pad_ref[0:2, 0:16] = gains_ref[...]
        flat = pad_ref[...]
        turned = flat
        for i in range(1, 8):
            turned = jnp.where(at["flat"] % 8 == i, pltpu.roll(flat, 16 * i, 1), turned)
        row = lax.broadcasted_iota(jnp.int32, (16, EXTRA), 0)
        band = at["flat"] // 8
        placed = jnp.where(row == band, turned[0:1, :], 0.0) + jnp.where(row == band + 4, turned[1:2, :], 0.0)
        for part in range(3):
            for i in range(PAIRS):
                piece = wq_ref[:, part * D + i * DUO : part * D + (i + 1) * DUO].astype(bf16)
                if i == 0:
                    head_ref[dp, z, core, :, part * DUO : (part + 1) * DUO] = piece
                else:
                    held_ref[i - 1, dp, z, core, :, part * DUO : (part + 1) * DUO] = piece
        head_ref[dp, z, core, :, CHUNK:] = placed.astype(bf16)
        greeted(partners)
        stages(GATHER_PLAN[0][:4])
        heldo_ref[dp, z, core] = wo_ref[...].astype(bf16)
        for i in range(2):
            heldu_ref[i, dp, z, core] = wu_ref[:, i * (FF // 2) : (i + 1) * (FF // 2)].astype(bf16)
            heldd_ref[i, dp, z, core] = wd_ref[i * 32 : (i + 1) * 32, :].astype(bf16)
        stages(GATHER_PLAN[0][4:10])
        fetch().wait()

        @pl.loop(0, blocks)
        def _(i):
            unit_ref[block_rows(i), :] = normalise(rows_ref[block_rows(i), :].astype(f32))[0]

        stages(GATHER_PLAN[0][10:])
        packed = head_ref[..., CHUNK:].astype(f32)
        total = jnp.sum(packed.reshape(32, 16, EXTRA), axis=0)
        gain_ref[...] = jnp.zeros_like(gain_ref)
        for i in range(2):
            for j in range(4):
                gain_ref[i : i + 1, EXTRA * j : EXTRA * (j + 1)] = total[4 * i + j : 4 * i + j + 1, :]

    for when, plan in GATHER_PLAN.items():
        if 0 < when < 8:

            @pl.when(step == when)
            def _(plan=plan):
                stages(plan)

    rows = block_rows(block)

    @pl.when(pair == 0)
    def _():
        normed_ref[rows, :] = (unit_ref[rows, :] * gain_ref[0:1, :]).astype(bf16)

    for i in range(PAIRS):

        @pl.when(jnp.logical_and(block == 0, pair == i))
        def _(i=i):
            piece = held_ref[i - 1] if i else head_ref[..., :CHUNK]
            wpair_ref[...] = piece.reshape(D, CHUNK)

    @pl.when(block == 0)
    def _():
        spread_projection(omega_ref, wide_ref)

    forward_step(
        block, starts_ref, lens_ref, normed_ref[rows, :], wpair_ref[...], wide_ref,
        qkv_ref, fq_ref, fk_ref, o_ref, rden_ref, prefix_ref, state_ref,
    )

    @pl.when(step == PAIRS * blocks - 1)
    def _():
        stages(GATHER_PLAN[8])
        for w in range(4, 9):
            keep(w).wait()
        for w in range(9):
            for k in range(10):
                copy(w, k).wait_send()


def normal_parts(hidden):
    inner = 0.5 + 0.5 * lax.erf(hidden * (0.5**0.5))
    return inner, jnp.exp2(hidden * hidden * (-0.5 * log2_e)) * (1.0 / math.sqrt(2.0 * math.pi))


def feed_forward_kernel(
    block, chunk,
    lens_ref, x_ref, o_ref, cot_ref, wo_ref, wu_ref, wd_ref, gain_ref,
    out_ref, dmid_ref, do_ref, gwo_ref, gwu_ref, gwd_ref,
    awo_ref, awu_ref, awd_ref, norm_ref, normt_ref, dyt_ref, dy_ref, y_ref, dn_ref,
):
    step = pl.program_id(0)
    steps = pl.num_programs(0)

    @pl.when(step == 0)
    def _():
        awo_ref[...] = jnp.zeros_like(awo_ref)
        awu_ref[...] = jnp.zeros_like(awu_ref)
        awd_ref[...] = jnp.zeros_like(awd_ref)

    per_seg = SEG // block
    position = lax.broadcasted_iota(jnp.int32, (block, 1), 0) + (step % per_seg) * block
    valid = (position < lens_ref[step // per_seg]).astype(f32)
    dy = (cot_ref[...].astype(f32) * valid).astype(bf16)
    dy_ref[...] = dy
    dyt_ref[...] = dy.T
    gain = gain_ref[1:2, :]
    attended = o_ref[...]
    middle = x_ref[...].astype(f32) + dot_nn(attended, wo_ref[...])
    unit, inverse = normalise(middle)
    normed = (unit * gain).astype(bf16)
    norm_ref[...] = normed
    normt_ref[...] = normed.T
    y_ref[...] = middle
    dn_ref[...] = jnp.zeros_like(dn_ref)

    for index in range(FF // chunk):
        at = slice(index * chunk, (index + 1) * chunk)
        hidden = dot_nn(norm_ref[...], wu_ref[:, at])
        inner, bell = normal_parts(hidden)
        active = (hidden * inner).astype(bf16)
        slope = inner + hidden * bell
        y_ref[...] += dot_nn(active, wd_ref[at, :])
        grad_hidden = (slope * dot_nt(dy_ref[...], wd_ref[at, :])).astype(bf16)
        awd_ref[:, at] += dot_nn(dyt_ref[...], active)
        awu_ref[:, at] += dot_nn(normt_ref[...], grad_hidden)
        dn_ref[...] += dot_nt(grad_hidden, wu_ref[:, at])

    out_ref[...] = y_ref[...].astype(bf16)
    grad_middle = dy_ref[...].astype(f32) + normalise_back(dn_ref[...], gain, unit, inverse)
    dmid_ref[...] = grad_middle
    branch = grad_middle.astype(bf16)
    awo_ref[...] += dot_tn(attended, branch)
    do_ref[...] = dot_nt(branch, wo_ref[...])

    @pl.when(step == steps - 1)
    def _():
        gwo_ref[...] = awo_ref[...].astype(bf16)
        gwu_ref[...] = awu_ref[...].astype(bf16)
        gwd_ref[...] = awd_ref[...].astype(bf16).T


def backward_step(
    block, blocks, starts_ref, qkv_ref, fq_ref, fk_ref, o_ref, rden_ref, do_ref, prefix_ref, wide_ref,
    suffix_ref, store,
):
    per_seg = SEG // BLOCK

    @pl.when(block % per_seg == per_seg - 1)
    def _():
        after = jnp.minimum(block // per_seg + 1, blocks // per_seg - 1)
        ends = jnp.logical_or(block == blocks - 1, starts_ref[after] != 0)
        suffix_ref[...] = jnp.where(ends, 0.0, suffix_ref[...])

    lane, low = lane_masks(TILE)
    causal, anti = causal_masks()
    state_row = lax.broadcasted_iota(jnp.int32, (DUO, FEAT), 0)
    for tile in reversed(range(TILES_BLOCK)):
        at = slice(tile * TILE, (tile + 1) * TILE)
        scaled = do_ref[at, :] * rden_ref[0, at, :]
        product = scaled * o_ref[at, :].astype(f32)
        scaled = scaled.astype(bf16).astype(f32)
        ones = with_ones(qkv_ref[0, at, 2 * DUO :], low)
        back = [[], [], []]
        for odd in range(2):
            free = 0 if odd else HD
            mine = jnp.logical_not(low) if odd else low
            grad_den = -jnp.sum(jnp.where(mine, product, 0.0), axis=-1, keepdims=True)
            grad_one = jnp.where(mine, scaled, jnp.where(lane == free, grad_den, 0.0)).astype(bf16)
            query_feat = fq_ref[0, at, odd * FEAT : (odd + 1) * FEAT]
            key_feat = fk_ref[0, at, odd * FEAT : (odd + 1) * FEAT]
            one = ones[odd]
            after = suffix_ref[odd]
            edge = after[free : free + 1, :]
            rest = edge - edge.astype(bf16).astype(f32)
            after_low = jnp.where(state_row == free + 1, rest, after).astype(bf16)
            before_low = prefix_ref[0, tile, odd]
            weights_t = jnp.where(anti, dot_nt(key_feat, query_feat), 0.0).astype(bf16)
            grad_w = jnp.where(causal, dot_nt(grad_one, one), 0.0).astype(bf16)
            grad_wt = jnp.where(anti, dot_nt(one, grad_one), 0.0).astype(bf16)
            grad_fq = dot_nn(grad_w, key_feat) + dot_nn(grad_one, before_low)
            grad_fk = dot_nn(grad_wt, query_feat) + dot_nn(one, after_low)
            back[2].append(dot_nn(weights_t, grad_one) + dot_nt(key_feat, after_low))
            suffix_ref[odd] = after + dot_tn(grad_one, query_feat)
            grad_pq = (grad_fq * query_feat.astype(f32)).astype(bf16)
            grad_pk = (grad_fk * key_feat.astype(f32)).astype(bf16)
            back[0].append(dot_nt(grad_pq, wide_ref[odd]))
            back[1].append(dot_nt(grad_pk, wide_ref[odd]))
        for part in range(2):
            top = jnp.where(low, back[part][0], back[part][1])
            bottom = pltpu.roll(jnp.where(low, back[part][1], back[part][0]), HD, 1)
            values = qkv_ref[0, at, part * DUO : (part + 1) * DUO].astype(f32)
            store(tile, part, top * feat_scale - bottom * (feat_scale * feat_scale) * values)
        store(tile, 2, jnp.where(low, back[2][0], back[2][1]))


def pair_lanes(pair):
    return pl.ds(pl.multiple_of(pair * CHUNK, CHUNK), CHUNK)


def store_into(dqkv_ref, pair, block):
    def store(tile, part, value):
        rows = pl.ds(pl.multiple_of(block * BLOCK + tile * TILE, TILE), TILE)
        lanes = pl.ds(pl.multiple_of(pair * CHUNK + part * DUO, DUO), DUO)
        dqkv_ref[rows, lanes] = value.astype(bf16)

    return store


def input_gradient(i, x_ref, dqkv_ref, weight_ref, gain, dmid_ref):
    rows = pl.ds(pl.multiple_of(i * TILE, TILE), TILE)
    grad_normed = dot_nt(dqkv_ref[rows, :], weight_ref[...])
    unit, inverse = normalise(x_ref[rows, :].astype(f32))
    dmid_ref[rows, :] = dmid_ref[rows, :] + normalise_back(grad_normed, gain, unit, inverse)
    return rows


def backward_local_kernel(
    starts_ref, normed_ref, qkv_ref, fq_ref, fk_ref, o_ref, rden_ref, do_ref, prefix_ref, omega_ref, gain_ref,
    x_ref, dmid_in_ref, weight_ref,
    gin_ref, gw_ref,
    suffix_ref, wide_ref, dqkv_ref, turned_ref,
):
    pair, step = pl.program_id(0), pl.program_id(1)
    blocks = pl.num_programs(1)
    block = blocks - 1 - step

    @pl.when(step == 0)
    def _():
        ones_projection(omega_ref, wide_ref)

    @pl.when(pair == 0)
    def _():
        turned_ref[:, block_rows(block)] = normed_ref[...].T

    backward_step(
        block, blocks, starts_ref, qkv_ref, fq_ref, fk_ref, o_ref, rden_ref, do_ref, prefix_ref, wide_ref,
        suffix_ref, store_into(dqkv_ref, pair, block),
    )

    @pl.when(step == blocks - 1)
    def _():
        gw_ref[...] = dot_nn(turned_ref[...], dqkv_ref[:, pair_lanes(pair)]).astype(bf16)

    @pl.when(jnp.logical_and(step == blocks - 1, pair == PAIRS - 1))
    def _():
        gin_ref[...] = dmid_in_ref[...]

        @pl.loop(0, blocks * TILES_BLOCK)
        def _(i):
            input_gradient(i, x_ref, dqkv_ref, weight_ref, gain_ref[0:1, :], gin_ref)


def eye_row(column):
    row = lax.broadcasted_iota(jnp.int32, (16, 16), 0)
    lane = lax.broadcasted_iota(jnp.int32, (16, 16), 1)
    return jnp.sum(jnp.where(row == lane, column, 0.0), axis=0, keepdims=True)


def row_squares(value):
    return jnp.sum(value * value, axis=-1, keepdims=True).sum(axis=0, keepdims=True)


def backward_kernel(
    starts_ref, normed_ref, qkv_ref, fq_ref, fk_ref, o_ref, rden_ref, do_ref, prefix_ref, omega_ref, gain_ref,
    wq_ref, wu_ref, own_gain_ref, x_ref, dmid_ref, weight_ref, go_ref, gu_ref, gd_ref,
    gin_ref, ro_ref, ru_ref, rd_ref, rq_ref, rg_ref, norm_ref,
    suffix_ref, wide_ref, dqkv_ref, turned_ref, gq_ref,
    rows_ref, mid_ref, held_ref,
    po_ref, pu_ref, pd_ref, pq_ref, so_ref, su_ref, sd_ref, sq_ref, bo_ref, bu_ref, bd_ref, bq_ref,
    last_ref, near_ref, send, recv, local, out_sem, last_send, last_recv, near_send, near_recv,
):
    pair, inner_step = pl.program_id(0), pl.program_id(1)
    blocks = pl.num_programs(1)
    block = blocks - 1 - inner_step
    step = pair * blocks + inner_step
    at = place()
    dp, z, core = at["dp"], at["z"], at["core"]
    grads = [go_ref] + halves(gu_ref, gd_ref) + [gq_ref.at[i] for i in range(PAIRS)]

    def each(out, up, down, pairs):
        return [out, up.at[0], up.at[1], down.at[0], down.at[1]] + [pairs.at[i] for i in range(PAIRS)]

    parts = each(po_ref, pu_ref, pd_ref, pq_ref)
    sums = each(so_ref, su_ref, sd_ref, sq_ref)
    boxes = each(bo_ref, bu_ref, bd_ref, bq_ref)
    results = [ro_ref, ru_ref.at[:, : FF // 2], ru_ref.at[:, FF // 2 :], rd_ref.at[:32], rd_ref.at[32:]]
    results += [rq_ref.at[i] for i in range(PAIRS)]
    others = all_devices(at)

    def copy(w, k):
        return scatter_copy(at, grads[w], parts[w], sums[w], boxes[w], send.at[w], recv.at[w], k)

    def keep(w):
        return pltpu.make_async_copy(grads[w].at[:, :, core], parts[w], local.at[w])

    def late(i):
        src = (x_ref, dmid_ref, weight_ref)[i]
        dst = (rows_ref, mid_ref, held_ref)[i]
        return pltpu.make_async_copy(src, dst, local.at[5 + i])

    def stages(plan):
        for w, stage in plan:
            if w < 5:
                if stage == 0:
                    keep(w).start()
                if stage == 1:
                    keep(w).wait()
                mine = lambda index, w=w: parts[w][index]
            else:
                mine = lambda index, w=w: gq_ref[w - 5, index, :, core]
            scatter_stage(at, functools.partial(copy, w), mine, parts[w], sums[w], boxes[w], stage)
            if stage == 4:
                results[w][...] = scatter_total(at, parts[w], boxes[w])

    @pl.when(step == 0)
    def _():
        greet(others)
        for i in range(3):
            late(i).start()

    @pl.when(step == 1)
    def _():
        greeted(others)

    for when, plan in SCATTER_PLAN.items():

        @pl.when(step == when)
        def _(plan=plan):
            stages(plan)

    @pl.when(inner_step == 0)
    def _():
        ones_projection(omega_ref, wide_ref)

    @pl.when(pair == 0)
    def _():
        turned_ref[:, block_rows(block)] = normed_ref[...].T

    backward_step(
        block, blocks, starts_ref, qkv_ref, fq_ref, fk_ref, o_ref, rden_ref, do_ref, prefix_ref, wide_ref,
        suffix_ref, store_into(dqkv_ref, pair, block),
    )

    for i in range(PAIRS):

        @pl.when(step == (i + 1) * blocks - 1)
        def _(i=i):
            grad = dot_nn(turned_ref[...], dqkv_ref[:, i * CHUNK : (i + 1) * CHUNK]).astype(bf16)
            gq_ref[i] = grad.reshape(4, 4, 2, 16, CHUNK)
            stages([(5 + i, 0)])

    @pl.when(step == PAIRS * blocks - 1)
    def _():
        for i in range(3):
            late(i).wait()
        tiles = blocks * TILES_BLOCK

        def inputs_part(first, last):
            @pl.loop(first * tiles // 8, last * tiles // 8)
            def _(i):
                rows = input_gradient(i, rows_ref, dqkv_ref, held_ref, gain_ref[0:1, :], mid_ref)
                pltpu.make_async_copy(mid_ref.at[rows], gin_ref.at[rows], out_sem.at[i]).start()

        def last(i):
            return direct_copy(at, parts[8], last_ref, last_send, last_recv, i)

        stages([(4, 3), (6, 3), (7, 3)])
        inputs_part(0, 1)
        copy(8, 0).wait_recv()
        for i in range(4):
            index = (dp + i) % 4
            parts[8][index] = add_low(gq_ref[3, index, :, core], sums[8][index])
            for j in range(4):
                if i + j:
                    last(4 * i + j).start()
        inputs_part(1, 5)
        stages([(1, 4), (2, 4), (3, 4), (5, 4), (4, 4), (6, 4), (7, 4)])
        inputs_part(5, 8)
        early = row_squares(ro_ref[...]) + row_squares(ru_ref[...]) + row_squares(rd_ref[...])
        for i in range(PAIRS - 1):
            early = early + row_squares(rq_ref[i])
        up_low = wu_ref[...].astype(bf16).astype(f32)
        gain_low = own_gain_ref[...].astype(bf16).astype(f32)
        second = eye_row(jnp.sum(ru_ref[...] * up_low, axis=-1, keepdims=True)) / gain_low[1:2, :]
        total = parts[8][dp, z].astype(f32)
        for i in range(1, 16):
            last(i).wait_recv()
            total = total + last_ref[i - 1].astype(f32)
        rq_ref[3] = total
        first = jnp.zeros((16, 1), f32)
        for i in range(PAIRS):
            for part in range(3):
                low_w = wq_ref[:, part * D + i * DUO : part * D + (i + 1) * DUO].astype(bf16).astype(f32)
                first = first + jnp.sum(
                    rq_ref[i, :, part * DUO : (part + 1) * DUO] * low_w, axis=-1, keepdims=True
                )
        first = eye_row(first) / gain_low[0:1, :]
        rg_ref[0:1, :] = first
        rg_ref[1:2, :] = second
        squares = early + row_squares(rq_ref[PAIRS - 1]) + row_squares(first) + row_squares(second)
        mine = near_ref.at[at["flat"]]
        mine[...] = jnp.broadcast_to(squares, (8, 128))

        def near(i):
            return pltpu.make_async_remote_copy(
                src_ref=mine, dst_ref=mine, send_sem=near_send.at[i], recv_sem=near_recv.at[i],
                device_id=others[i], device_id_type=MESH,
            )

        for i in range(31):
            near(i).start()
        for i in range(31):
            near(i).wait_recv()
        group = near_ref[0]
        for i in range(1, 32):
            group = group + near_ref[i]
        norm_ref[...] = group

        @pl.loop(0, tiles)
        def _(i):
            rows = pl.ds(pl.multiple_of(i * TILE, TILE), TILE)
            pltpu.make_async_copy(mid_ref.at[rows], gin_ref.at[rows], out_sem.at[i]).wait()

        for i in range(31):
            near(i).wait_send()
        for i in range(1, 16):
            last(i).wait_send()
        copy(8, 0).wait_send()
        for w in range(8):
            for k in range(7):
                copy(w, k).wait_send()


def update_kernel(
    count_ref, total_ref, rq_ref, ro_ref, ru_ref, rd_ref, rg_ref,
    wq_ref, wo_ref, wu_ref, wd_ref, wg_ref, mq_ref, mo_ref, mu_ref, md_ref, mg_ref,
    vq_ref, vo_ref, vu_ref, vd_ref, vg_ref, gin_ref,
    norm_ref, gq_ref, nvq_ref, nwq_ref, go_ref, nvo_ref, nwo_ref, gu_ref, nvu_ref, nwu_ref,
    gd_ref, nvd_ref, nwd_ref, gg_ref, nvg_ref, nwg_ref, gin_out_ref,
):
    gin_out_ref[...] = gin_ref[...]

    @pl.when(pl.program_id(0) == 0)
    def _():
        update_weights(
            count_ref, total_ref, rq_ref, ro_ref, ru_ref, rd_ref, rg_ref,
            wq_ref, wo_ref, wu_ref, wd_ref, wg_ref, mq_ref, mo_ref, mu_ref, md_ref, mg_ref,
            vq_ref, vo_ref, vu_ref, vd_ref, vg_ref,
            norm_ref, gq_ref, nvq_ref, nwq_ref, go_ref, nvo_ref, nwo_ref, gu_ref, nvu_ref, nwu_ref,
            gd_ref, nvd_ref, nwd_ref, gg_ref, nvg_ref, nwg_ref,
        )


def update_weights(
    count_ref, total_ref, rq_ref, ro_ref, ru_ref, rd_ref, rg_ref,
    wq_ref, wo_ref, wu_ref, wd_ref, wg_ref, mq_ref, mo_ref, mu_ref, md_ref, mg_ref,
    vq_ref, vo_ref, vu_ref, vd_ref, vg_ref,
    norm_ref, gq_ref, nvq_ref, nwq_ref, go_ref, nvo_ref, nwo_ref, gu_ref, nvu_ref, nwu_ref,
    gd_ref, nvd_ref, nwd_ref, gg_ref, nvg_ref, nwg_ref,
):
    norm = jnp.sqrt(total_ref[0:1, 0:1])
    norm_ref[...] = norm
    factor = jnp.minimum(1.0, clip_level / norm)
    count = jnp.full((1, 1), count_ref[0], jnp.int32).astype(f32)
    first_fix = 1.0 - jnp.exp2(count * math.log2(beta_first))
    second_fix = 1.0 - jnp.exp2(count * math.log2(beta_second))

    def update(grad, at, weight, first, second, rate, outs):
        clipped = grad * factor
        first_new = beta_first * first[at] + (1.0 - beta_first) * clipped
        second_new = beta_second * second[at] + (1.0 - beta_second) * clipped * clipped
        direction = first_new / first_fix / (jnp.sqrt(second_new / second_fix) + adam_eps)
        outs[0][at] = clipped
        outs[1][at] = second_new
        outs[2][at] = weight[at] - rate * (direction + decay_weight * weight[at])

    for part in range(3):
        for i in range(PAIRS):
            at = (slice(None), slice(part * D + i * DUO, part * D + (i + 1) * DUO))
            grad = rq_ref[i, :, part * DUO : (part + 1) * DUO]
            update(grad, at, wq_ref, mq_ref, vq_ref, rate_matrix, (gq_ref, nvq_ref, nwq_ref))
    update(ro_ref[...], ..., wo_ref, mo_ref, vo_ref, rate_matrix, (go_ref, nvo_ref, nwo_ref))
    update(ru_ref[...], ..., wu_ref, mu_ref, vu_ref, rate_matrix, (gu_ref, nvu_ref, nwu_ref))
    update(rd_ref[...], ..., wd_ref, md_ref, vd_ref, rate_matrix, (gd_ref, nvd_ref, nwd_ref))
    update(rg_ref[...], ..., wg_ref, mg_ref, vg_ref, rate_gain, (gg_ref, nvg_ref, nwg_ref))


ROWS = {"pair": 16, "out": 16, "up": 16, "down": 64}
COLS = {"pair": CHUNK, "out": D, "up": FF, "down": D}
LATE = ("out", "up", "down")
smem = pl.BlockSpec(memory_space=pltpu.SMEM)
hbm = pl.BlockSpec(memory_space=pl.ANY)
vmem = pl.BlockSpec(memory_space=pltpu.VMEM)


def shaped(shape, dtype):
    return jax.ShapeDtypeStruct(shape, dtype)


def params(collective_id=None):
    if collective_id is None:
        return pltpu.CompilerParams(vmem_limit_bytes=VMEM_LIMIT)
    return pltpu.CompilerParams(vmem_limit_bytes=VMEM_LIMIT, collective_id=collective_id, has_side_effects=True)


def whole(shape):
    return pl.BlockSpec(shape, lambda *_: (0,) * len(shape), pipeline_mode=pl.Buffered(1))


def whole_out(shape):
    return pl.BlockSpec(shape, lambda *_: (0,) * len(shape))


def five(name):
    return (4, 4, 2, ROWS[name], COLS[name])


def forward_outs(tokens):
    tiles = tokens // TILE
    specs = [
        pl.BlockSpec((1, BLOCK, CHUNK), lambda p, b: (p, b, 0)),
        pl.BlockSpec((1, BLOCK, 2 * FEAT), lambda p, b: (p, b, 0)),
        pl.BlockSpec((1, BLOCK, 2 * FEAT), lambda p, b: (p, b, 0)),
        pl.BlockSpec((BLOCK, DUO), lambda p, b: (b, p)),
        pl.BlockSpec((1, BLOCK, DUO), lambda p, b: (p, b, 0)),
        pl.BlockSpec((1, TILES_BLOCK, 2, DUO, FEAT), lambda p, b: (p, b, 0, 0, 0)),
        whole_out((tokens, D)),
    ]
    shapes = [
        shaped((PAIRS, tokens, CHUNK), bf16),
        shaped((PAIRS, tokens, 2 * FEAT), bf16),
        shaped((PAIRS, tokens, 2 * FEAT), bf16),
        shaped((tokens, D), bf16),
        shaped((PAIRS, tokens, DUO), f32),
        shaped((PAIRS, tiles, 2, DUO, FEAT), bf16),
        shaped((tokens, D), bf16),
    ]
    scratch = [pltpu.VMEM((2, DUO, FEAT), f32), pltpu.VMEM((DUO, 2 * FEAT), bf16)]
    return specs, shapes, scratch


pair_omega = pl.BlockSpec((2, HD, FEAT), lambda p, b: (p, 0, 0))
pair_weight = pl.BlockSpec((D, CHUNK), lambda p, b: (0, p))


def forward_local(starts, lens, x, weight, gains, omega):
    tokens = x.shape[0]
    specs, shapes, scratch = forward_outs(tokens)
    return pl.pallas_call(
        forward_local_kernel,
        grid=(PAIRS, tokens // BLOCK),
        in_specs=[smem, smem, whole((tokens, D)), pair_weight, whole((8, D)), pair_omega],
        out_specs=specs,
        out_shape=shapes,
        scratch_shapes=scratch,
        compiler_params=params(),
    )(starts, lens, x, weight, gains, omega)


def forward(starts, lens, x, omega, wq, wo, wu, wd, gains):
    tokens = x.shape[0]
    specs, shapes, scratch = forward_outs(tokens)
    return pl.pallas_call(
        forward_kernel,
        grid=(PAIRS, tokens // BLOCK),
        in_specs=[smem, smem, hbm, pair_omega] + [whole(array.shape) for array in (wq, wo, wu, wd, gains)],
        out_specs=specs + [pair_weight, whole_out((8, D)), hbm, hbm, hbm],
        out_shape=shapes + [shaped((D, WIDE), bf16), shaped((8, D), f32)]
        + [shaped(five(name), bf16) for name in LATE],
        scratch_shapes=scratch
        + [
            pltpu.VMEM((tokens, D), bf16),
            pltpu.VMEM((tokens, D), f32),
            pltpu.VMEM((4, 4, 2, 16, CHUNK + EXTRA), bf16),
            pltpu.VMEM((PAIRS - 1, *five("pair")), bf16),
        ]
        + [
            pltpu.VMEM(five("out"), bf16),
            pltpu.VMEM((2, 4, 4, 2, 16, FF // 2), bf16),
            pltpu.VMEM((2, 4, 4, 2, 32, D), bf16),
            pltpu.VMEM((8, EXTRA), f32),
            pltpu.SemaphoreType.DMA((9, 10)),
            pltpu.SemaphoreType.DMA((9, 10)),
            pltpu.SemaphoreType.DMA((9,)),
        ],
        compiler_params=params(0),
    )(starts, lens, x, omega, wq, wo, wu, wd, gains)


def feed_forward(lens, x, o, cot, wo, wu, wd, gains, block=512, chunk=512):
    tokens = x.shape[0]
    rows = pl.BlockSpec((block, D), lambda i: (i, 0))
    return pl.pallas_call(
        functools.partial(feed_forward_kernel, block, chunk),
        grid=(tokens // block,),
        in_specs=[smem, rows, rows, rows, whole((D, D)), whole((D, FF)), whole((FF, D)), whole((8, D))],
        out_specs=[rows, rows, rows, whole_out((D, D)), whole_out((D, FF)), whole_out((FF, D))],
        out_shape=[
            shaped((tokens, D), bf16),
            shaped((tokens, D), f32),
            shaped((tokens, D), f32),
            shaped((D, D), bf16),
            shaped((D, FF), bf16),
            shaped((FF, D), bf16),
        ],
        scratch_shapes=[
            pltpu.VMEM((D, D), f32), pltpu.VMEM((D, FF), f32), pltpu.VMEM((D, FF), f32),
            pltpu.VMEM((block, D), bf16), pltpu.VMEM((D, block), bf16), pltpu.VMEM((D, block), bf16),
            pltpu.VMEM((block, D), bf16), pltpu.VMEM((block, D), f32), pltpu.VMEM((block, D), f32),
        ],
        compiler_params=params(),
    )(lens, x, o, cot, wo, wu, wd, gains)


def backward_ins(blocks):
    last = blocks - 1
    return [
        smem,
        pl.BlockSpec((BLOCK, D), lambda p, b: (jnp.where(p == 0, last - b, 0), 0)),
        pl.BlockSpec((1, BLOCK, CHUNK), lambda p, b: (p, last - b, 0)),
        pl.BlockSpec((1, BLOCK, 2 * FEAT), lambda p, b: (p, last - b, 0)),
        pl.BlockSpec((1, BLOCK, 2 * FEAT), lambda p, b: (p, last - b, 0)),
        pl.BlockSpec((BLOCK, DUO), lambda p, b: (last - b, p)),
        pl.BlockSpec((1, BLOCK, DUO), lambda p, b: (p, last - b, 0)),
        pl.BlockSpec((BLOCK, DUO), lambda p, b: (last - b, p)),
        pl.BlockSpec((1, TILES_BLOCK, 2, DUO, FEAT), lambda p, b: (p, last - b, 0, 0, 0)),
        pair_omega,
        whole((8, D)),
    ]


def backward_scratch(tokens):
    return [
        pltpu.VMEM((2, DUO, FEAT), f32),
        pltpu.VMEM((2, DUO, FEAT), bf16),
        pltpu.VMEM((tokens, WIDE), bf16),
        pltpu.VMEM((D, tokens), bf16),
    ]


def backward_local(args, x, dmid, weight):
    tokens = x.shape[0]
    return pl.pallas_call(
        backward_local_kernel,
        grid=(PAIRS, tokens // BLOCK),
        in_specs=backward_ins(tokens // BLOCK) + [whole((tokens, D)), whole((tokens, D)), whole((D, WIDE))],
        out_specs=[whole_out((tokens, D)), pair_weight],
        out_shape=[shaped((tokens, D), f32), shaped((D, WIDE), bf16)],
        scratch_shapes=backward_scratch(tokens),
        compiler_params=params(),
    )(*args, x, dmid, weight)


def backward(args, wq, wu, gains, x, dmid, weight, grads):
    tokens = x.shape[0]
    half = [(4, 4, 16, D), (2, 4, 4, 16, FF // 2), (2, 4, 4, 32, D), (PAIRS, 4, 4, 16, CHUNK)]
    grads = [grad.reshape(five(name)) for grad, name in zip(grads, LATE)]
    dma = pltpu.SemaphoreType.DMA
    return pl.pallas_call(
        backward_kernel,
        grid=(PAIRS, tokens // BLOCK),
        in_specs=backward_ins(tokens // BLOCK) + [whole(wq.shape), whole(wu.shape), whole(gains.shape)] + [hbm] * 6,
        out_specs=[hbm]
        + [whole_out((ROWS[name], COLS[name])) for name in LATE]
        + [whole_out((PAIRS, 16, CHUNK)), whole_out((2, 16)), whole_out((8, 128))],
        out_shape=[shaped((tokens, D), f32)]
        + [shaped((ROWS[name], COLS[name]), f32) for name in LATE]
        + [shaped((PAIRS, 16, CHUNK), f32), shaped((2, 16), f32), shaped((8, 128), f32)],
        scratch_shapes=backward_scratch(tokens)
        + [pltpu.VMEM((PAIRS, *five("pair")), bf16)]
        + [pltpu.VMEM((tokens, D), bf16), pltpu.VMEM((tokens, D), f32), pltpu.VMEM((D, WIDE), bf16)]
        + [pltpu.VMEM(shape, bf16) for shape in half] * 3
        + [pltpu.VMEM((15, 16, CHUNK), bf16), pltpu.VMEM((32, 8, 128), f32)]
        + [dma((9, 7)), dma((9, 7)), dma((8,)), dma((tokens // TILE,)), dma((15,)), dma((15,)), dma((31,)), dma((31,))],
        compiler_params=params(1),
    )(*args, wq, wu, gains, x, dmid, weight, *grads)


def update_all(count, total, grads, weights, firsts, seconds, grad_inputs):
    shapes = [shaped((1, 1), f32)]
    for weight in weights:
        shapes += [shaped(weight.shape, f32)] * 3
    arrays = (total, *grads, *weights, *firsts, *seconds)
    rows = pl.BlockSpec((UPDATE_ROWS, D), lambda i: (i, 0))
    return pl.pallas_call(
        update_kernel,
        grid=(grad_inputs.shape[0] // UPDATE_ROWS,),
        in_specs=[smem] + [whole(array.shape) for array in arrays] + [rows],
        out_specs=[whole_out(shape.shape) for shape in shapes] + [rows],
        out_shape=shapes + [shaped(grad_inputs.shape, f32)],
        compiler_params=params(),
    )(count.reshape(1), *arrays, grad_inputs)


def to_pairs(weight):
    split = weight.reshape(weight.shape[0], 3, PAIRS, DUO)
    return jnp.swapaxes(split, 1, 2).reshape(weight.shape)


def from_pairs(weight):
    split = weight.reshape(weight.shape[0], PAIRS, 3, DUO)
    return jnp.swapaxes(split, 1, 2).reshape(weight.shape)


def on_device(
    sizes, inputs, cotangent, feature_omega, seg_start, seg_len, step_count,
    w_qkv, w_out, w_up, w_down, gains,
    m_qkv, m_out, m_up, m_down, m_gains,
    v_qkv, v_out, v_up, v_down, v_gains,
):
    weights = (w_qkv, w_out, w_up, w_down, gains)
    firsts = (m_qkv, m_out, m_up, m_down, m_gains)
    seconds = (v_qkv, v_out, v_up, v_down, v_gains)
    if sizes == (4, 8):
        (qkv, fq, fk, attended, rden, prefix, normed, qkv_full, gain_full, out_full, up_full, down_full) = forward(
            seg_start, seg_len, inputs, feature_omega, *weights
        )
        out_rows, dmid, grad_attended, grad_out, grad_up, grad_down = feed_forward(
            seg_len, inputs, attended, cotangent, out_full.reshape(D, D), up_full.reshape(D, FF),
            down_full.reshape(FF, D), gain_full,
        )
        grad_inputs, r_out, r_up, r_down, r_qkv, r_gains, total = backward(
            (seg_start, normed, qkv, fq, fk, attended, rden, grad_attended, prefix, feature_omega, gain_full),
            w_qkv, w_up, gains, inputs, dmid, qkv_full, (grad_out, grad_up, grad_down),
        )
        norm, *updated, grad_inputs = update_all(
            step_count, total, (r_qkv, r_out, r_up, r_down, r_gains), weights, firsts, seconds, grad_inputs
        )
        return (out_rows, grad_inputs, norm.reshape(()), *updated)

    def gather(piece, axis=0):
        return lax.all_gather(piece.astype(bf16), AXES, axis=axis, tiled=True)

    qkv_full, out_full, up_full, down_full = (gather(piece) for piece in weights[:4])
    qkv_full = to_pairs(qkv_full)
    gain_full = jnp.pad(gather(gains, 1).astype(f32), ((0, 6), (0, 0)))
    qkv, fq, fk, attended, rden, prefix, normed = forward_local(
        seg_start, seg_len, inputs, qkv_full, gain_full, feature_omega
    )
    out_rows, dmid, grad_attended, grad_out, grad_up, grad_down = feed_forward(
        seg_len, inputs, attended, cotangent, out_full, up_full, down_full, gain_full
    )
    grad_inputs, grad_qkv = backward_local(
        (seg_start, normed, qkv, fq, fk, attended, rden, grad_attended, prefix, feature_omega, gain_full),
        inputs, dmid, qkv_full,
    )

    def scatter(piece):
        return lax.psum_scatter(piece.astype(f32), AXES, scatter_dimension=0, tiled=True)

    reduced = [scatter(piece) for piece in (from_pairs(grad_qkv), grad_out, grad_up, grad_down)]
    low = [weight.astype(bf16).astype(f32) for weight in weights]
    first = jnp.sum(reduced[0] * low[0], axis=1) / low[4][0]
    second = jnp.sum(reduced[2] * low[2], axis=1) / low[4][1]
    reduced.append(jnp.stack([first, second], axis=0))
    grad_norm = jnp.sqrt(lax.psum(sum(jnp.sum(piece * piece) for piece in reduced), AXES))
    factor = jnp.minimum(1.0, clip_level / grad_norm)
    count = step_count.astype(f32)
    first_fix = 1.0 - jnp.power(beta_first, count)
    second_fix = 1.0 - jnp.power(beta_second, count)
    updated = []
    rates = (rate_matrix,) * 4 + (rate_gain,)
    for weight, first, second, gradient, rate in zip(weights, firsts, seconds, reduced, rates):
        clipped = gradient * factor
        first_new = beta_first * first + (1.0 - beta_first) * clipped
        second_new = beta_second * second + (1.0 - beta_second) * clipped * clipped
        direction = first_new / first_fix / (jnp.sqrt(second_new / second_fix) + adam_eps)
        updated += [clipped, second_new, weight - rate * (direction + decay_weight * weight)]
    return (out_rows, grad_inputs, grad_norm, *updated)


def solution(mesh):
    return jax.shard_map(
        functools.partial(on_device, tuple(mesh.shape[name] for name in AXES)),
        mesh=mesh,
        in_specs=(
            P(("dp", "fsdp"), None),
            P(("dp", "fsdp"), None),
            P(),
            P(("dp", "fsdp")),
            P(("dp", "fsdp")),
            P(),
            P(("dp", "fsdp"), None),
            P(("dp", "fsdp"), None),
            P(("dp", "fsdp"), None),
            P(("dp", "fsdp"), None),
            P(None, ("dp", "fsdp")),
            P(("dp", "fsdp"), None),
            P(("dp", "fsdp"), None),
            P(("dp", "fsdp"), None),
            P(("dp", "fsdp"), None),
            P(None, ("dp", "fsdp")),
            P(("dp", "fsdp"), None),
            P(("dp", "fsdp"), None),
            P(("dp", "fsdp"), None),
            P(("dp", "fsdp"), None),
            P(None, ("dp", "fsdp")),
        ),
        out_specs=(
            P(("dp", "fsdp"), None),
            P(("dp", "fsdp"), None),
            P(),
            P(("dp", "fsdp"), None),
            P(("dp", "fsdp"), None),
            P(("dp", "fsdp"), None),
            P(("dp", "fsdp"), None),
            P(("dp", "fsdp"), None),
            P(("dp", "fsdp"), None),
            P(("dp", "fsdp"), None),
            P(("dp", "fsdp"), None),
            P(("dp", "fsdp"), None),
            P(("dp", "fsdp"), None),
            P(("dp", "fsdp"), None),
            P(("dp", "fsdp"), None),
            P(None, ("dp", "fsdp")),
            P(None, ("dp", "fsdp")),
            P(None, ("dp", "fsdp")),
        ),
        check_vma=False,
    )
```

time: 1150 us -> 168 us (0.15); the launches traced: 1140 us -> 168 us
  waiting for transfers between devices: 587 us -> 0 us
  matrix products: 285 us -> 0 us
  Pallas kernels: 0 us -> 166 us
  blocking collectives: 119 us -> 0 us
  other arithmetic: 65.6 us -> 0 us
  local copies, waits for them, and re-layouts: 58.5 us -> 0 us
  between operations: 21.3 us -> 1.5 us
    reduce_scatter x4 -> x0, waiting for transfers between devices: 514 us -> none  [the longest x1 141 us: on_device(): lax.psum_scatter(grad_up, ('dp', 'fsdp'), scatter_dimension=0, tiled=True)]
    dot_general x34 -> x0, matrix products: 285 us -> none  [the longest x1 46.2 us: on_device(): hidden = jnp.dot(normed_two, up_full, preferred_element_type=jnp.float32)]
    pallas_call x0 -> x4, Pallas kernels: none -> 166 us  [the longest x1 65.4 us: backward(): pl.pallas_call(backward_kernel, grid=(PAIRS, tokens // BLOCK), in_specs=b...]
    all_gather x2 -> x0, blocking collectives: 82.4 us -> none  [the longest x1 43 us: fetch(): lax.all_gather(shards[4], ('dp', 'fsdp'), axis=1, tiled=True)]
    unnamed x9 -> x0, waiting for transfers between devices: 73.5 us -> none
    reduce_sum x14 -> x0, other arithmetic: 43.3 us -> none  [the longest x2 28.5 us: feature_back(): jnp.sum(weighted, axis=-1, keepdims=True)]
    psum x1 -> x0, blocking collectives: 36.8 us -> none  [on_device(): grad_norm = jnp.sqrt(lax.psum(local_squares, ('dp', 'fsdp')))]
    unnamed x182 -> x0, local copies, waits for them, and re-layouts: 32.8 us -> none
  transfers between devices with their start and end apart: 8 -> 0, of which waited for: 5 -> 0; matrix products, arithmetic and copies ran while one was open for 17% -> 0% of each run, Pallas kernels for 0% -> 0%
where the time goes in v2:
time: 168 us
  Pallas kernels  166 us (99%)
    pallas_call x1, Pallas kernels, backward(): pl.pallas_call(backward_kernel, grid=(PAIRS, tokens // BLOCK), in_specs=b...  65.4 us
    pallas_call x1, Pallas kernels, forward(): pl.pallas_call(forward_kernel, grid=(PAIRS, tokens // BLOCK), in_specs=[s...  53.1 us
    pallas_call x1, Pallas kernels, feed_forward(): pl.pallas_call(functools.partial(feed_forward_kernel, block, chunk), grid...  41.6 us
    pallas_call x1, Pallas kernels, update_all(): pl.pallas_call(update_kernel, grid=(grad_inputs.shape[0] // UPDATE_ROWS,)...  6.17 us

profile of v2, /device:TPU:0, one launch (start us, length us, event | category | flops | bytes accessed | tf_op | source)
XLA Modules:
  0.0 167.8 jit_solution(6599002901466962935)
XLA Ops:
  0.7 53.1 %shard_map.340 = (bf16[4,2048,384]{2,1,0:T(8,128)(2,1)}, bf16[4,2048,512]{2,1,0:T(8,128)(2,1)}, bf16[4,2048,512]{2,1,0:T(8,128)(2,1)}, bf16[2048,512]{1,0:T(8,12...) custom-call(s32[2]{0:T(128)} %starts_ref.3, ...), custom_call_target="tpu_custom_call" | custom-call | tf_op jit(solution)/shard_map/pallas_call | solution.py:960
  53.8 41.6 %shard_map.341 = (bf16[2048,512]{1,0:T(8,128)(2,1)}, f32[2048,512]{1,0:T(8,128)}, f32[2048,512]{1,0:T(8,128)}, bf16[512,512]{1,0:T(8,128)(2,1)}, bf16[512,2048]{1,0:T(8,128)(2,1)}, /*index=5*/bf16[2048,512]{1,0:T(8,128)(2,1)}) custom-call(s32[2]{0:T(128)} %lens_ref.3, bf16[2048,512]{1,0:T(8,128)(2,1)} %x_ref.5, bf16[2048,512]{1,0:T(8,128)(2,1)} %get-tuple-element.60.o_ref, ...), custom_call_target="tpu_custom_call" | custom-call | tf_op jit(solution)/shard_map/pallas_call | solution.py:990
  95.4 65.4 %shard_map.342 = (f32[2048,512]{1,0:T(8,128)}, f32[16,512]{1,0:T(8,128)}, f32[16,2048]{1,0:T(8,128)}, f32[64,512]{1,0:T(8,128)}, f32[4,16,384]{2,1,0:T(8,128)}, /*index=5*/f32[2,16]{1,0:T(2,128)}, f32[8,128]{1,0:T(8,128)}) custom-call(s32[2]{0:T(128)} %starts_ref.3, bf16[2048,512]{1,0:T(8,128)(2,1)} %get-tuple-element.66.normed_ref, ...), custom_call_target="tpu_custom_call" | custom-call | tf_op jit(solution)/shard_map/pallas_call | solution.py:1056
  161.5 6.2 %shard_map.343 = (f32[1,1]{1,0:T(1,128)}, f32[16,1536]{1,0:T(8,128)}, f32[16,1536]{1,0:T(8,128)}, f32[16,1536]{1,0:T(8,128)}, f32[16,512]{1,0:T(8,128)}, /*index...) custom-call(s32[1]{0:T(128)} %bitcast.8.count_ref, ...), custom_call_target="tpu_custom_call" | custom-call | tf_op jit(solution)/shard_map/pallas_call | solution.py:1082

commit v3 on v2

--- a/solution.py
+++ b/solution.py
@@ -19,7 +19,11 @@
 DUO = 2 * HD
 BLOCK = 1024
 TILES_BLOCK = BLOCK // TILE
-UPDATE_ROWS = 512
+FORWARD_MIB = 60
+BACKWARD_MIB = 52
+UPDATE_MIB = 20
+FF_BLOCK = 512
+FF_CHUNK = 512
 WIDE = 3 * D
 CHUNK = 3 * DUO
 EXTRA = 128
@@ -39,7 +43,6 @@
 f32 = jnp.float32
 bf16 = jnp.bfloat16
 MESH = pl.DeviceIdType.MESH
-VMEM_LIMIT = 63 << 20
 
 
 def dot_nn(a, b):
@@ -163,17 +166,18 @@
 
 
 GATHER_PLAN = {
-    0: [(0, 0), (1, 0), (2, 0), (3, 0), (0, 1), (4, 0), (5, 0), (6, 0), (7, 0), (8, 0),
-        (0, 2), (1, 1), (2, 1), (3, 1), (0, 3), (0, 4), (1, 2), (4, 1), (5, 1)],
-    1: [(1, 3), (2, 2), (3, 2), (6, 1)],
-    2: [(1, 4), (4, 2), (5, 2), (7, 1), (2, 3), (3, 3)],
-    3: [(6, 2), (8, 1), (4, 3)],
-    4: [(2, 4), (5, 3)],
-    5: [(7, 2), (6, 3)],
-    6: [(3, 4), (8, 2), (4, 4), (5, 4)],
-    7: [(7, 3), (8, 3), (6, 4)],
-    8: [(7, 4), (8, 4)],
+    0: [(0, 0), (1, 0), (2, 0), (3, 0), (0, 1), (5, 0), (6, 0), (7, 0), (8, 0), (4, 0),
+        (0, 2), (1, 1), (2, 1), (3, 1), (0, 3), (0, 4), (1, 2), (5, 1)],
+    1: [(6, 1), (1, 3), (2, 2), (3, 2)],
+    2: [(1, 4), (7, 1), (5, 2), (8, 1)],
+    3: [(6, 2), (4, 1), (2, 3), (3, 3)],
+    4: [(2, 4), (7, 2)],
+    5: [(8, 2), (5, 3)],
+    6: [(3, 4), (4, 2), (6, 3), (5, 4)],
+    7: [(7, 3), (8, 3), (4, 3), (6, 4)],
+    8: [(4, 4), (7, 4), (8, 4)],
 }
+GATHER_END = [(7, 4), (8, 4)]
 
 
 def scatter_copy(at, grad, part, sums, boxes, send, recv, k):
@@ -284,58 +288,73 @@
     qkv_ref[0] = dot_nn(normed, weight).astype(bf16)
     position = lax.broadcasted_iota(jnp.int32, (BLOCK, 1), 0) + (block % per_seg) * BLOCK
     valid = (position < lens_ref[block // per_seg]).astype(f32)
-    _, low = lane_masks(BLOCK)
-    feats = []
-    for part, feat_ref in enumerate((fq_ref, fk_ref)):
-        rows = qkv_ref[0, :, part * DUO : (part + 1) * DUO]
-        wide = rows.astype(f32)
-        square = wide * wide
-        proj = dot_nn(rows, wide_ref[...])
-        for odd in range(2):
-            total = jnp.sum(
-                jnp.where(low, 0.0, square) if odd else jnp.where(low, square, 0.0), axis=-1, keepdims=True
-            )
-            value = jnp.exp2(
-                proj[:, odd * FEAT : (odd + 1) * FEAT] * (feat_scale * log2_e)
-                - total * (0.5 * feat_scale * feat_scale * log2_e)
-            )
-            if part:
-                value = value * valid
-            value = value.astype(bf16)
-            feat_ref[0, :, odd * FEAT : (odd + 1) * FEAT] = value
-            feats.append(value)
     _, low = lane_masks(TILE)
     causal, _ = causal_masks()
+    states = [state_ref[odd] for odd in range(2)]
     cuts = [slice(tile * TILE, (tile + 1) * TILE) for tile in range(TILES_BLOCK)]
-    values = qkv_ref[0, :, 2 * DUO :]
-    ones = [with_ones(values[at], low) for at in cuts]
-    turned = [[one.T for one in pair] for pair in ones]
-    weights = [
-        [
-            jnp.where(causal, dot_nt(feats[odd][at], feats[2 + odd][at]), 0.0).astype(bf16)
-            for odd in range(2)
+    made, mixed = {}, {}
+
+    def features(tile):
+        at = cuts[tile]
+        feats = []
+        for part, feat_ref in enumerate((fq_ref, fk_ref)):
+            rows = qkv_ref[0, at, part * DUO : (part + 1) * DUO]
+            wide = rows.astype(f32)
+            square = wide * wide
+            proj = dot_nn(rows, wide_ref[...])
+            for odd in range(2):
+                total = jnp.sum(
+                    jnp.where(low, 0.0, square) if odd else jnp.where(low, square, 0.0), axis=-1, keepdims=True
+                )
+                value = jnp.exp2(
+                    proj[:, odd * FEAT : (odd + 1) * FEAT] * (feat_scale * log2_e)
+                    - total * (0.5 * feat_scale * feat_scale * log2_e)
+                )
+                if part:
+                    value = value * valid[at]
+                value = value.astype(bf16)
+                feat_ref[0, at, odd * FEAT : (odd + 1) * FEAT] = value
+                feats.append(value)
+        made[tile] = feats, with_ones(qkv_ref[0, at, 2 * DUO :], low)
+
+    def scores(tile):
+        feats, ones = made[tile]
+        weights = [
+            jnp.where(causal, dot_nt(feats[odd], feats[2 + odd]), 0.0).astype(bf16) for odd in range(2)
         ]
-        for at in cuts
-    ]
-    sums = [[dot_nn(turned[i][odd], feats[2 + odd][at]) for odd in range(2)] for i, at in enumerate(cuts)]
-    states = [state_ref[odd] for odd in range(2)]
-    for i, at in enumerate(cuts):
-        mixed = []
+        sums = [dot_nn(ones[odd].T, feats[2 + odd]) for odd in range(2)]
+        mixed[tile] = weights, sums
+
+    def finish(tile):
+        at = cuts[tile]
+        (feats, ones), (weights, sums) = made[tile], mixed[tile]
+        both = []
         for odd in range(2):
             before_low = states[odd].astype(bf16)
-            prefix_ref[0, i, odd] = before_low
-            mixed.append(dot_nn(weights[i][odd], ones[i][odd]) + dot_nt(feats[odd][at], before_low))
-            states[odd] = states[odd] + sums[i][odd]
-        top = jnp.where(low, mixed[0], mixed[1])
-        bottom = pltpu.roll(jnp.where(low, mixed[1], mixed[0]), HD, 1)
+            prefix_ref[0, tile, odd] = before_low
+            both.append(dot_nn(weights[odd], ones[odd]) + dot_nt(feats[odd], before_low))
+            states[odd] = states[odd] + sums[odd]
+        top = jnp.where(low, both[0], both[1])
+        bottom = pltpu.roll(jnp.where(low, both[1], both[0]), HD, 1)
         o_ref[at, :] = (top / bottom).astype(bf16)
         rden_ref[0, at, :] = 1.0 / bottom
+
+    for step in range(TILES_BLOCK + 2):
+        if step < TILES_BLOCK:
+            features(step)
+        if 1 <= step <= TILES_BLOCK:
+            scores(step - 1)
+        if step >= 2:
+            finish(step - 2)
     for odd in range(2):
         state_ref[odd] = states[odd]
 
 
 def block_rows(block):
     return pl.ds(pl.multiple_of(block * BLOCK, BLOCK), BLOCK)
+
+
+ATTENTION_STEPS = 8
 
 
 def forward_local_kernel(
@@ -361,28 +380,28 @@
 
 
 def forward_kernel(
-    starts_ref, lens_ref, x_ref, omega_ref, wq_ref, wo_ref, wu_ref, wd_ref, gains_ref,
+    count_ref, starts_ref, lens_ref, x_ref, omega_ref, wq_ref, wo_ref, wu_ref, wd_ref, gains_ref, cot_ref,
     qkv_ref, fq_ref, fk_ref, o_ref, rden_ref, prefix_ref, normed_ref, wpair_ref, gain_ref,
-    fullo_ref, fullu_ref, fulld_ref,
-    state_ref, wide_ref, rows_ref, unit_ref, head_ref, held_ref, heldo_ref, heldu_ref, heldd_ref, pad_ref,
-    send, recv, local,
+    out_ref, dmid_ref, do_ref, gwo_ref, gwu_ref, gwd_ref,
+    state_ref, wide_ref, rows_ref, unit_ref, attended_ref,
+    head_ref, held_ref, heldo_ref, heldu_ref, heldd_ref, pad_ref,
+    awo_ref, awu_ref, awd_ref, norm_ref, normt_ref, dy_ref, send, recv, local,
 ):
-    pair, block = pl.program_id(0), pl.program_id(1)
-    blocks = pl.num_programs(1)
-    step = pair * blocks + block
+    step = pl.program_id(0)
+    blocks = ATTENTION_STEPS // PAIRS
+    pair, block = step // blocks, step % blocks
     at = place()
     dp, z, core = at["dp"], at["z"], at["core"]
-    full = [head_ref, held_ref.at[0], held_ref.at[1], held_ref.at[2], heldo_ref]
-    full += [heldu_ref.at[0], heldu_ref.at[1], heldd_ref.at[0], heldd_ref.at[1]]
+    full = [head_ref, held_ref.at[0], held_ref.at[1], held_ref.at[2], heldo_ref] + halves(heldu_ref, heldd_ref)
     own = [array.at[dp, z, core] for array in full]
-    leave = [fullo_ref] + halves(fullu_ref, fulld_ref)
     partners = near_devices(at)
 
     def copy(w, k):
         return gather_copy(at, own[w], full[w], send.at[w], recv.at[w], k)
 
-    def keep(w):
-        return pltpu.make_async_copy(full[w], leave[w - 4], local.at[w])
+    def leave(w):
+        src = (heldo_ref, heldu_ref, heldd_ref)[w]
+        return pltpu.make_async_copy(src, (gwo_ref, gwu_ref, gwd_ref)[w], local.at[w])
 
     def fetch():
         return pltpu.make_async_copy(x_ref, rows_ref, local.at[0])
@@ -390,8 +409,6 @@
     def stages(plan):
         for w, stage in plan:
             gather_stage(functools.partial(copy, w), stage)
-            if stage == 4 and w > 3:
-                keep(w).start()
 
     @pl.when(step == 0)
     def _():
@@ -417,9 +434,8 @@
         greeted(partners)
         stages(GATHER_PLAN[0][:4])
         heldo_ref[dp, z, core] = wo_ref[...].astype(bf16)
-        for i in range(2):
-            heldu_ref[i, dp, z, core] = wu_ref[:, i * (FF // 2) : (i + 1) * (FF // 2)].astype(bf16)
-            heldd_ref[i, dp, z, core] = wd_ref[i * 32 : (i + 1) * 32, :].astype(bf16)
+        heldu_ref[dp, z, core] = wu_ref[...].astype(bf16)
+        heldd_ref[dp, z, core] = wd_ref[...].astype(bf16)
         stages(GATHER_PLAN[0][4:10])
         fetch().wait()
 
@@ -436,42 +452,65 @@
                 gain_ref[i : i + 1, EXTRA * j : EXTRA * (j + 1)] = total[4 * i + j : 4 * i + j + 1, :]
 
     for when, plan in GATHER_PLAN.items():
-        if 0 < when < 8:
+        if when:
 
             @pl.when(step == when)
             def _(plan=plan):
                 stages(plan)
 
-    rows = block_rows(block)
-
-    @pl.when(pair == 0)
-    def _():
-        normed_ref[rows, :] = (unit_ref[rows, :] * gain_ref[0:1, :]).astype(bf16)
-
     for i in range(PAIRS):
 
-        @pl.when(jnp.logical_and(block == 0, pair == i))
+        @pl.when(step == i * blocks)
         def _(i=i):
             piece = held_ref[i - 1] if i else head_ref[..., :CHUNK]
             wpair_ref[...] = piece.reshape(D, CHUNK)
-
-    @pl.when(block == 0)
-    def _():
-        spread_projection(omega_ref, wide_ref)
-
-    forward_step(
-        block, starts_ref, lens_ref, normed_ref[rows, :], wpair_ref[...], wide_ref,
-        qkv_ref, fq_ref, fk_ref, o_ref, rden_ref, prefix_ref, state_ref,
-    )
-
-    @pl.when(step == PAIRS * blocks - 1)
-    def _():
-        stages(GATHER_PLAN[8])
-        for w in range(4, 9):
-            keep(w).wait()
+            spread_projection(omega_ref, wide_ref)
+
+    @pl.when(step < ATTENTION_STEPS)
+    def _():
+        rows = block_rows(block)
+
+        @pl.when(pair == 0)
+        def _():
+            normed_ref[rows, :] = (unit_ref[rows, :] * gain_ref[0:1, :]).astype(bf16)
+
+        forward_step(
+            block, starts_ref, lens_ref, normed_ref[rows, :], wpair_ref[...], wide_ref,
+            qkv_ref, fq_ref, fk_ref, o_ref, rden_ref, prefix_ref, state_ref,
+        )
+        attended_ref[rows, pl.ds(pl.multiple_of(pair * DUO, DUO), DUO)] = o_ref[...]
+
+    @pl.when(step >= ATTENTION_STEPS)
+    def _():
+        late = step - ATTENTION_STEPS
+        rows = pl.ds(pl.multiple_of(late * FF_BLOCK, FF_BLOCK), FF_BLOCK)
+
+        def arrive():
+            @pl.when(late == 0)
+            def _():
+                stages(GATHER_END)
+
+        feed_forward_step(
+            late, lens_ref, rows_ref[rows, :], attended_ref[rows, :], cot_ref[...],
+            lambda: heldo_ref[...].reshape(D, D),
+            lambda c: heldu_ref[..., c * FF_CHUNK : (c + 1) * FF_CHUNK].reshape(D, FF_CHUNK),
+            lambda c: heldd_ref[c].reshape(FF_CHUNK, D), gain_ref[1:2, :],
+            out_ref.at[rows], dmid_ref, do_ref, awo_ref, awu_ref, awd_ref, norm_ref, normt_ref, dy_ref, arrive,
+        )
+
+    @pl.when(step == pl.num_programs(0) - 1)
+    def _():
         for w in range(9):
             for k in range(10):
                 copy(w, k).wait_send()
+        heldo_ref[...] = awo_ref[...].astype(bf16).reshape(heldo_ref.shape)
+        leave(0).start()
+        heldu_ref[...] = awu_ref[...].astype(bf16).reshape(heldu_ref.shape)
+        leave(1).start()
+        heldd_ref[...] = awd_ref[...].astype(bf16).reshape(heldd_ref.shape)
+        leave(2).start()
+        for w in range(3):
+            leave(w).wait()
 
 
 def normal_parts(hidden):
@@ -479,61 +518,67 @@
     return inner, jnp.exp2(hidden * hidden * (-0.5 * log2_e)) * (1.0 / math.sqrt(2.0 * math.pi))
 
 
-def feed_forward_kernel(
-    block, chunk,
-    lens_ref, x_ref, o_ref, cot_ref, wo_ref, wu_ref, wd_ref, gain_ref,
-    out_ref, dmid_ref, do_ref, gwo_ref, gwu_ref, gwd_ref,
-    awo_ref, awu_ref, awd_ref, norm_ref, normt_ref, dyt_ref, dy_ref, y_ref, dn_ref,
+def feed_forward_step(
+    step, lens_ref, x, attended, cot, wo, wu, wd, gain,
+    out_ref, dmid_ref, do_ref, awo_ref, awu_ref, awd_ref, norm_ref, normt_ref, dy_ref, arrive=lambda: None,
 ):
-    step = pl.program_id(0)
-    steps = pl.num_programs(0)
-
     @pl.when(step == 0)
     def _():
         awo_ref[...] = jnp.zeros_like(awo_ref)
         awu_ref[...] = jnp.zeros_like(awu_ref)
         awd_ref[...] = jnp.zeros_like(awd_ref)
 
-    per_seg = SEG // block
-    position = lax.broadcasted_iota(jnp.int32, (block, 1), 0) + (step % per_seg) * block
+    per_seg = SEG // FF_BLOCK
+    position = lax.broadcasted_iota(jnp.int32, (FF_BLOCK, 1), 0) + (step % per_seg) * FF_BLOCK
     valid = (position < lens_ref[step // per_seg]).astype(f32)
-    dy = (cot_ref[...].astype(f32) * valid).astype(bf16)
-    dy_ref[...] = dy
-    dyt_ref[...] = dy.T
-    gain = gain_ref[1:2, :]
-    attended = o_ref[...]
-    middle = x_ref[...].astype(f32) + dot_nn(attended, wo_ref[...])
+    dy_ref[...] = (cot.astype(f32) * valid).astype(bf16)
+    middle = x.astype(f32) + dot_nn(attended, wo())
     unit, inverse = normalise(middle)
     normed = (unit * gain).astype(bf16)
     norm_ref[...] = normed
     normt_ref[...] = normed.T
-    y_ref[...] = middle
-    dn_ref[...] = jnp.zeros_like(dn_ref)
-
-    for index in range(FF // chunk):
-        at = slice(index * chunk, (index + 1) * chunk)
-        hidden = dot_nn(norm_ref[...], wu_ref[:, at])
+    total = middle
+    back = 0.0
+    for index in range(FF // FF_CHUNK):
+        at = slice(index * FF_CHUNK, (index + 1) * FF_CHUNK)
+        up, down = wu(index), wd(index)
+        hidden = dot_nn(norm_ref[...], up)
         inner, bell = normal_parts(hidden)
         active = (hidden * inner).astype(bf16)
         slope = inner + hidden * bell
-        y_ref[...] += dot_nn(active, wd_ref[at, :])
-        grad_hidden = (slope * dot_nt(dy_ref[...], wd_ref[at, :])).astype(bf16)
-        awd_ref[:, at] += dot_nn(dyt_ref[...], active)
+        total = total + dot_nn(active, down)
+        grad_hidden = (slope * dot_nt(dy_ref[...], down)).astype(bf16)
+        awd_ref[at, :] += dot_tn(active, dy_ref[...])
         awu_ref[:, at] += dot_nn(normt_ref[...], grad_hidden)
-        dn_ref[...] += dot_nt(grad_hidden, wu_ref[:, at])
-
-    out_ref[...] = y_ref[...].astype(bf16)
-    grad_middle = dy_ref[...].astype(f32) + normalise_back(dn_ref[...], gain, unit, inverse)
+        back = back + dot_nt(grad_hidden, up)
+    out_ref[...] = total.astype(bf16)
+    grad_middle = dy_ref[...].astype(f32) + normalise_back(back, gain, unit, inverse)
     dmid_ref[...] = grad_middle
     branch = grad_middle.astype(bf16)
     awo_ref[...] += dot_tn(attended, branch)
-    do_ref[...] = dot_nt(branch, wo_ref[...])
-
-    @pl.when(step == steps - 1)
+    do_ref[...] = dot_nt(branch, wo())
+
+
+def feed_forward_local_kernel(
+    lens_ref, x_ref, o_ref, cot_ref, wo_ref, wu_ref, wd_ref, gain_ref,
+    out_ref, dmid_ref, do_ref, gwo_ref, gwu_ref, gwd_ref,
+    awo_ref, awu_ref, awd_ref, norm_ref, normt_ref, dy_ref,
+):
+    def chunk(index):
+        return slice(index * FF_CHUNK, (index + 1) * FF_CHUNK)
+
+    step = pl.program_id(0)
+    feed_forward_step(
+        step, lens_ref, x_ref[...], o_ref[...], cot_ref[...],
+        lambda: wo_ref[...], lambda c: wu_ref[:, chunk(c)], lambda c: wd_ref[chunk(c), :], gain_ref[1:2, :],
+        out_ref, dmid_ref, do_ref, awo_ref, awu_ref, awd_ref, norm_ref, normt_ref, dy_ref,
+    )
+
+    @pl.when(step == pl.num_programs(0) - 1)
     def _():
         gwo_ref[...] = awo_ref[...].astype(bf16)
         gwu_ref[...] = awu_ref[...].astype(bf16)
-        gwd_ref[...] = awd_ref[...].astype(bf16).T
+        gwd_ref[...] = awd_ref[...].astype(bf16)
 
 
 def backward_step(
@@ -615,7 +660,7 @@
     starts_ref, normed_ref, qkv_ref, fq_ref, fk_ref, o_ref, rden_ref, do_ref, prefix_ref, omega_ref, gain_ref,
     x_ref, dmid_in_ref, weight_ref,
     gin_ref, gw_ref,
-    suffix_ref, wide_ref, dqkv_ref, turned_ref,
+    suffix_ref, wide_ref, dqkv_ref, rowsn_ref,
 ):
     pair, step = pl.program_id(0), pl.program_id(1)
     blocks = pl.num_programs(1)
@@ -627,7 +672,7 @@
 
     @pl.when(pair == 0)
     def _():
-        turned_ref[:, block_rows(block)] = normed_ref[...].T
+        rowsn_ref[block_rows(block), :] = normed_ref[...]
 
     backward_step(
         block, blocks, starts_ref, qkv_ref, fq_ref, fk_ref, o_ref, rden_ref, do_ref, prefix_ref, wide_ref,
@@ -636,7 +681,7 @@
 
     @pl.when(step == blocks - 1)
     def _():
-        gw_ref[...] = dot_nn(turned_ref[...], dqkv_ref[:, pair_lanes(pair)]).astype(bf16)
+        gw_ref[...] = dot_tn(rowsn_ref[...], dqkv_ref[:, pair_lanes(pair)]).astype(bf16)
 
     @pl.when(jnp.logical_and(step == blocks - 1, pair == PAIRS - 1))
     def _():
@@ -661,10 +706,10 @@
     starts_ref, normed_ref, qkv_ref, fq_ref, fk_ref, o_ref, rden_ref, do_ref, prefix_ref, omega_ref, gain_ref,
     wq_ref, wu_ref, own_gain_ref, x_ref, dmid_ref, weight_ref, go_ref, gu_ref, gd_ref,
     gin_ref, ro_ref, ru_ref, rd_ref, rq_ref, rg_ref, norm_ref,
-    suffix_ref, wide_ref, dqkv_ref, turned_ref, gq_ref,
-    rows_ref, mid_ref, held_ref,
+    suffix_ref, wide_ref, dqkv_ref, rowsn_ref, gq_ref,
+    rows_ref, held_ref,
     po_ref, pu_ref, pd_ref, pq_ref, so_ref, su_ref, sd_ref, sq_ref, bo_ref, bu_ref, bd_ref, bq_ref,
-    last_ref, near_ref, send, recv, local, out_sem, last_send, last_recv, near_send, near_recv,
+    last_ref, near_ref, send, recv, local, last_send, last_recv, near_send, near_recv,
 ):
     pair, inner_step = pl.program_id(0), pl.program_id(1)
     blocks = pl.num_programs(1)
@@ -692,7 +737,7 @@
 
     def late(i):
         src = (x_ref, dmid_ref, weight_ref)[i]
-        dst = (rows_ref, mid_ref, held_ref)[i]
+        dst = (rows_ref, gin_ref, held_ref)[i]
         return pltpu.make_async_copy(src, dst, local.at[5 + i])
 
     def stages(plan):
@@ -731,7 +776,7 @@
 
     @pl.when(pair == 0)
     def _():
-        turned_ref[:, block_rows(block)] = normed_ref[...].T
+        rowsn_ref[block_rows(block), :] = normed_ref[...]
 
     backward_step(
         block, blocks, starts_ref, qkv_ref, fq_ref, fk_ref, o_ref, rden_ref, do_ref, prefix_ref, wide_ref,
@@ -742,7 +787,7 @@
 
         @pl.when(step == (i + 1) * blocks - 1)
         def _(i=i):
-            grad = dot_nn(turned_ref[...], dqkv_ref[:, i * CHUNK : (i + 1) * CHUNK]).astype(bf16)
+            grad = dot_tn(rowsn_ref[...], dqkv_ref[:, i * CHUNK : (i + 1) * CHUNK]).astype(bf16)
             gq_ref[i] = grad.reshape(4, 4, 2, 16, CHUNK)
             stages([(5 + i, 0)])
 
@@ -755,8 +800,7 @@
         def inputs_part(first, last):
             @pl.loop(first * tiles // 8, last * tiles // 8)
             def _(i):
-                rows = input_gradient(i, rows_ref, dqkv_ref, held_ref, gain_ref[0:1, :], mid_ref)
-                pltpu.make_async_copy(mid_ref.at[rows], gin_ref.at[rows], out_sem.at[i]).start()
+                input_gradient(i, rows_ref, dqkv_ref, held_ref, gain_ref[0:1, :], gin_ref)
 
         def last(i):
             return direct_copy(at, parts[8], last_ref, last_send, last_recv, i)
@@ -813,11 +857,6 @@
             group = group + near_ref[i]
         norm_ref[...] = group
 
-        @pl.loop(0, tiles)
-        def _(i):
-            rows = pl.ds(pl.multiple_of(i * TILE, TILE), TILE)
-            pltpu.make_async_copy(mid_ref.at[rows], gin_ref.at[rows], out_sem.at[i]).wait()
-
         for i in range(31):
             near(i).wait_send()
         for i in range(1, 16):
@@ -831,21 +870,27 @@
 def update_kernel(
     count_ref, total_ref, rq_ref, ro_ref, ru_ref, rd_ref, rg_ref,
     wq_ref, wo_ref, wu_ref, wd_ref, wg_ref, mq_ref, mo_ref, mu_ref, md_ref, mg_ref,
-    vq_ref, vo_ref, vu_ref, vd_ref, vg_ref, gin_ref,
+    vq_ref, vo_ref, vu_ref, vd_ref, vg_ref, gin_ref, out_ref,
     norm_ref, gq_ref, nvq_ref, nwq_ref, go_ref, nvo_ref, nwo_ref, gu_ref, nvu_ref, nwu_ref,
-    gd_ref, nvd_ref, nwd_ref, gg_ref, nvg_ref, nwg_ref, gin_out_ref,
+    gd_ref, nvd_ref, nwd_ref, gg_ref, nvg_ref, nwg_ref, gin_out_ref, out_out_ref, sem,
 ):
-    gin_out_ref[...] = gin_ref[...]
-
-    @pl.when(pl.program_id(0) == 0)
-    def _():
-        update_weights(
-            count_ref, total_ref, rq_ref, ro_ref, ru_ref, rd_ref, rg_ref,
-            wq_ref, wo_ref, wu_ref, wd_ref, wg_ref, mq_ref, mo_ref, mu_ref, md_ref, mg_ref,
-            vq_ref, vo_ref, vu_ref, vd_ref, vg_ref,
-            norm_ref, gq_ref, nvq_ref, nwq_ref, go_ref, nvo_ref, nwo_ref, gu_ref, nvu_ref, nwu_ref,
-            gd_ref, nvd_ref, nwd_ref, gg_ref, nvg_ref, nwg_ref,
-        )
+    quarter = gin_ref.shape[0] // 4
+    moves = []
+    for i in range(4):
+        rows = pl.ds(i * quarter, quarter)
+        for j, (src, dst) in enumerate(((gin_ref, gin_out_ref), (out_ref, out_out_ref))):
+            moves.append(pltpu.make_async_copy(src.at[rows], dst.at[rows], sem.at[j, i]))
+    for move in moves:
+        move.start()
+    update_weights(
+        count_ref, total_ref, rq_ref, ro_ref, ru_ref, rd_ref, rg_ref,
+        wq_ref, wo_ref, wu_ref, wd_ref, wg_ref, mq_ref, mo_ref, mu_ref, md_ref, mg_ref,
+        vq_ref, vo_ref, vu_ref, vd_ref, vg_ref,
+        norm_ref, gq_ref, nvq_ref, nwq_ref, go_ref, nvo_ref, nwo_ref, gu_ref, nvu_ref, nwu_ref,
+        gd_ref, nvd_ref, nwd_ref, gg_ref, nvg_ref, nwg_ref,
+    )
+    for move in moves:
+        move.wait()
 
 
 def update_weights(
@@ -894,10 +939,10 @@
     return jax.ShapeDtypeStruct(shape, dtype)
 
 
-def params(collective_id=None):
+def params(collective_id=None, mib=63):
     if collective_id is None:
-        return pltpu.CompilerParams(vmem_limit_bytes=VMEM_LIMIT)
-    return pltpu.CompilerParams(vmem_limit_bytes=VMEM_LIMIT, collective_id=collective_id, has_side_effects=True)
+        return pltpu.CompilerParams(vmem_limit_bytes=mib << 20)
+    return pltpu.CompilerParams(vmem_limit_bytes=mib << 20, collective_id=collective_id, has_side_effects=True)
 
 
 def whole(shape):
@@ -954,42 +999,63 @@
     )(starts, lens, x, weight, gains, omega)
 
 
-def forward(starts, lens, x, omega, wq, wo, wu, wd, gains):
+def forward(count, starts, lens, x, omega, wq, wo, wu, wd, gains, cot):
     tokens = x.shape[0]
+    blocks = tokens // BLOCK
+    steps = PAIRS * blocks
     specs, shapes, scratch = forward_outs(tokens)
+
+    def early(index_map):
+        return lambda i: index_map(
+            jnp.minimum(i // blocks, PAIRS - 1), jnp.where(i < steps, i % blocks, blocks - 1)
+        )
+
+    specs = [pl.BlockSpec(spec.block_shape, early(spec.index_map)) for spec in specs]
+    weight = pl.BlockSpec(pair_weight.block_shape, early(pair_weight.index_map))
+    heads = pl.BlockSpec(pair_omega.block_shape, early(pair_omega.index_map))
+    rows = pl.BlockSpec((FF_BLOCK, D), lambda i: (jnp.maximum(i - steps, 0), 0))
     return pl.pallas_call(
         forward_kernel,
-        grid=(PAIRS, tokens // BLOCK),
-        in_specs=[smem, smem, hbm, pair_omega] + [whole(array.shape) for array in (wq, wo, wu, wd, gains)],
-        out_specs=specs + [pair_weight, whole_out((8, D)), hbm, hbm, hbm],
-        out_shape=shapes + [shaped((D, WIDE), bf16), shaped((8, D), f32)]
+        grid=(steps + tokens // FF_BLOCK,),
+        in_specs=[smem, smem, smem, hbm, heads] + [whole(array.shape) for array in (wq, wo, wu, wd, gains)] + [rows],
+        out_specs=specs + [weight, whole_out((8, D)), vmem, rows, rows, hbm, hbm, hbm],
+        out_shape=shapes
+        + [shaped((D, WIDE), bf16), shaped((8, D), f32)]
+        + [pltpu.VMEM((tokens, D), bf16), shaped((tokens, D), f32), shaped((tokens, D), f32)]
         + [shaped(five(name), bf16) for name in LATE],
         scratch_shapes=scratch
         + [
             pltpu.VMEM((tokens, D), bf16),
             pltpu.VMEM((tokens, D), f32),
+            pltpu.VMEM((tokens, D), bf16),
             pltpu.VMEM((4, 4, 2, 16, CHUNK + EXTRA), bf16),
             pltpu.VMEM((PAIRS - 1, *five("pair")), bf16),
         ]
+        + [pltpu.VMEM(five(name), bf16) for name in LATE]
+        + [pltpu.VMEM((8, EXTRA), f32)]
+        + feed_forward_scratch()
         + [
-            pltpu.VMEM(five("out"), bf16),
-            pltpu.VMEM((2, 4, 4, 2, 16, FF // 2), bf16),
-            pltpu.VMEM((2, 4, 4, 2, 32, D), bf16),
-            pltpu.VMEM((8, EXTRA), f32),
             pltpu.SemaphoreType.DMA((9, 10)),
             pltpu.SemaphoreType.DMA((9, 10)),
-            pltpu.SemaphoreType.DMA((9,)),
+            pltpu.SemaphoreType.DMA((3,)),
         ],
-        compiler_params=params(0),
-    )(starts, lens, x, omega, wq, wo, wu, wd, gains)
-
-
-def feed_forward(lens, x, o, cot, wo, wu, wd, gains, block=512, chunk=512):
+        compiler_params=params(0, FORWARD_MIB),
+    )(count, starts, lens, x, omega, wq, wo, wu, wd, gains, cot)
+
+
+def feed_forward_scratch():
+    return [
+        pltpu.VMEM((D, D), f32), pltpu.VMEM((D, FF), f32), pltpu.VMEM((FF, D), f32),
+        pltpu.VMEM((FF_BLOCK, D), bf16), pltpu.VMEM((D, FF_BLOCK), bf16), pltpu.VMEM((FF_BLOCK, D), bf16),
+    ]
+
+
+def feed_forward_local(lens, x, o, cot, wo, wu, wd, gains):
     tokens = x.shape[0]
-    rows = pl.BlockSpec((block, D), lambda i: (i, 0))
+    rows = pl.BlockSpec((FF_BLOCK, D), lambda i: (i, 0))
     return pl.pallas_call(
-        functools.partial(feed_forward_kernel, block, chunk),
-        grid=(tokens // block,),
+        feed_forward_local_kernel,
+        grid=(tokens // FF_BLOCK,),
         in_specs=[smem, rows, rows, rows, whole((D, D)), whole((D, FF)), whole((FF, D)), whole((8, D))],
         out_specs=[rows, rows, rows, whole_out((D, D)), whole_out((D, FF)), whole_out((FF, D))],
         out_shape=[
@@ -1000,11 +1066,7 @@
             shaped((D, FF), bf16),
             shaped((FF, D), bf16),
         ],
-        scratch_shapes=[
-            pltpu.VMEM((D, D), f32), pltpu.VMEM((D, FF), f32), pltpu.VMEM((D, FF), f32),
-            pltpu.VMEM((block, D), bf16), pltpu.VMEM((D, block), bf16), pltpu.VMEM((D, block), bf16),
-            pltpu.VMEM((block, D), bf16), pltpu.VMEM((block, D), f32), pltpu.VMEM((block, D), f32),
-        ],
+        scratch_shapes=feed_forward_scratch(),
         compiler_params=params(),
     )(lens, x, o, cot, wo, wu, wd, gains)
 
@@ -1031,7 +1093,7 @@
         pltpu.VMEM((2, DUO, FEAT), f32),
         pltpu.VMEM((2, DUO, FEAT), bf16),
         pltpu.VMEM((tokens, WIDE), bf16),
-        pltpu.VMEM((D, tokens), bf16),
+        pltpu.VMEM((tokens, D), bf16),
     ]
 
 
@@ -1051,42 +1113,37 @@
 def backward(args, wq, wu, gains, x, dmid, weight, grads):
     tokens = x.shape[0]
     half = [(4, 4, 16, D), (2, 4, 4, 16, FF // 2), (2, 4, 4, 32, D), (PAIRS, 4, 4, 16, CHUNK)]
-    grads = [grad.reshape(five(name)) for grad, name in zip(grads, LATE)]
     dma = pltpu.SemaphoreType.DMA
     return pl.pallas_call(
         backward_kernel,
         grid=(PAIRS, tokens // BLOCK),
         in_specs=backward_ins(tokens // BLOCK) + [whole(wq.shape), whole(wu.shape), whole(gains.shape)] + [hbm] * 6,
-        out_specs=[hbm]
-        + [whole_out((ROWS[name], COLS[name])) for name in LATE]
-        + [whole_out((PAIRS, 16, CHUNK)), whole_out((2, 16)), whole_out((8, 128))],
-        out_shape=[shaped((tokens, D), f32)]
-        + [shaped((ROWS[name], COLS[name]), f32) for name in LATE]
-        + [shaped((PAIRS, 16, CHUNK), f32), shaped((2, 16), f32), shaped((8, 128), f32)],
+        out_specs=[vmem] * 7,
+        out_shape=[pltpu.VMEM((tokens, D), f32)]
+        + [pltpu.VMEM((ROWS[name], COLS[name]), f32) for name in LATE]
+        + [pltpu.VMEM((PAIRS, 16, CHUNK), f32), pltpu.VMEM((2, 16), f32), pltpu.VMEM((8, 128), f32)],
         scratch_shapes=backward_scratch(tokens)
         + [pltpu.VMEM((PAIRS, *five("pair")), bf16)]
-        + [pltpu.VMEM((tokens, D), bf16), pltpu.VMEM((tokens, D), f32), pltpu.VMEM((D, WIDE), bf16)]
+        + [pltpu.VMEM((tokens, D), bf16), pltpu.VMEM((D, WIDE), bf16)]
         + [pltpu.VMEM(shape, bf16) for shape in half] * 3
         + [pltpu.VMEM((15, 16, CHUNK), bf16), pltpu.VMEM((32, 8, 128), f32)]
-        + [dma((9, 7)), dma((9, 7)), dma((8,)), dma((tokens // TILE,)), dma((15,)), dma((15,)), dma((31,)), dma((31,))],
-        compiler_params=params(1),
+        + [dma((9, 7)), dma((9, 7)), dma((8,)), dma((15,)), dma((15,)), dma((31,)), dma((31,))],
+        compiler_params=params(1, BACKWARD_MIB),
     )(*args, wq, wu, gains, x, dmid, weight, *grads)
 
 
-def update_all(count, total, grads, weights, firsts, seconds, grad_inputs):
+def update_all(count, total, grads, weights, firsts, seconds, grad_inputs, out_rows):
     shapes = [shaped((1, 1), f32)]
     for weight in weights:
         shapes += [shaped(weight.shape, f32)] * 3
-    arrays = (total, *grads, *weights, *firsts, *seconds)
-    rows = pl.BlockSpec((UPDATE_ROWS, D), lambda i: (i, 0))
     return pl.pallas_call(
         update_kernel,
-        grid=(grad_inputs.shape[0] // UPDATE_ROWS,),
-        in_specs=[smem] + [whole(array.shape) for array in arrays] + [rows],
-        out_specs=[whole_out(shape.shape) for shape in shapes] + [rows],
-        out_shape=shapes + [shaped(grad_inputs.shape, f32)],
-        compiler_params=params(),
-    )(count.reshape(1), *arrays, grad_inputs)
+        in_specs=[smem] + [vmem] * 23,
+        out_specs=[vmem] * 16 + [hbm, hbm],
+        out_shape=shapes + [shaped(grad_inputs.shape, f32), shaped(out_rows.shape, bf16)],
+        scratch_shapes=[pltpu.SemaphoreType.DMA((2, 4))],
+        compiler_params=params(mib=UPDATE_MIB),
+    )(count, total, *grads, *weights, *firsts, *seconds, grad_inputs, out_rows)
 
 
 def to_pairs(weight):
@@ -1109,19 +1166,15 @@
     firsts = (m_qkv, m_out, m_up, m_down, m_gains)
     seconds = (v_qkv, v_out, v_up, v_down, v_gains)
     if sizes == (4, 8):
-        (qkv, fq, fk, attended, rden, prefix, normed, qkv_full, gain_full, out_full, up_full, down_full) = forward(
-            seg_start, seg_len, inputs, feature_omega, *weights
-        )
-        out_rows, dmid, grad_attended, grad_out, grad_up, grad_down = feed_forward(
-            seg_len, inputs, attended, cotangent, out_full.reshape(D, D), up_full.reshape(D, FF),
-            down_full.reshape(FF, D), gain_full,
-        )
+        count = step_count.reshape(1)
+        (qkv, fq, fk, attended, rden, prefix, normed, qkv_full, gain_full, out_rows, dmid, grad_attended,
+         *grads) = forward(count, seg_start, seg_len, inputs, feature_omega, *weights, cotangent)
         grad_inputs, r_out, r_up, r_down, r_qkv, r_gains, total = backward(
             (seg_start, normed, qkv, fq, fk, attended, rden, grad_attended, prefix, feature_omega, gain_full),
-            w_qkv, w_up, gains, inputs, dmid, qkv_full, (grad_out, grad_up, grad_down),
+            w_qkv, w_up, gains, inputs, dmid, qkv_full, grads,
         )
-        norm, *updated, grad_inputs = update_all(
-            step_count, total, (r_qkv, r_out, r_up, r_down, r_gains), weights, firsts, seconds, grad_inputs
+        norm, *updated, grad_inputs, out_rows = update_all(
+            count, total, (r_qkv, r_out, r_up, r_down, r_gains), weights, firsts, seconds, grad_inputs, out_rows
         )
         return (out_rows, grad_inputs, norm.reshape(()), *updated)
 
@@ -1134,7 +1187,7 @@
     qkv, fq, fk, attended, rden, prefix, normed = forward_local(
         seg_start, seg_len, inputs, qkv_full, gain_full, feature_omega
     )
-    out_rows, dmid, grad_attended, grad_out, grad_up, grad_down = feed_forward(
+    out_rows, dmid, grad_attended, grad_out, grad_up, grad_down = feed_forward_local(
         seg_len, inputs, attended, cotangent, out_full, up_full, down_full, gain_full
     )
     grad_inputs, grad_qkv = backward_local(

time: 168 us -> 159 us (0.946)
  Pallas kernels: 166 us -> 157 us
    pallas_call x3 -> x2, Pallas kernels: 101 us -> 92.5 us  [the longest x1 88.7 us: forward(): pl.pallas_call(forward_kernel, grid=(steps + tokens // FF_BLOCK,), in_spe...]
where the time goes in v3:
time: 159 us
  Pallas kernels  157 us (99%)
  between operations  1.72 us (1%)
    pallas_call x1, Pallas kernels, forward(): pl.pallas_call(forward_kernel, grid=(steps + tokens // FF_BLOCK,), in_spe...  88.7 us
    pallas_call x1, Pallas kernels, backward(): pl.pallas_call(backward_kernel, grid=(PAIRS, tokens // BLOCK), in_specs=b...  65 us
    pallas_call x1, Pallas kernels, update_all(): pl.pallas_call(update_kernel, in_specs=[smem] + [vmem] * 23, out_specs=[v...  3.79 us

profile of v3, /device:TPU:0, one launch (start us, length us, event | category | flops | bytes accessed | tf_op | source)
XLA Modules:
  0.0 159.3 jit_solution(4492983366646481225)
XLA Ops:
  1.3 88.7 %shard_map.340 = (bf16[4,2048,384]{2,1,0:T(8,128)(2,1)}, bf16[4,2048,512]{2,1,0:T(8,128)(2,1)}, bf16[4,2048,512]{2,1,0:T(8,128)(2,1)}, bf16[2048,512]{1,0:T(8,12...) custom-call(s32[1]{0:T(128)} %bitcast.2.count_ref, ...), custom_call_target="tpu_custom_call" | custom-call | tf_op jit(solution)/shard_map/pallas_call | solution.py:1017
  90.0 0.0 copy-start
  90.0 0.0 copy-start.1
  90.0 0.0 copy-start.2
  90.0 0.0 copy-start.3
  90.0 0.0 copy-start.4
  90.0 0.0 copy-start.5
  90.1 0.0 copy-start.6
  90.1 0.0 copy-start.7
  90.1 0.0 copy-start.8
  90.1 0.0 copy-start.9
  90.1 0.0 copy-start.10
  90.1 0.0 copy-start.11
  90.1 0.0 copy-start.12
  90.1 0.0 copy-start.13
  90.2 0.0 copy-start.14
  90.2 65.0 %shard_map.341 = (f32[2048,512]{1,0:T(8,128)S(1)}, f32[16,512]{1,0:T(8,128)S(1)}, f32[16,2048]{1,0:T(8,128)S(1)}, f32[64,512]{1,0:T(8,128)S(1)}, f32[4,16,384]{2...) custom-call(s32[2]{0:T(128)} %starts_ref.3, bf16[2048,512]{1,0:T(8,128)(2,1)} %get-tuple-element.58.normed_ref, ...), custom_call_target="tpu_custom_call" | custom-call | tf_op jit(solution)/shard_map/pallas_call | solution.py:1117
  155.2 0.0 copy-done
  155.2 0.0 copy-done.1
  155.2 0.0 copy-done.2
  155.2 0.0 copy-done.3
  155.2 0.0 copy-done.4
  155.2 0.0 copy-done.5
  155.2 0.0 copy-done.6
  155.2 0.0 copy-done.7
  155.2 0.0 copy-done.8
  155.2 0.0 copy-done.9
  155.3 0.0 copy-done.10
  155.3 0.0 copy-done.11
  155.3 0.0 copy-done.12
  155.3 0.0 copy-done.13
  155.3 0.0 copy-done.14
  155.3 3.8 %shard_map.342 = (f32[1,1]{1,0:T(1,128)}, f32[16,1536]{1,0:T(8,128)}, f32[16,1536]{1,0:T(8,128)}, f32[16,1536]{1,0:T(8,128)}, f32[16,512]{1,0:T(8,128)}, /*index...) custom-call(s32[1]{0:T(128)} %bitcast.3.count_ref, ...), custom_call_target="tpu_custom_call" | custom-call | tf_op jit(solution)/shard_map/pallas_call | solution.py:1139
Async XLA Ops:
  90.0 65.2 %copy-start = (f32[16,2048]{1,0:T(8,128)S(1)}, f32[16,2048]{1,0:T(8,128)}, u32[]{:S(2)}) copy-start(f32[16,2048]{1,0:T(8,128)} %wu_ref.5) | copy-start | bytes 393220
  90.0 65.2 %copy-start.1 = (f32[16,1536]{1,0:T(8,128)S(1)}, f32[16,1536]{1,0:T(8,128)}, u32[]{:S(2)}) copy-start(f32[16,1536]{1,0:T(8,128)} %wq_ref.5) | copy-start | bytes 294916
  90.0 65.2 %copy-start.2 = (f32[64,512]{1,0:T(8,128)S(1)}, f32[64,512]{1,0:T(8,128)}, u32[]{:S(2)}) copy-start(f32[64,512]{1,0:T(8,128)} %wd_ref.3) | copy-start | bytes 393220
  90.0 65.2 %copy-start.3 = (f32[16,2048]{1,0:T(8,128)S(1)}, f32[16,2048]{1,0:T(8,128)}, u32[]{:S(2)}) copy-start(f32[16,2048]{1,0:T(8,128)} %mu_ref.1) | copy-start | bytes 393220
  90.0 65.2 %copy-start.4 = (f32[64,512]{1,0:T(8,128)S(1)}, f32[64,512]{1,0:T(8,128)}, u32[]{:S(2)}) copy-start(f32[64,512]{1,0:T(8,128)} %md_ref.1) | copy-start | bytes 393220
  90.0 65.2 %copy-start.5 = (f32[16,2048]{1,0:T(8,128)S(1)}, f32[16,2048]{1,0:T(8,128)}, u32[]{:S(2)}) copy-start(f32[16,2048]{1,0:T(8,128)} %vu_ref.1) | copy-start | bytes 393220
  90.1 65.2 %copy-start.6 = (f32[64,512]{1,0:T(8,128)S(1)}, f32[64,512]{1,0:T(8,128)}, u32[]{:S(2)}) copy-start(f32[64,512]{1,0:T(8,128)} %vd_ref.1) | copy-start | bytes 393220
  90.1 65.2 %copy-start.7 = (f32[16,512]{1,0:T(8,128)S(1)}, f32[16,512]{1,0:T(8,128)}, u32[]{:S(2)}) copy-start(f32[16,512]{1,0:T(8,128)} %wo_ref.3) | copy-start | bytes 98308
  90.1 65.2 %copy-start.8 = (f32[16,1536]{1,0:T(8,128)S(1)}, f32[16,1536]{1,0:T(8,128)}, u32[]{:S(2)}) copy-start(f32[16,1536]{1,0:T(8,128)} %mq_ref.1) | copy-start | bytes 294916
  90.1 65.1 %copy-start.9 = (f32[16,1536]{1,0:T(8,128)S(1)}, f32[16,1536]{1,0:T(8,128)}, u32[]{:S(2)}) copy-start(f32[16,1536]{1,0:T(8,128)} %vq_ref.1) | copy-start | bytes 294916
  90.1 65.1 %copy-start.10 = (f32[16,512]{1,0:T(8,128)S(1)}, f32[16,512]{1,0:T(8,128)}, u32[]{:S(2)}) copy-start(f32[16,512]{1,0:T(8,128)} %mo_ref.1) | copy-start | bytes 98308
  90.1 65.1 %copy-start.11 = (f32[16,512]{1,0:T(8,128)S(1)}, f32[16,512]{1,0:T(8,128)}, u32[]{:S(2)}) copy-start(f32[16,512]{1,0:T(8,128)} %vo_ref.1) | copy-start | bytes 98308
  90.1 65.1 %copy-start.12 = (f32[2,16]{1,0:T(2,128)S(1)}, f32[2,16]{1,0:T(2,128)}, u32[]{:S(2)}) copy-start(f32[2,16]{1,0:T(2,128)} %wg_ref.1) | copy-start | bytes 388
  90.1 65.1 %copy-start.13 = (f32[2,16]{1,0:T(2,128)S(1)}, f32[2,16]{1,0:T(2,128)}, u32[]{:S(2)}) copy-start(f32[2,16]{1,0:T(2,128)} %mg_ref.1) | copy-start | bytes 388
  90.2 65.1 %copy-start.14 = (f32[2,16]{1,0:T(2,128)S(1)}, f32[2,16]{1,0:T(2,128)}, u32[]{:S(2)}) copy-start(f32[2,16]{1,0:T(2,128)} %vg_ref.1) | copy-start | bytes 388

commit v4 on v3

--- a/solution.py
+++ b/solution.py
@@ -19,10 +19,11 @@
 DUO = 2 * HD
 BLOCK = 1024
 TILES_BLOCK = BLOCK // TILE
-FORWARD_MIB = 60
+FORWARD_MIB = 61
 BACKWARD_MIB = 52
 UPDATE_MIB = 20
-FF_BLOCK = 512
+FF_BLOCK = 1024
+FF_PART = 512
 FF_CHUNK = 512
 WIDE = 3 * D
 CHUNK = 3 * DUO
@@ -165,9 +166,12 @@
             copy(k).wait_recv()
 
 
+GATHER_START = (
+    [(0, 0), (1, 0), (2, 0), (3, 0)],
+    [(0, 1), (5, 0), (6, 0), (7, 0), (8, 0), (4, 0)],
+    [(0, 2), (1, 1), (2, 1), (3, 1), (0, 3), (0, 4), (1, 2), (5, 1)],
+)
 GATHER_PLAN = {
-    0: [(0, 0), (1, 0), (2, 0), (3, 0), (0, 1), (5, 0), (6, 0), (7, 0), (8, 0), (4, 0),
-        (0, 2), (1, 1), (2, 1), (3, 1), (0, 3), (0, 4), (1, 2), (5, 1)],
     1: [(6, 1), (1, 3), (2, 2), (3, 2)],
     2: [(1, 4), (7, 1), (5, 2), (8, 1)],
     3: [(6, 2), (4, 1), (2, 3), (3, 3)],
@@ -177,7 +181,6 @@
     7: [(7, 3), (8, 3), (4, 3), (6, 4)],
     8: [(4, 4), (7, 4), (8, 4)],
 }
-GATHER_END = [(7, 4), (8, 4)]
 
 
 def scatter_copy(at, grad, part, sums, boxes, send, recv, k):
@@ -252,13 +255,14 @@
 
 
 SCATTER_PLAN = {
-    1: [(0, 0), (1, 0), (2, 0), (3, 0), (4, 0)],
-    2: [(0, 1), (1, 1), (2, 1)],
-    3: [(5, 1), (3, 1), (0, 2)],
-    4: [(1, 2), (2, 2), (4, 1)],
-    5: [(5, 2), (6, 1), (3, 2), (0, 3)],
-    6: [(4, 2), (7, 1), (1, 3), (2, 3)],
-    7: [(6, 2), (5, 3), (3, 3), (7, 2), (0, 4)],
+    0: [(0, 0), (1, 0), (2, 0), (3, 0), (4, 0)],
+    1: [(0, 1), (1, 1), (2, 1)],
+    2: [(3, 1), (0, 2)],
+    3: [(5, 1), (1, 2), (2, 2), (4, 1)],
+    4: [(3, 2), (0, 3)],
+    5: [(5, 2), (6, 1), (4, 2), (1, 3), (2, 3)],
+    6: [(7, 1), (3, 3), (5, 3)],
+    7: [(6, 2), (4, 3), (7, 2), (0, 4), (1, 4)],
 }
 
 
@@ -276,7 +280,7 @@
 
 def forward_step(
     block, starts_ref, lens_ref, normed, weight, wide_ref,
-    qkv_ref, fq_ref, fk_ref, o_ref, rden_ref, prefix_ref, state_ref,
+    qkv_ref, fq_ref, fk_ref, att_ref, o_ref, rden_ref, prefix_ref, state_ref,
 ):
     per_seg = SEG // BLOCK
 
@@ -322,6 +326,8 @@
         weights = [
             jnp.where(causal, dot_nt(feats[odd], feats[2 + odd]), 0.0).astype(bf16) for odd in range(2)
         ]
+        for odd in range(2):
+            att_ref[0, cuts[tile], odd * TILE : (odd + 1) * TILE] = weights[odd]
         sums = [dot_nn(ones[odd].T, feats[2 + odd]) for odd in range(2)]
         mixed[tile] = weights, sums
 
@@ -359,7 +365,7 @@
 
 def forward_local_kernel(
     starts_ref, lens_ref, x_ref, w_ref, gain_ref, omega_ref,
-    qkv_ref, fq_ref, fk_ref, o_ref, rden_ref, prefix_ref, normed_ref, state_ref, wide_ref,
+    qkv_ref, fq_ref, fk_ref, att_ref, o_ref, rden_ref, prefix_ref, normed_ref, state_ref, wide_ref,
 ):
     pair, block = pl.program_id(0), pl.program_id(1)
     rows = block_rows(block)
@@ -375,13 +381,13 @@
 
     forward_step(
         block, starts_ref, lens_ref, normed_ref[rows, :], w_ref[...], wide_ref,
-        qkv_ref, fq_ref, fk_ref, o_ref, rden_ref, prefix_ref, state_ref,
+        qkv_ref, fq_ref, fk_ref, att_ref, o_ref, rden_ref, prefix_ref, state_ref,
     )
 
 
 def forward_kernel(
     count_ref, starts_ref, lens_ref, x_ref, omega_ref, wq_ref, wo_ref, wu_ref, wd_ref, gains_ref, cot_ref,
-    qkv_ref, fq_ref, fk_ref, o_ref, rden_ref, prefix_ref, normed_ref, wpair_ref, gain_ref,
+    qkv_ref, fq_ref, fk_ref, att_ref, o_ref, rden_ref, prefix_ref, normed_ref, wpair_ref, gain_ref,
     out_ref, dmid_ref, do_ref, gwo_ref, gwu_ref, gwd_ref,
     state_ref, wide_ref, rows_ref, unit_ref, attended_ref,
     head_ref, held_ref, heldo_ref, heldu_ref, heldd_ref, pad_ref,
@@ -432,18 +438,18 @@
                     held_ref[i - 1, dp, z, core, :, part * DUO : (part + 1) * DUO] = piece
         head_ref[dp, z, core, :, CHUNK:] = placed.astype(bf16)
         greeted(partners)
-        stages(GATHER_PLAN[0][:4])
+        stages(GATHER_START[0])
         heldo_ref[dp, z, core] = wo_ref[...].astype(bf16)
         heldu_ref[dp, z, core] = wu_ref[...].astype(bf16)
         heldd_ref[dp, z, core] = wd_ref[...].astype(bf16)
-        stages(GATHER_PLAN[0][4:10])
+        stages(GATHER_START[1])
         fetch().wait()
 
         @pl.loop(0, blocks)
         def _(i):
             unit_ref[block_rows(i), :] = normalise(rows_ref[block_rows(i), :].astype(f32))[0]
 
-        stages(GATHER_PLAN[0][10:])
+        stages(GATHER_START[2])
         packed = head_ref[..., CHUNK:].astype(f32)
         total = jnp.sum(packed.reshape(32, 16, EXTRA), axis=0)
         gain_ref[...] = jnp.zeros_like(gain_ref)
@@ -452,11 +458,10 @@
                 gain_ref[i : i + 1, EXTRA * j : EXTRA * (j + 1)] = total[4 * i + j : 4 * i + j + 1, :]
 
     for when, plan in GATHER_PLAN.items():
-        if when:
-
-            @pl.when(step == when)
-            def _(plan=plan):
-                stages(plan)
+
+        @pl.when(step == when)
+        def _(plan=plan):
+            stages(plan)
 
     for i in range(PAIRS):
 
@@ -476,7 +481,7 @@
 
         forward_step(
             block, starts_ref, lens_ref, normed_ref[rows, :], wpair_ref[...], wide_ref,
-            qkv_ref, fq_ref, fk_ref, o_ref, rden_ref, prefix_ref, state_ref,
+            qkv_ref, fq_ref, fk_ref, att_ref, o_ref, rden_ref, prefix_ref, state_ref,
         )
         attended_ref[rows, pl.ds(pl.multiple_of(pair * DUO, DUO), DUO)] = o_ref[...]
 
@@ -484,18 +489,13 @@
     def _():
         late = step - ATTENTION_STEPS
         rows = pl.ds(pl.multiple_of(late * FF_BLOCK, FF_BLOCK), FF_BLOCK)
-
-        def arrive():
-            @pl.when(late == 0)
-            def _():
-                stages(GATHER_END)
 
         feed_forward_step(
             late, lens_ref, rows_ref[rows, :], attended_ref[rows, :], cot_ref[...],
             lambda: heldo_ref[...].reshape(D, D),
             lambda c: heldu_ref[..., c * FF_CHUNK : (c + 1) * FF_CHUNK].reshape(D, FF_CHUNK),
             lambda c: heldd_ref[c].reshape(FF_CHUNK, D), gain_ref[1:2, :],
-            out_ref.at[rows], dmid_ref, do_ref, awo_ref, awu_ref, awd_ref, norm_ref, normt_ref, dy_ref, arrive,
+            out_ref.at[rows], dmid_ref, do_ref, awo_ref, awu_ref, awd_ref, norm_ref, normt_ref, dy_ref,
         )
 
     @pl.when(step == pl.num_programs(0) - 1)
@@ -520,7 +520,7 @@
 
 def feed_forward_step(
     step, lens_ref, x, attended, cot, wo, wu, wd, gain,
-    out_ref, dmid_ref, do_ref, awo_ref, awu_ref, awd_ref, norm_ref, normt_ref, dy_ref, arrive=lambda: None,
+    out_ref, dmid_ref, do_ref, awo_ref, awu_ref, awd_ref, norm_ref, normt_ref, dy_ref,
 ):
     @pl.when(step == 0)
     def _():
@@ -529,34 +529,57 @@
         awd_ref[...] = jnp.zeros_like(awd_ref)
 
     per_seg = SEG // FF_BLOCK
-    position = lax.broadcasted_iota(jnp.int32, (FF_BLOCK, 1), 0) + (step % per_seg) * FF_BLOCK
-    valid = (position < lens_ref[step // per_seg]).astype(f32)
-    dy_ref[...] = (cot.astype(f32) * valid).astype(bf16)
-    middle = x.astype(f32) + dot_nn(attended, wo())
-    unit, inverse = normalise(middle)
-    normed = (unit * gain).astype(bf16)
-    norm_ref[...] = normed
-    normt_ref[...] = normed.T
-    total = middle
-    back = 0.0
-    for index in range(FF // FF_CHUNK):
-        at = slice(index * FF_CHUNK, (index + 1) * FF_CHUNK)
-        up, down = wu(index), wd(index)
-        hidden = dot_nn(norm_ref[...], up)
-        inner, bell = normal_parts(hidden)
-        active = (hidden * inner).astype(bf16)
-        slope = inner + hidden * bell
-        total = total + dot_nn(active, down)
-        grad_hidden = (slope * dot_nt(dy_ref[...], down)).astype(bf16)
-        awd_ref[at, :] += dot_tn(active, dy_ref[...])
-        awu_ref[:, at] += dot_nn(normt_ref[...], grad_hidden)
-        back = back + dot_nt(grad_hidden, up)
-    out_ref[...] = total.astype(bf16)
-    grad_middle = dy_ref[...].astype(f32) + normalise_back(back, gain, unit, inverse)
-    dmid_ref[...] = grad_middle
-    branch = grad_middle.astype(bf16)
-    awo_ref[...] += dot_tn(attended, branch)
-    do_ref[...] = dot_nt(branch, wo())
+    halves_at = [slice(i * FF_PART, (i + 1) * FF_PART) for i in range(FF_BLOCK // FF_PART)]
+    kept = {}
+
+    def before(i):
+        at = halves_at[i]
+        position = lax.broadcasted_iota(jnp.int32, (FF_PART, 1), 0) + (step % per_seg) * FF_BLOCK + i * FF_PART
+        valid = (position < lens_ref[step // per_seg]).astype(f32)
+        dy_ref[at, :] = (cot[at].astype(f32) * valid).astype(bf16)
+        middle = x[at].astype(f32) + dot_nn(attended[at], wo())
+        unit, inverse = normalise(middle)
+        normed = (unit * gain).astype(bf16)
+        norm_ref[at, :] = normed
+        normt_ref[:, at] = normed.T
+        kept[i] = middle, unit, inverse
+
+    def chunks(i):
+        at = halves_at[i]
+        total, unit, inverse = kept[i]
+        back = 0.0
+        for index in range(FF // FF_CHUNK):
+            cut = slice(index * FF_CHUNK, (index + 1) * FF_CHUNK)
+            up, down = wu(index), wd(index)
+            hidden = dot_nn(norm_ref[at, :], up)
+            inner, bell = normal_parts(hidden)
+            active = (hidden * inner).astype(bf16)
+            slope = inner + hidden * bell
+            total = total + dot_nn(active, down)
+            grad_hidden = (slope * dot_nt(dy_ref[at, :], down)).astype(bf16)
+            awd_ref[cut, :] += dot_tn(active, dy_ref[at, :])
+            awu_ref[:, cut] += dot_nn(normt_ref[:, at], grad_hidden)
+            back = back + dot_nt(grad_hidden, up)
+        out_ref[at, :] = total.astype(bf16)
+        kept[i] = back, unit, inverse
+
+    def after(i):
+        at = halves_at[i]
+        back, unit, inverse = kept[i]
+        grad_middle = dy_ref[at, :].astype(f32) + normalise_back(back, gain, unit, inverse)
+        dmid_ref[at, :] = grad_middle
+        branch = grad_middle.astype(bf16)
+        awo_ref[...] += dot_tn(attended[at], branch)
+        do_ref[at, :] = dot_nt(branch, wo())
+
+    before(0)
+    for i in range(len(halves_at)):
+        if i + 1 < len(halves_at):
+            before(i + 1)
+        chunks(i)
+        if i:
+            after(i - 1)
+    after(len(halves_at) - 1)
 
 
 def feed_forward_local_kernel(
@@ -582,7 +605,7 @@
 
 
 def backward_step(
-    block, blocks, starts_ref, qkv_ref, fq_ref, fk_ref, o_ref, rden_ref, do_ref, prefix_ref, wide_ref,
+    block, blocks, starts_ref, qkv_ref, fq_ref, fk_ref, att_ref, o_ref, rden_ref, do_ref, prefix_ref, wide_ref,
     suffix_ref, store,
 ):
     per_seg = SEG // BLOCK
@@ -616,12 +639,12 @@
             rest = edge - edge.astype(bf16).astype(f32)
             after_low = jnp.where(state_row == free + 1, rest, after).astype(bf16)
             before_low = prefix_ref[0, tile, odd]
-            weights_t = jnp.where(anti, dot_nt(key_feat, query_feat), 0.0).astype(bf16)
+            weights = att_ref[0, at, odd * TILE : (odd + 1) * TILE]
             grad_w = jnp.where(causal, dot_nt(grad_one, one), 0.0).astype(bf16)
             grad_wt = jnp.where(anti, dot_nt(one, grad_one), 0.0).astype(bf16)
             grad_fq = dot_nn(grad_w, key_feat) + dot_nn(grad_one, before_low)
             grad_fk = dot_nn(grad_wt, query_feat) + dot_nn(one, after_low)
-            back[2].append(dot_nn(weights_t, grad_one) + dot_nt(key_feat, after_low))
+            back[2].append(dot_tn(weights, grad_one) + dot_nt(key_feat, after_low))
             suffix_ref[odd] = after + dot_tn(grad_one, query_feat)
             grad_pq = (grad_fq * query_feat.astype(f32)).astype(bf16)
             grad_pk = (grad_fk * key_feat.astype(f32)).astype(bf16)
@@ -657,7 +680,7 @@
 
 
 def backward_local_kernel(
-    starts_ref, normed_ref, qkv_ref, fq_ref, fk_ref, o_ref, rden_ref, do_ref, prefix_ref, omega_ref, gain_ref,
+    starts_ref, normed_ref, qkv_ref, fq_ref, fk_ref, att_ref, o_ref, rden_ref, do_ref, prefix_ref, omega_ref, gain_ref,
     x_ref, dmid_in_ref, weight_ref,
     gin_ref, gw_ref,
     suffix_ref, wide_ref, dqkv_ref, rowsn_ref,
@@ -675,7 +698,7 @@
         rowsn_ref[block_rows(block), :] = normed_ref[...]
 
     backward_step(
-        block, blocks, starts_ref, qkv_ref, fq_ref, fk_ref, o_ref, rden_ref, do_ref, prefix_ref, wide_ref,
+        block, blocks, starts_ref, qkv_ref, fq_ref, fk_ref, att_ref, o_ref, rden_ref, do_ref, prefix_ref, wide_ref,
         suffix_ref, store_into(dqkv_ref, pair, block),
     )
 
@@ -703,7 +726,7 @@
 
 
 def backward_kernel(
-    starts_ref, normed_ref, qkv_ref, fq_ref, fk_ref, o_ref, rden_ref, do_ref, prefix_ref, omega_ref, gain_ref,
+    starts_ref, normed_ref, qkv_ref, fq_ref, fk_ref, att_ref, o_ref, rden_ref, do_ref, prefix_ref, omega_ref, gain_ref,
     wq_ref, wu_ref, own_gain_ref, x_ref, dmid_ref, weight_ref, go_ref, gu_ref, gd_ref,
     gin_ref, ro_ref, ru_ref, rd_ref, rq_ref, rg_ref, norm_ref,
     suffix_ref, wide_ref, dqkv_ref, rowsn_ref, gq_ref,
@@ -760,7 +783,7 @@
         for i in range(3):
             late(i).start()
 
-    @pl.when(step == 1)
+    @pl.when(step == 0)
     def _():
         greeted(others)
 
@@ -779,7 +802,7 @@
         rowsn_ref[block_rows(block), :] = normed_ref[...]
 
     backward_step(
-        block, blocks, starts_ref, qkv_ref, fq_ref, fk_ref, o_ref, rden_ref, do_ref, prefix_ref, wide_ref,
+        block, blocks, starts_ref, qkv_ref, fq_ref, fk_ref, att_ref, o_ref, rden_ref, do_ref, prefix_ref, wide_ref,
         suffix_ref, store_into(dqkv_ref, pair, block),
     )
 
@@ -805,7 +828,7 @@
         def last(i):
             return direct_copy(at, parts[8], last_ref, last_send, last_recv, i)
 
-        stages([(4, 3), (6, 3), (7, 3)])
+        stages([(6, 3), (7, 3)])
         inputs_part(0, 1)
         copy(8, 0).wait_recv()
         for i in range(4):
@@ -815,7 +838,7 @@
                 if i + j:
                     last(4 * i + j).start()
         inputs_part(1, 5)
-        stages([(1, 4), (2, 4), (3, 4), (5, 4), (4, 4), (6, 4), (7, 4)])
+        stages([(2, 4), (3, 4), (5, 4), (4, 4), (6, 4), (7, 4)])
         inputs_part(5, 8)
         early = row_squares(ro_ref[...]) + row_squares(ru_ref[...]) + row_squares(rd_ref[...])
         for i in range(PAIRS - 1):
@@ -874,10 +897,11 @@
     norm_ref, gq_ref, nvq_ref, nwq_ref, go_ref, nvo_ref, nwo_ref, gu_ref, nvu_ref, nwu_ref,
     gd_ref, nvd_ref, nwd_ref, gg_ref, nvg_ref, nwg_ref, gin_out_ref, out_out_ref, sem,
 ):
-    quarter = gin_ref.shape[0] // 4
+    pieces = 8
+    height = gin_ref.shape[0] // pieces
     moves = []
-    for i in range(4):
-        rows = pl.ds(i * quarter, quarter)
+    for i in range(pieces):
+        rows = pl.ds(i * height, height)
         for j, (src, dst) in enumerate(((gin_ref, gin_out_ref), (out_ref, out_out_ref))):
             moves.append(pltpu.make_async_copy(src.at[rows], dst.at[rows], sem.at[j, i]))
     for move in moves:
@@ -963,6 +987,7 @@
         pl.BlockSpec((1, BLOCK, CHUNK), lambda p, b: (p, b, 0)),
         pl.BlockSpec((1, BLOCK, 2 * FEAT), lambda p, b: (p, b, 0)),
         pl.BlockSpec((1, BLOCK, 2 * FEAT), lambda p, b: (p, b, 0)),
+        pl.BlockSpec((1, BLOCK, 2 * TILE), lambda p, b: (p, b, 0)),
         pl.BlockSpec((BLOCK, DUO), lambda p, b: (b, p)),
         pl.BlockSpec((1, BLOCK, DUO), lambda p, b: (p, b, 0)),
         pl.BlockSpec((1, TILES_BLOCK, 2, DUO, FEAT), lambda p, b: (p, b, 0, 0, 0)),
@@ -972,6 +997,7 @@
         shaped((PAIRS, tokens, CHUNK), bf16),
         shaped((PAIRS, tokens, 2 * FEAT), bf16),
         shaped((PAIRS, tokens, 2 * FEAT), bf16),
+        shaped((PAIRS, tokens, 2 * TILE), bf16),
         shaped((tokens, D), bf16),
         shaped((PAIRS, tokens, DUO), f32),
         shaped((PAIRS, tiles, 2, DUO, FEAT), bf16),
@@ -1079,6 +1105,7 @@
         pl.BlockSpec((1, BLOCK, CHUNK), lambda p, b: (p, last - b, 0)),
         pl.BlockSpec((1, BLOCK, 2 * FEAT), lambda p, b: (p, last - b, 0)),
         pl.BlockSpec((1, BLOCK, 2 * FEAT), lambda p, b: (p, last - b, 0)),
+        pl.BlockSpec((1, BLOCK, 2 * TILE), lambda p, b: (p, last - b, 0)),
         pl.BlockSpec((BLOCK, DUO), lambda p, b: (last - b, p)),
         pl.BlockSpec((1, BLOCK, DUO), lambda p, b: (p, last - b, 0)),
         pl.BlockSpec((BLOCK, DUO), lambda p, b: (last - b, p)),
@@ -1141,7 +1168,7 @@
         in_specs=[smem] + [vmem] * 23,
         out_specs=[vmem] * 16 + [hbm, hbm],
         out_shape=shapes + [shaped(grad_inputs.shape, f32), shaped(out_rows.shape, bf16)],
-        scratch_shapes=[pltpu.SemaphoreType.DMA((2, 4))],
+        scratch_shapes=[pltpu.SemaphoreType.DMA((2, 8))],
         compiler_params=params(mib=UPDATE_MIB),
     )(count, total, *grads, *weights, *firsts, *seconds, grad_inputs, out_rows)
 
@@ -1167,10 +1194,10 @@
     seconds = (v_qkv, v_out, v_up, v_down, v_gains)
     if sizes == (4, 8):
         count = step_count.reshape(1)
-        (qkv, fq, fk, attended, rden, prefix, normed, qkv_full, gain_full, out_rows, dmid, grad_attended,
+        (qkv, fq, fk, weights_kept, attended, rden, prefix, normed, qkv_full, gain_full, out_rows, dmid, grad_attended,
          *grads) = forward(count, seg_start, seg_len, inputs, feature_omega, *weights, cotangent)
         grad_inputs, r_out, r_up, r_down, r_qkv, r_gains, total = backward(
-            (seg_start, normed, qkv, fq, fk, attended, rden, grad_attended, prefix, feature_omega, gain_full),
+            (seg_start, normed, qkv, fq, fk, weights_kept, attended, rden, grad_attended, prefix, feature_omega, gain_full),
             w_qkv, w_up, gains, inputs, dmid, qkv_full, grads,
         )
         norm, *updated, grad_inputs, out_rows = update_all(
@@ -1184,14 +1211,14 @@
     qkv_full, out_full, up_full, down_full = (gather(piece) for piece in weights[:4])
     qkv_full = to_pairs(qkv_full)
     gain_full = jnp.pad(gather(gains, 1).astype(f32), ((0, 6), (0, 0)))
-    qkv, fq, fk, attended, rden, prefix, normed = forward_local(
+    qkv, fq, fk, weights_kept, attended, rden, prefix, normed = forward_local(
         seg_start, seg_len, inputs, qkv_full, gain_full, feature_omega
     )
     out_rows, dmid, grad_attended, grad_out, grad_up, grad_down = feed_forward_local(
         seg_len, inputs, attended, cotangent, out_full, up_full, down_full, gain_full
     )
     grad_inputs, grad_qkv = backward_local(
-        (seg_start, normed, qkv, fq, fk, attended, rden, grad_attended, prefix, feature_omega, gain_full),
+        (seg_start, normed, qkv, fq, fk, weights_kept, attended, rden, grad_attended, prefix, feature_omega, gain_full),
         inputs, dmid, qkv_full,
     )
 

time: 159 us -> 156 us (0.981)
  Pallas kernels: 157 us -> 154 us
    pallas_call x1, Pallas kernels: 88.7 us -> 86.6 us  [forward(): pl.pallas_call(forward_kernel, grid=(steps + tokens // FF_BLOCK,), in_spe...]
where the time goes in v4:
time: 156 us
  Pallas kernels  154 us (99%)
  between operations  1.72 us (1%)
    pallas_call x1, Pallas kernels, forward(): pl.pallas_call(forward_kernel, grid=(steps + tokens // FF_BLOCK,), in_spe...  86.6 us
    pallas_call x1, Pallas kernels, backward(): pl.pallas_call(backward_kernel, grid=(PAIRS, tokens // BLOCK), in_specs=b...  63.9 us
    pallas_call x1, Pallas kernels, update_all(): pl.pallas_call(update_kernel, in_specs=[smem] + [vmem] * 23, out_specs=[v...  3.86 us

profile of v4, /device:TPU:0, one launch (start us, length us, event | category | flops | bytes accessed | tf_op | source)
XLA Modules:
  0.0 156.2 jit_solution(3212959159670910389)
XLA Ops:
  1.3 86.6 %shard_map.340 = (bf16[4,2048,384]{2,1,0:T(8,128)(2,1)}, bf16[4,2048,512]{2,1,0:T(8,128)(2,1)}, bf16[4,2048,512]{2,1,0:T(8,128)(2,1)}, bf16[4,2048,512]{2,1,0:T(...) custom-call(s32[1]{0:T(128)} %bitcast.2.count_ref, ...), custom_call_target="tpu_custom_call" | custom-call | tf_op jit(solution)/shard_map/pallas_call | solution.py:1043
  87.9 0.0 copy-start
  88.0 0.0 copy-start.1
  88.0 0.0 copy-start.2
  88.0 0.0 copy-start.3
  88.0 0.0 copy-start.4
  88.0 0.0 copy-start.5
  88.0 0.0 copy-start.6
  88.0 0.0 copy-start.7
  88.0 0.0 copy-start.8
  88.1 0.0 copy-start.9
  88.1 0.0 copy-start.10
  88.1 0.0 copy-start.11
  88.1 0.0 copy-start.12
  88.1 0.0 copy-start.13
  88.1 0.0 copy-start.14
  88.1 63.9 %shard_map.341 = (f32[2048,512]{1,0:T(8,128)S(1)}, f32[16,512]{1,0:T(8,128)S(1)}, f32[16,2048]{1,0:T(8,128)S(1)}, f32[64,512]{1,0:T(8,128)S(1)}, f32[4,16,384]{2...) custom-call(s32[2]{0:T(128)} %starts_ref.3, bf16[2048,512]{1,0:T(8,128)(2,1)} %get-tuple-element.59.normed_ref, ...), custom_call_target="tpu_custom_call" | custom-call | tf_op jit(solution)/shard_map/pallas_call | solution.py:1144
  152.1 0.0 copy-done
  152.1 0.0 copy-done.1
  152.1 0.0 copy-done.2
  152.1 0.0 copy-done.3
  152.1 0.0 copy-done.4
  152.1 0.0 copy-done.5
  152.1 0.0 copy-done.6
  152.1 0.0 copy-done.7
  152.1 0.0 copy-done.8
  152.2 0.0 copy-done.9
  152.2 0.0 copy-done.10
  152.2 0.0 copy-done.11
  152.2 0.0 copy-done.12
  152.2 0.0 copy-done.13
  152.2 0.0 copy-done.14
  152.2 3.9 %shard_map.342 = (f32[1,1]{1,0:T(1,128)}, f32[16,1536]{1,0:T(8,128)}, f32[16,1536]{1,0:T(8,128)}, f32[16,1536]{1,0:T(8,128)}, f32[16,512]{1,0:T(8,128)}, /*index...) custom-call(s32[1]{0:T(128)} %bitcast.3.count_ref, ...), custom_call_target="tpu_custom_call" | custom-call | tf_op jit(solution)/shard_map/pallas_call | solution.py:1166
Async XLA Ops:
  87.9 64.1 %copy-start = (f32[16,2048]{1,0:T(8,128)S(1)}, f32[16,2048]{1,0:T(8,128)}, u32[]{:S(2)}) copy-start(f32[16,2048]{1,0:T(8,128)} %wu_ref.5) | copy-start | bytes 393220
  88.0 64.1 %copy-start.1 = (f32[16,1536]{1,0:T(8,128)S(1)}, f32[16,1536]{1,0:T(8,128)}, u32[]{:S(2)}) copy-start(f32[16,1536]{1,0:T(8,128)} %wq_ref.5) | copy-start | bytes 294916
  88.0 64.1 %copy-start.2 = (f32[64,512]{1,0:T(8,128)S(1)}, f32[64,512]{1,0:T(8,128)}, u32[]{:S(2)}) copy-start(f32[64,512]{1,0:T(8,128)} %wd_ref.3) | copy-start | bytes 393220
  88.0 64.1 %copy-start.3 = (f32[16,2048]{1,0:T(8,128)S(1)}, f32[16,2048]{1,0:T(8,128)}, u32[]{:S(2)}) copy-start(f32[16,2048]{1,0:T(8,128)} %mu_ref.1) | copy-start | bytes 393220
  88.0 64.1 %copy-start.4 = (f32[64,512]{1,0:T(8,128)S(1)}, f32[64,512]{1,0:T(8,128)}, u32[]{:S(2)}) copy-start(f32[64,512]{1,0:T(8,128)} %md_ref.1) | copy-start | bytes 393220
  88.0 64.1 %copy-start.5 = (f32[16,2048]{1,0:T(8,128)S(1)}, f32[16,2048]{1,0:T(8,128)}, u32[]{:S(2)}) copy-start(f32[16,2048]{1,0:T(8,128)} %vu_ref.1) | copy-start | bytes 393220
  88.0 64.1 %copy-start.6 = (f32[64,512]{1,0:T(8,128)S(1)}, f32[64,512]{1,0:T(8,128)}, u32[]{:S(2)}) copy-start(f32[64,512]{1,0:T(8,128)} %vd_ref.1) | copy-start | bytes 393220
  88.0 64.1 %copy-start.7 = (f32[16,512]{1,0:T(8,128)S(1)}, f32[16,512]{1,0:T(8,128)}, u32[]{:S(2)}) copy-start(f32[16,512]{1,0:T(8,128)} %wo_ref.3) | copy-start | bytes 98308
  88.0 64.1 %copy-start.8 = (f32[16,1536]{1,0:T(8,128)S(1)}, f32[16,1536]{1,0:T(8,128)}, u32[]{:S(2)}) copy-start(f32[16,1536]{1,0:T(8,128)} %mq_ref.1) | copy-start | bytes 294916
  88.1 64.1 %copy-start.9 = (f32[16,1536]{1,0:T(8,128)S(1)}, f32[16,1536]{1,0:T(8,128)}, u32[]{:S(2)}) copy-start(f32[16,1536]{1,0:T(8,128)} %vq_ref.1) | copy-start | bytes 294916
  88.1 64.1 %copy-start.10 = (f32[16,512]{1,0:T(8,128)S(1)}, f32[16,512]{1,0:T(8,128)}, u32[]{:S(2)}) copy-start(f32[16,512]{1,0:T(8,128)} %mo_ref.1) | copy-start | bytes 98308
  88.1 64.1 %copy-start.11 = (f32[16,512]{1,0:T(8,128)S(1)}, f32[16,512]{1,0:T(8,128)}, u32[]{:S(2)}) copy-start(f32[16,512]{1,0:T(8,128)} %vo_ref.1) | copy-start | bytes 98308
  88.1 64.1 %copy-start.12 = (f32[2,16]{1,0:T(2,128)S(1)}, f32[2,16]{1,0:T(2,128)}, u32[]{:S(2)}) copy-start(f32[2,16]{1,0:T(2,128)} %wg_ref.1) | copy-start | bytes 388
  88.1 64.1 %copy-start.13 = (f32[2,16]{1,0:T(2,128)S(1)}, f32[2,16]{1,0:T(2,128)}, u32[]{:S(2)}) copy-start(f32[2,16]{1,0:T(2,128)} %mg_ref.1) | copy-start | bytes 388
  88.1 64.1 %copy-start.14 = (f32[2,16]{1,0:T(2,128)S(1)}, f32[2,16]{1,0:T(2,128)}, u32[]{:S(2)}) copy-start(f32[2,16]{1,0:T(2,128)} %vg_ref.1) | copy-start | bytes 388

commit v5 on v4

--- a/solution.py
+++ b/solution.py
@@ -780,6 +780,9 @@
     @pl.when(step == 0)
     def _():
         greet(others)
+
+    @pl.when(step == 3)
+    def _():
         for i in range(3):
             late(i).start()
 
@@ -897,7 +900,7 @@
     norm_ref, gq_ref, nvq_ref, nwq_ref, go_ref, nvo_ref, nwo_ref, gu_ref, nvu_ref, nwu_ref,
     gd_ref, nvd_ref, nwd_ref, gg_ref, nvg_ref, nwg_ref, gin_out_ref, out_out_ref, sem,
 ):
-    pieces = 8
+    pieces = 4
     height = gin_ref.shape[0] // pieces
     moves = []
     for i in range(pieces):
@@ -1168,7 +1171,7 @@
         in_specs=[smem] + [vmem] * 23,
         out_specs=[vmem] * 16 + [hbm, hbm],
         out_shape=shapes + [shaped(grad_inputs.shape, f32), shaped(out_rows.shape, bf16)],
-        scratch_shapes=[pltpu.SemaphoreType.DMA((2, 8))],
+        scratch_shapes=[pltpu.SemaphoreType.DMA((2, 4))],
         compiler_params=params(mib=UPDATE_MIB),
     )(count, total, *grads, *weights, *firsts, *seconds, grad_inputs, out_rows)
 

time: 156 us -> 156 us (level)
  no operation moved by 1% of the time
where the time goes in v5:
time: 156 us
  Pallas kernels  154 us (99%)
  between operations  1.72 us (1%)
    pallas_call x1, Pallas kernels, forward(): pl.pallas_call(forward_kernel, grid=(steps + tokens // FF_BLOCK,), in_spe...  86.6 us
    pallas_call x1, Pallas kernels, backward(): pl.pallas_call(backward_kernel, grid=(PAIRS, tokens // BLOCK), in_specs=b...  63.9 us
    pallas_call x1, Pallas kernels, update_all(): pl.pallas_call(update_kernel, in_specs=[smem] + [vmem] * 23, out_specs=[v...  3.79 us

profile of v5, /device:TPU:0, one launch (start us, length us, event | category | flops | bytes accessed | tf_op | source)
XLA Modules:
  0.0 156.2 jit_solution(1348846605504720757)
XLA Ops:
  1.3 86.6 %shard_map.340 = (bf16[4,2048,384]{2,1,0:T(8,128)(2,1)}, bf16[4,2048,512]{2,1,0:T(8,128)(2,1)}, bf16[4,2048,512]{2,1,0:T(8,128)(2,1)}, bf16[4,2048,512]{2,1,0:T(...) custom-call(s32[1]{0:T(128)} %bitcast.2.count_ref, ...), custom_call_target="tpu_custom_call" | custom-call | tf_op jit(solution)/shard_map/pallas_call | solution.py:1046
  88.0 0.0 copy-start
  88.0 0.0 copy-start.1
  88.0 0.0 copy-start.2
  88.0 0.0 copy-start.3
  88.0 0.0 copy-start.4
  88.0 0.0 copy-start.5
  88.0 0.0 copy-start.6
  88.0 0.0 copy-start.7
  88.0 0.0 copy-start.8
  88.1 0.0 copy-start.9
  88.1 0.0 copy-start.10
  88.1 0.0 copy-start.11
  88.1 0.0 copy-start.12
  88.1 0.0 copy-start.13
  88.1 0.0 copy-start.14
  88.1 63.9 %shard_map.341 = (f32[2048,512]{1,0:T(8,128)S(1)}, f32[16,512]{1,0:T(8,128)S(1)}, f32[16,2048]{1,0:T(8,128)S(1)}, f32[64,512]{1,0:T(8,128)S(1)}, f32[4,16,384]{2...) custom-call(s32[2]{0:T(128)} %starts_ref.3, bf16[2048,512]{1,0:T(8,128)(2,1)} %get-tuple-element.59.normed_ref, ...), custom_call_target="tpu_custom_call" | custom-call | tf_op jit(solution)/shard_map/pallas_call | solution.py:1147
  152.1 0.0 copy-done
  152.1 0.0 copy-done.1
  152.1 0.0 copy-done.2
  152.1 0.0 copy-done.3
  152.1 0.0 copy-done.4
  152.1 0.0 copy-done.5
  152.1 0.0 copy-done.6
  152.1 0.0 copy-done.7
  152.1 0.0 copy-done.8
  152.1 0.0 copy-done.9
  152.2 0.0 copy-done.10
  152.2 0.0 copy-done.11
  152.2 0.0 copy-done.12
  152.2 0.0 copy-done.13
  152.2 0.0 copy-done.14
  152.2 3.8 %shard_map.342 = (f32[1,1]{1,0:T(1,128)}, f32[16,1536]{1,0:T(8,128)}, f32[16,1536]{1,0:T(8,128)}, f32[16,1536]{1,0:T(8,128)}, f32[16,512]{1,0:T(8,128)}, /*index...) custom-call(s32[1]{0:T(128)} %bitcast.3.count_ref, ...), custom_call_target="tpu_custom_call" | custom-call | tf_op jit(solution)/shard_map/pallas_call | solution.py:1169
Async XLA Ops:
  88.0 64.1 %copy-start = (f32[16,2048]{1,0:T(8,128)S(1)}, f32[16,2048]{1,0:T(8,128)}, u32[]{:S(2)}) copy-start(f32[16,2048]{1,0:T(8,128)} %wu_ref.5) | copy-start | bytes 393220
  88.0 64.1 %copy-start.1 = (f32[16,1536]{1,0:T(8,128)S(1)}, f32[16,1536]{1,0:T(8,128)}, u32[]{:S(2)}) copy-start(f32[16,1536]{1,0:T(8,128)} %wq_ref.5) | copy-start | bytes 294916
  88.0 64.1 %copy-start.2 = (f32[64,512]{1,0:T(8,128)S(1)}, f32[64,512]{1,0:T(8,128)}, u32[]{:S(2)}) copy-start(f32[64,512]{1,0:T(8,128)} %wd_ref.3) | copy-start | bytes 393220
  88.0 64.1 %copy-start.3 = (f32[16,2048]{1,0:T(8,128)S(1)}, f32[16,2048]{1,0:T(8,128)}, u32[]{:S(2)}) copy-start(f32[16,2048]{1,0:T(8,128)} %mu_ref.1) | copy-start | bytes 393220
  88.0 64.1 %copy-start.4 = (f32[64,512]{1,0:T(8,128)S(1)}, f32[64,512]{1,0:T(8,128)}, u32[]{:S(2)}) copy-start(f32[64,512]{1,0:T(8,128)} %md_ref.1) | copy-start | bytes 393220
  88.0 64.1 %copy-start.5 = (f32[16,2048]{1,0:T(8,128)S(1)}, f32[16,2048]{1,0:T(8,128)}, u32[]{:S(2)}) copy-start(f32[16,2048]{1,0:T(8,128)} %vu_ref.1) | copy-start | bytes 393220
  88.0 64.1 %copy-start.6 = (f32[64,512]{1,0:T(8,128)S(1)}, f32[64,512]{1,0:T(8,128)}, u32[]{:S(2)}) copy-start(f32[64,512]{1,0:T(8,128)} %vd_ref.1) | copy-start | bytes 393220
  88.0 64.1 %copy-start.7 = (f32[16,512]{1,0:T(8,128)S(1)}, f32[16,512]{1,0:T(8,128)}, u32[]{:S(2)}) copy-start(f32[16,512]{1,0:T(8,128)} %wo_ref.3) | copy-start | bytes 98308
  88.0 64.1 %copy-start.8 = (f32[16,1536]{1,0:T(8,128)S(1)}, f32[16,1536]{1,0:T(8,128)}, u32[]{:S(2)}) copy-start(f32[16,1536]{1,0:T(8,128)} %mq_ref.1) | copy-start | bytes 294916
  88.1 64.1 %copy-start.9 = (f32[16,1536]{1,0:T(8,128)S(1)}, f32[16,1536]{1,0:T(8,128)}, u32[]{:S(2)}) copy-start(f32[16,1536]{1,0:T(8,128)} %vq_ref.1) | copy-start | bytes 294916
  88.1 64.1 %copy-start.10 = (f32[16,512]{1,0:T(8,128)S(1)}, f32[16,512]{1,0:T(8,128)}, u32[]{:S(2)}) copy-start(f32[16,512]{1,0:T(8,128)} %mo_ref.1) | copy-start | bytes 98308
  88.1 64.1 %copy-start.11 = (f32[16,512]{1,0:T(8,128)S(1)}, f32[16,512]{1,0:T(8,128)}, u32[]{:S(2)}) copy-start(f32[16,512]{1,0:T(8,128)} %vo_ref.1) | copy-start | bytes 98308
  88.1 64.1 %copy-start.12 = (f32[2,16]{1,0:T(2,128)S(1)}, f32[2,16]{1,0:T(2,128)}, u32[]{:S(2)}) copy-start(f32[2,16]{1,0:T(2,128)} %wg_ref.1) | copy-start | bytes 388
  88.1 64.1 %copy-start.13 = (f32[2,16]{1,0:T(2,128)S(1)}, f32[2,16]{1,0:T(2,128)}, u32[]{:S(2)}) copy-start(f32[2,16]{1,0:T(2,128)} %mg_ref.1) | copy-start | bytes 388
  88.1 64.1 %copy-start.14 = (f32[2,16]{1,0:T(2,128)S(1)}, f32[2,16]{1,0:T(2,128)}, u32[]{:S(2)}) copy-start(f32[2,16]{1,0:T(2,128)} %vg_ref.1) | copy-start | bytes 388
